TPU v7x, 32 devices: a whole 2x2x4 slice. The times are simulated.
32 devices in a mesh: gx: 4 (over x, core), gy: 4 (over z), gz: 2 (over y).
Axes of the slice: x: 2, y: 2, z: 4, core: 2. Of those that a mesh axis runs over, the one named last changes fastest.
Arguments:
- positions: float32 [3, 8, 8, 4, 128], P(None, 'gx', 'gy', 'gz'), may hold values from 0 to 1
- velocities: float32 [3, 8, 8, 4, 128], P(None, 'gx', 'gy', 'gz'), may hold values from -3 to 3
- spins: float32 [3, 8, 8, 4, 128], P(None, 'gx', 'gy', 'gz'), may hold values from -6 to 6
- radii: float32 [8, 8, 4, 128], P('gx', 'gy', 'gz'), may hold values from 0.08 to 0.13
- counts: int32 [8, 8, 4], P('gx', 'gy', 'gz'), may hold values from 16 to 128
- springs: float32 [3, 4, 8, 8, 4, 128], P(None, None, 'gx', 'gy', 'gz'), may hold values from -0.36 to 0.36
- partners: int32 [4, 8, 8, 4, 128], P(None, 'gx', 'gy', 'gz'), may hold values from -1 to 895, as said below
- cells: int32 [8, 8, 4, 128], P('gx', 'gy', 'gz'), may hold values from 0 to 16383
- departures: int32 [4, 4, 2, 6, 128], P('gx', 'gy', 'gz'), may hold values from -1 to 1023, as said below
- fluid_velocity: float32 [3, 64, 128, 512], P(None, 'gx', 'gy', 'gz'), may hold values from -6 to 6
- pressure: float32 [64, 128, 512], P('gx', 'gy', 'gz'), may hold values from -6 to 6
- pressure_source: float32 [64, 128, 512], P('gx', 'gy', 'gz'), may hold values from -6 to 6
Outputs:
- new_positions: float32 [3, 8, 8, 4, 128], P(None, 'gx', 'gy', 'gz')
- new_velocities: float32 [3, 8, 8, 4, 128], P(None, 'gx', 'gy', 'gz')
- new_spins: float32 [3, 8, 8, 4, 128], P(None, 'gx', 'gy', 'gz')
- new_springs: float32 [3, 4, 8, 8, 4, 128], P(None, None, 'gx', 'gy', 'gz')
- fluid_force: float32 [3, 64, 128, 512], P(None, 'gx', 'gy', 'gz')
- new_pressure: float32 [64, 128, 512], P('gx', 'gy', 'gz')
- arrived: float32 [4, 4, 2, 22, 6, 128], P('gx', 'gy', 'gz')
- arrived_partners: int32 [4, 4, 2, 4, 6, 128], P('gx', 'gy', 'gz')
Inputs may be any that keep to these rules, and one draw needn't show every extreme that they name: `partners`: -1 marks an empty history slot; otherwise the code is bin * 128 + slot with bin 0 for the particle's own bin and 1 to 6 for the bins at -x, +x, -y, +y, -z, +z; a code never names the particle itself. `departures`: an entry is a local slot index ((bx * 2 + by) * 2 + bz) * 128 + slot, or -1; a slot appears at most once on its device; in each direction the used entries come first; in every draw some device fills all 128 entries of some direction.
All inputs are finite; a program needn't handle non-finite values.
Results may differ from a plain program's by a relative error of at most 0.0003.
Values sent between devices are 32-bit elements; how exact they have to be, the bound alone decides.
No kernel may reach another device: no remote copies, remote signals or barrier semaphores. Data moves between devices by JAX's collectives and lax.ppermute only.
A program may use at most 192 MiB of HBM per device.

v0:
```python
import functools
import math

import jax
import jax.numpy as jnp
from jax import lax
from jax.experimental import pallas as pl
from jax.experimental.pallas import tpu as pltpu
from jax.sharding import PartitionSpec as P

SUBSTEPS = 2

normal_stiff = 100.0
normal_damp = 2.0
shear_stiff = 30.0
friction = 0.5
time_step = 0.05
drag_coeff = 0.8
gravity = 1.0
soft_length = 0.05
force_floor = 0.5
volume_coeff = 100.0
neighbours = ((0, 0, 0), (-1, 0, 0), (1, 0, 0), (0, -1, 0), (0, 1, 0), (0, 0, -1), (0, 0, 1))
AXES = ("gx", "gy", "gz")
FIELDS = 10
DEAD = -8.0
TINY = 1e-30
GROUP = 4
f32 = jnp.float32


class Plan:
    def __init__(self, shape):
        self.dims = shape
        self.count = shape[0] * shape[1] * shape[2]

    def index(self, place):
        return (place[0] * self.dims[1] + place[1]) * self.dims[2] + place[2]

    def places(self):
        d = self.dims
        return [(a, b, c) for a in range(d[0]) for b in range(d[1]) for c in range(d[2])]

    def face(self, axis, side):
        edge = self.dims[axis] - 1 if side > 0 else 0
        return [self.index(p) for p in self.places() if p[axis] == edge]

    def neighbour(self, place, number):
        move = neighbours[number]
        other = tuple(p + m for p, m in zip(place, move))
        if all(0 <= o < d for o, d in zip(other, self.dims)):
            return True, self.index(other)
        axis = (number - 1) // 2
        across = [o for k, o in enumerate(place) if k != axis]
        width = [d for k, d in enumerate(self.dims) if k != axis][1]
        return False, across[0] * width + across[1]


def rolls(axis, size):
    if axis == "gx" and size > 2:
        return [
            [(i, (i + 1) % size) for i in range(size)],
            [((i + 1) % size, i) for i in range(size)],
        ]
    out = []
    for start in range(2 if size > 2 else 1):
        pairs = []
        for i in range(start, size - 1, 2):
            pairs += [(i, i + 1), (i + 1, i)]
        out.append(pairs)
    return out


def is_ring(axis, size):
    return axis == "gx" and size > 2


def ordered_send(axis, size, low, high):
    if is_ring(axis, size):
        return [high, low]
    even = lax.axis_index(axis) % 2 == 0
    first = jnp.where(even, high, low)
    if size == 2:
        return [first]
    return [first, jnp.where(even, low, high)]


def ordered_receive(axis, size, blocks):
    if is_ring(axis, size):
        return blocks[0], blocks[1]
    if size == 2:
        return blocks[0], blocks[0]
    even = lax.axis_index(axis) % 2 == 0
    return jnp.where(even, blocks[1], blocks[0]), jnp.where(even, blocks[0], blocks[1])


def at_end(axis, size, side):
    edge = size - 1 if side > 0 else 0
    return lax.axis_index(axis) == edge


def exchange(blocks, sizes):
    out = []
    k = 0
    for axis, size in zip(AXES, sizes):
        for pairs in rolls(axis, size):
            out.append(lax.ppermute(blocks[k], axis, pairs))
            k += 1
    return out


def per_axis(refs, sizes):
    out = []
    k = 0
    for axis, size in zip(AXES, sizes):
        n = len(rolls(axis, size))
        out.append(refs[k : k + n])
        k += n
    return out


def send_count(sizes):
    return sum(len(rolls(a, s)) for a, s in zip(AXES, sizes))


def put_faces(plan, sizes, state_ref, send_refs):
    for axis, refs in enumerate(per_axis(send_refs, sizes)):
        low = plan.face(axis, -1)
        high = plan.face(axis, 1)
        width = len(low)
        for k in range(width):
            a = state_ref[:, low[k], :]
            b = state_ref[:, high[k], :]
            for ref, block in zip(refs, ordered_send(AXES[axis], sizes[axis], a, b)):
                ref[pl.ds(k, FIELDS, stride=width), :] = block


def pack_kernel(plan, sizes, pos, vel, spin, rad, counts, pressure, *outs):
    state = outs[0]
    sends = outs[1:]
    state[0:3] = pos[...]
    state[3:6] = vel[...]
    state[6:9] = spin[...]
    slots = rad.shape[-1]
    lane = lax.broadcasted_iota(jnp.int32, (1, slots), 1)
    for b in range(plan.count):
        state[9, b : b + 1, :] = jnp.where(lane < counts[b], rad[b : b + 1, :], DEAD)
    put_faces(plan, sizes, state, sends)
    nx, ny, nz = pressure.shape
    lanes = slots
    chunks = nz // lanes
    split = per_axis(sends, sizes)
    base = FIELDS * len(plan.face(0, 1))
    for ref, block in zip(
        split[0], ordered_send("gx", sizes[0], pressure[0], pressure[nx - 1])
    ):
        for c in range(chunks):
            ref[base + c * ny : base + (c + 1) * ny, :] = block[:, c * lanes : (c + 1) * lanes]
    base = FIELDS * len(plan.face(1, 1))
    for ref, block in zip(
        split[1], ordered_send("gy", sizes[1], pressure[:, 0, :], pressure[:, ny - 1, :])
    ):
        for c in range(chunks):
            ref[base + c * nx : base + (c + 1) * nx, :] = block[:, c * lanes : (c + 1) * lanes]
    base = FIELDS * len(plan.face(2, 1))
    wide = lax.broadcasted_iota(jnp.int32, (ny, lanes), 1)
    low = jnp.zeros((ny, lanes), f32)
    high = jnp.zeros((ny, lanes), f32)
    for x in range(nx):
        low = jnp.where(wide == x, jnp.broadcast_to(pressure[x, :, 0:1], (ny, lanes)), low)
        high = jnp.where(
            wide == x, jnp.broadcast_to(pressure[x, :, nz - 1 : nz], (ny, lanes)), high
        )
    for ref, block in zip(split[2], ordered_send("gz", sizes[2], low, high)):
        ref[base : base + ny, :] = block


def spread_own(b, state, radius, spread, columns):
    for f in range(3):
        columns[f : f + 1, :] = state[f, b : b + 1, :]
        columns[3 + f : 4 + f, :] = state[3 + f, b : b + 1, :] * (normal_damp / normal_stiff)
    columns[6:7, :] = radius[b : b + 1, :]
    columns[7:8, :] = radius[b : b + 1, :]
    slots = columns.shape[-1]
    turned = jnp.transpose(columns[...], (1, 0))
    for f in range(7):
        spread[f] = jnp.broadcast_to(turned[:, f : f + 1], (slots, slots))


def pair_forces(b, chosen, others, spread, parts, total, first):
    slots = spread.shape[-1]
    trips = slots // (8 * GROUP)

    def trip(g, carry):
        for t in range(GROUP):
            rows = pl.ds(pl.multiple_of((g * GROUP + t) * 8, 8), 8)
            mine = [spread[f, rows, :] for f in range(7)]
            sums = None
            for n in chosen:
                their = [jnp.broadcast_to(others[n, f, b : b + 1, :], (8, slots)) for f in range(7)]
                sep = [mine[k] - their[k] for k in range(3)]
                square = sep[0] * sep[0] + (sep[1] * sep[1] + (sep[2] * sep[2] + soft_length**2))
                inverse = lax.rsqrt(square)
                over = (mine[6] + their[6]) - square * inverse
                positive = jnp.maximum(over, 0.0)
                root = positive * lax.rsqrt(jnp.maximum(over, TINY))
                dot = (mine[3] - their[3]) * sep[0]
                dot = dot + (mine[4] - their[4]) * sep[1]
                dot = dot + (mine[5] - their[5]) * sep[2]
                weight = (positive - dot * inverse) * (root * inverse)
                new = [weight * sep[k] for k in range(3)]
                sums = new if sums is None else [s + w for s, w in zip(sums, new)]
            for k in range(3):
                parts[k, rows, :] = sums[k]
        return carry

    lax.fori_loop(0, trips, trip, 0)
    for k in range(3):
        row = jnp.sum(jnp.transpose(parts[k], (1, 0)), axis=0, keepdims=True) * normal_stiff
        total[k, b : b + 1, :] = row if first else total[k, b : b + 1, :] + row


def scale_rows(n, place, rows):
    move = neighbours[n]
    return rows


def own_pairs(plan, state, radius, total, others, spread, columns, parts):
    scale = normal_damp / normal_stiff
    places = plan.places()
    for n in range(7):
        for place in places:
            own, other = plan.neighbour(place, n)
            b = plan.index(place)
            if not own:
                continue
            for f in range(3):
                row = state[f, other : other + 1, :]
                if neighbours[n][f]:
                    row = row + float(neighbours[n][f])
                others[n, f, b : b + 1, :] = row
                others[n, 3 + f, b : b + 1, :] = state[3 + f, other : other + 1, :] * scale
            others[n, 6, b : b + 1, :] = state[9, other : other + 1, :]
    for place in places:
        b = plan.index(place)
        spread_own(b, state, radius, spread, columns)
        chosen = [n for n in range(7) if plan.neighbour(place, n)[0]]
        pair_forces(b, chosen, others, spread, parts, total, True)


def inner_kernel(plan, with_fluid, *refs):
    if with_fluid:
        state, radius, cells, fluid, total, gas, others, spread, columns, parts = refs
    else:
        state, radius, total, others, spread, columns, parts = refs
    own_pairs(plan, state, radius, total, others, spread, columns, parts)
    if not with_fluid:
        return
    slots = radius.shape[-1]
    span = [s // d for s, d in zip(fluid.shape[1:], plan.dims)]
    sub = lax.broadcasted_iota(jnp.int32, (8, slots), 0)
    for place in plan.places():
        b = plan.index(place)
        cell = cells[b : b + 1, :]
        column = jnp.broadcast_to(cell % span[2], (8, slots))
        row = jnp.broadcast_to(cell // span[2], (8, slots)) - sub
        sums = [jnp.zeros((8, slots), f32) for c in range(3)]
        for a in range(span[0]):
            for h in range(span[1] // 8):
                hit = row == a * span[1] + h * 8
                y0 = place[1] * span[1] + h * 8
                z0 = place[2] * span[2]
                for c in range(3):
                    block = fluid[c, place[0] * span[0] + a, y0 : y0 + 8, z0 : z0 + span[2]]
                    got = jnp.take_along_axis(block, column, axis=1)
                    sums[c] = jnp.where(hit, got, sums[c])
        for c in range(3):
            gas[c, b : b + 1, :] = jnp.sum(sums[c], axis=0, keepdims=True)


def step_core(plan, sizes, state, radius, inner, springs, partners, gas, halos, out, new_springs,
              around, others, spread, columns, parts, outer):
    scale = normal_damp / normal_stiff
    places = plan.places()
    slots = radius.shape[-1]
    split = per_axis(halos, sizes)
    around[0] = state[...]
    for axis in range(3):
        width = len(plan.face(axis, 1))
        for place in places:
            b = plan.index(place)
            for side in (0, 1):
                n = 1 + 2 * axis + side
                own, other = plan.neighbour(place, n)
                if own:
                    around[n, :, b, :] = state[:, other, :]
                    continue
                got = [ref[pl.ds(other, FIELDS, stride=width), :] for ref in split[axis]]
                before, after = ordered_receive(AXES[axis], sizes[axis], got)
                around[n, :, b, :] = after if side else before
    sub = lax.broadcasted_iota(jnp.int32, (plan.count, slots), 0)
    inner_count = [plan.dims[1] * plan.dims[2], plan.dims[2], 1]
    for n in range(1, 7):
        axis = (n - 1) // 2
        side = 1 if n % 2 == 0 else -1
        edge = plan.dims[axis] - 1 if side > 0 else 0
        level = sub // inner_count[axis] % plan.dims[axis]
        outside = (level == edge) & at_end(AXES[axis], sizes[axis], side)
        reach = around[n, 9]
        around[n, 9] = jnp.where(outside | (reach <= 0.0), DEAD, reach)
        for f in range(3):
            others[n, f] = around[n, f] + float(neighbours[n][f])
            others[n, 3 + f] = around[n, 3 + f] * scale
        others[n, 6] = around[n, 9]
    for place in places:
        b = plan.index(place)
        chosen = [n for n in range(7) if not plan.neighbour(place, n)[0]]
        spread_own(b, state, radius, spread, columns)
        pair_forces(b, chosen, others, spread, parts, outer, True)
    place_i = [state[k] for k in range(3)]
    speed_i = [state[3 + k] for k in range(3)]
    turn_i = [state[6 + k] for k in range(3)]
    rad_i = radius[...]
    shear_sum = [jnp.zeros_like(rad_i) for k in range(3)]
    twist = [jnp.zeros_like(rad_i) for k in range(3)]
    for h in range(partners.shape[0]):
        code = partners[h]
        valid = code >= 0
        code = jnp.maximum(code, 0)
        which = code // slots
        member = code % slots
        picked = []
        for f in range(FIELDS):
            value = jnp.take_along_axis(around[0, f], member, axis=1)
            for n in range(1, 7):
                got = jnp.take_along_axis(around[n, f], member, axis=1)
                value = jnp.where(which == n, got, value)
            picked.append(value)
        alive = valid & (picked[9] > 0.0)
        sep = []
        for k in range(3):
            shift = jnp.where(which == 2 + 2 * k, 1.0, jnp.where(which == 1 + 2 * k, -1.0, 0.0))
            sep.append(place_i[k] - picked[k] - shift)
        distance = jnp.sqrt(sep[0] * sep[0] + sep[1] * sep[1] + sep[2] * sep[2] + soft_length**2)
        unit = [s / distance for s in sep]
        over = jnp.maximum(rad_i + picked[9] - distance, 0.0)
        root = jnp.sqrt(over)
        rel = [speed_i[k] - picked[3 + k] for k in range(3)]
        approach = rel[0] * unit[0] + rel[1] * unit[1] + rel[2] * unit[2]
        pressing = normal_stiff * over * root - normal_damp * root * approach
        lever = [rad_i * turn_i[k] + picked[9] * picked[6 + k] for k in range(3)]
        contact = [
            rel[k]
            - (
                lever[(k + 1) % 3] * unit[(k + 2) % 3]
                - lever[(k + 2) % 3] * unit[(k + 1) % 3]
            )
            for k in range(3)
        ]
        along = contact[0] * unit[0] + contact[1] * unit[1] + contact[2] * unit[2]
        old = [springs[k, h] for k in range(3)]
        old_along = old[0] * unit[0] + old[1] * unit[1] + old[2] * unit[2]
        stretched = [
            old[k] - old_along * unit[k] + time_step * (contact[k] - along * unit[k])
            for k in range(3)
        ]
        length = jnp.sqrt(
            stretched[0] * stretched[0] + stretched[1] * stretched[1] + stretched[2] * stretched[2]
        )
        limit = jnp.minimum(
            1.0, friction * jnp.abs(pressing) / jnp.maximum(shear_stiff * length, force_floor)
        )
        limit = jnp.where(alive, limit, 0.0)
        fresh = [limit * stretched[k] for k in range(3)]
        for k in range(3):
            new_springs[k, h] = fresh[k]
            shear_sum[k] = shear_sum[k] - shear_stiff * fresh[k]
            twist[k] = twist[k] - shear_stiff * (
                fresh[(k + 1) % 3] * unit[(k + 2) % 3] - fresh[(k + 2) % 3] * unit[(k + 1) % 3]
            )
    safe = jnp.where(rad_i > 0.0, rad_i, 1.0)
    ratio = safe / 0.1
    mass = ratio * ratio * ratio
    inertia = 0.4 * mass * safe * safe
    for k in range(3):
        force = inner[k] + outer[k] + shear_sum[k] + drag_coeff * (gas[k] - speed_i[k])
        lift = gravity if k == 2 else 0.0
        speed = speed_i[k] + time_step * (force / mass - lift)
        out[k] = place_i[k] + time_step * speed
        out[3 + k] = speed
        out[6 + k] = turn_i[k] + time_step * (rad_i * twist[k]) / inertia
    out[9] = state[9]


def middle_kernel(plan, sizes, *refs):
    n = send_count(sizes)
    state, radius, inner, springs, partners, gas = refs[:6]
    halos = refs[6 : 6 + n]
    out, new_springs = refs[6 + n : 8 + n]
    sends = refs[8 + n : 8 + 2 * n]
    scratch = refs[8 + 2 * n :]
    step_core(plan, sizes, state, radius, inner, springs, partners, gas, halos, out, new_springs,
              *scratch)
    put_faces(plan, sizes, out, sends)


def last_kernel(plan, sizes, *refs):
    n = send_count(sizes)
    state, radius, inner, springs, partners, gas, departures = refs[:7]
    halos = refs[7 : 7 + n]
    places, speeds, turns, new_springs = refs[7 + n : 11 + n]
    sends = refs[11 + n : 11 + 2 * n]
    out = refs[11 + 2 * n]
    scratch = refs[12 + 2 * n :]
    step_core(plan, sizes, state, radius, inner, springs, partners, gas, halos, out, new_springs,
              *scratch)
    places[...] = out[0:3]
    speeds[...] = out[3:6]
    turns[...] = out[6:9]
    slots = radius.shape[-1]
    hist = partners.shape[0]
    count = plan.count
    sub = lax.broadcasted_iota(jnp.int32, (count, slots), 0)
    values = [out[f] for f in range(9)] + [radius[...]]
    values += [new_springs[k, h] for k in range(3) for h in range(hist)]
    values += [(partners[h] + 1).astype(f32) for h in range(hist)]
    width = len(values)
    picks = [[], [], [], [], [], []]
    for d in range(6):
        leaving = jnp.broadcast_to(departures[d : d + 1, :], (count, slots))
        hit = (leaving // slots == sub) & (leaving >= 0)
        member = jnp.maximum(leaving, 0) % slots
        for v in values:
            got = jnp.where(hit, jnp.take_along_axis(v, member, axis=1), 0.0)
            picks[d].append(jnp.sum(got, axis=0, keepdims=True))
    split = per_axis(sends, sizes)
    for axis in range(3):
        for f in range(width):
            blocks = ordered_send(
                AXES[axis], sizes[axis], picks[2 * axis][f], picks[2 * axis + 1][f]
            )
            for ref, block in zip(split[axis], blocks):
                ref[f : f + 1, :] = block


def deposit_kernel(plan, sizes, *refs):
    n = send_count(sizes)
    state, radius, counts, cells, gas, pressure, source = refs[:7]
    halos = refs[7 : 7 + n]
    force, new_pressure = refs[7 + n :]
    slots = radius.shape[-1]
    nx, ny, nz = pressure.shape
    lanes = slots
    chunks = nz // lanes
    span = [s // d for s, d in zip(pressure.shape, plan.dims)]
    rows = span[0] * span[1]
    lane = lax.broadcasted_iota(jnp.int32, (1, slots), 1)
    high_row = lax.broadcasted_iota(jnp.int32, (rows, slots), 0)
    column_row = lax.broadcasted_iota(jnp.int32, (span[2], slots), 0)
    for place in plan.places():
        b = plan.index(place)
        cell = cells[b : b + 1, :]
        live = lane < counts[b]
        rad = radius[b : b + 1, :]
        values = [
            jnp.where(live, drag_coeff * (state[c, b : b + 1, :] - gas[c, b : b + 1, :]), 0.0)
            for c in range(3)
        ]
        values.append(jnp.where(live, 4.0 / 3.0 * math.pi * rad * rad * rad, 0.0))
        at_row = high_row == cell // span[2]
        at_column = (column_row == cell % span[2]).astype(jnp.bfloat16)
        halves = []
        for v in values:
            top = v.astype(jnp.bfloat16).astype(f32)
            left = v - top
            mid = left.astype(jnp.bfloat16).astype(f32)
            low = left - mid
            halves.append(
                jnp.concatenate(
                    [jnp.where(at_row, part, 0.0).astype(jnp.bfloat16) for part in (top, mid, low)],
                    axis=1,
                )
            )
        left = jnp.concatenate(halves, axis=0)
        right = jnp.concatenate([at_column] * 3, axis=1)
        got = lax.dot_general(
            left, right, (((1,), (1,)), ((), ())), preferred_element_type=f32
        )
        x0, y0, z0 = (p * s for p, s in zip(place, span))
        block = (slice(x0, x0 + span[0]), slice(y0, y0 + span[1]), slice(z0, z0 + span[2]))
        pieces = [got[c * rows : (c + 1) * rows].reshape(span) for c in range(4)]
        for c in range(3):
            force[(c,) + block] = pieces[c]
        new_pressure[block] = volume_coeff * pieces[3] + pieces[2]
    split = per_axis(halos, sizes)
    dead = [
        [at_end(AXES[axis], sizes[axis], side) for side in (-1, 1)] for axis in range(3)
    ]
    base = FIELDS * len(plan.face(0, 1))
    slabs = []
    for ref in split[0]:
        slabs.append(
            jnp.concatenate(
                [ref[base + c * ny : base + (c + 1) * ny, :] for c in range(chunks)], axis=1
            )
        )
    x_ends = ordered_receive("gx", sizes[0], slabs)
    x_ends = [jnp.where(dead[0][s], 0.0, x_ends[s]) for s in (0, 1)]
    base = FIELDS * len(plan.face(1, 1))
    slabs = []
    for ref in split[1]:
        slabs.append(
            jnp.concatenate(
                [ref[base + c * nx : base + (c + 1) * nx, :] for c in range(chunks)], axis=1
            )
        )
    y_ends = ordered_receive("gy", sizes[1], slabs)
    y_ends = [jnp.where(dead[1][s], 0.0, y_ends[s]) for s in (0, 1)]
    base = FIELDS * len(plan.face(2, 1))
    z_ends = ordered_receive("gz", sizes[2], [ref[base : base + ny, :] for ref in split[2]])
    z_ends = [jnp.where(dead[2][s], 0.0, z_ends[s]) for s in (0, 1)]
    row = lax.broadcasted_iota(jnp.int32, (ny, nz), 0)
    column = lax.broadcasted_iota(jnp.int32, (ny, nz), 1)
    for x in range(nx):
        here = pressure[x]
        total = pressure[x - 1] if x > 0 else x_ends[0]
        total = total + (pressure[x + 1] if x < nx - 1 else x_ends[1])
        total = total + jnp.where(row == 0, y_ends[0][x : x + 1, :], pltpu.roll(here, 1, 0))
        total = total + jnp.where(
            row == ny - 1, y_ends[1][x : x + 1, :], pltpu.roll(here, ny - 1, 0)
        )
        total = total + jnp.where(column == 0, z_ends[0][:, x : x + 1], pltpu.roll(here, 1, 1))
        total = total + jnp.where(
            column == nz - 1, z_ends[1][:, x : x + 1], pltpu.roll(here, nz - 1, 1)
        )
        new_pressure[x] = (total + (source[x] + new_pressure[x])) * (1.0 / 6.0)


def arrive_kernel(sizes, *refs):
    n = send_count(sizes)
    halos = refs[:n]
    state, codes = refs[n:]
    split = per_axis(halos, sizes)
    width = state.shape[0]
    hist = codes.shape[0]
    for axis in range(3):
        got = [ref[0 : width + hist, :] for ref in split[axis]]
        before, after = ordered_receive(AXES[axis], sizes[axis], got)
        after = jnp.where(at_end(AXES[axis], sizes[axis], 1), 0.0, after)
        before = jnp.where(at_end(AXES[axis], sizes[axis], -1), 0.0, before)
        for d, block in ((2 * axis, after), (2 * axis + 1, before)):
            state[:, d, :] = block[0:width]
            codes[:, d, :] = block[width : width + hist].astype(jnp.int32) - 1


def call(kernel, outs, scratch, args, smem=(), flops=0):
    specs = [
        pl.BlockSpec(memory_space=pltpu.SMEM) if k in smem else pl.BlockSpec(memory_space=pltpu.VMEM)
        for k in range(len(args))
    ]
    return pl.pallas_call(
        kernel,
        out_shape=[jax.ShapeDtypeStruct(s, d) for s, d in outs],
        in_specs=specs,
        out_specs=[pl.BlockSpec(memory_space=pltpu.VMEM)] * len(outs),
        scratch_shapes=scratch,
        compiler_params=pltpu.CompilerParams(vmem_limit_bytes=32 * 1024 * 1024),
        cost_estimate=pl.CostEstimate(flops=flops, bytes_accessed=1 << 20, transcendentals=0),
    )(*args)


def body(sizes, positions, velocities, spins, radii, counts, springs, partners, cells, departures,
         fluid_velocity, pressure, pressure_source):
    plan = Plan(radii.shape[:3])
    count = plan.count
    slots = radii.shape[3]
    hist = partners.shape[0]
    nx, ny, nz = pressure.shape
    chunks = nz // slots
    flat = lambda a: a.reshape(a.shape[:-4] + (count, slots))
    pos, vel, spin = flat(positions), flat(velocities), flat(spins)
    radius = radii.reshape(count, slots)
    springs = springs.reshape(3, hist, count, slots)
    partners = partners.reshape(hist, count, slots)
    cells = cells.reshape(count, slots)
    counts = counts.reshape(count)
    leaving = departures.reshape(6, slots)

    faces = [FIELDS * len(plan.face(a, 1)) for a in range(3)]
    extra = [chunks * ny, chunks * nx, ny]
    vm = lambda *s: pltpu.VMEM(s, f32)

    def sends(rows):
        out = []
        for a in range(3):
            for _ in rolls(AXES[a], sizes[a]):
                out.append(((rows[a], slots), f32))
        return out

    pair_scratch = [vm(7, 7, count, slots), vm(7, slots, slots), vm(8, slots), vm(3, slots, slots)]
    step_scratch = [vm(7, FIELDS, count, slots)] + pair_scratch + [vm(3, count, slots)]
    state_shape = ((FIELDS, count, slots), f32)
    three = ((3, count, slots), f32)
    spring_shape = ((3, hist, count, slots), f32)
    bind = functools.partial

    state, *out = call(
        bind(pack_kernel, plan, sizes),
        [state_shape] + sends([f + e for f, e in zip(faces, extra)]),
        [],
        [pos, vel, spin, radius, counts, pressure],
        smem=(4,),
        flops=1 << 20,
    )
    first_halos = exchange(out, sizes)
    inner, gas = call(
        bind(inner_kernel, plan, True),
        [three, three],
        pair_scratch,
        [state, radius, cells, fluid_velocity],
        flops=1 << 25,
    )
    state, springs, *out = call(
        bind(middle_kernel, plan, sizes),
        [state_shape, spring_shape] + sends(faces),
        step_scratch,
        [state, radius, inner, springs, partners, gas] + first_halos,
        flops=1 << 25,
    )
    halos = exchange(out, sizes)
    (inner,) = call(
        bind(inner_kernel, plan, False), [three], pair_scratch, [state, radius], flops=1 << 25
    )
    width = 10 + 4 * hist
    padded = (width + 7) // 8 * 8
    places, speeds, turns, springs, *out = call(
        bind(last_kernel, plan, sizes),
        [three, three, three, spring_shape] + sends([padded] * 3),
        [vm(FIELDS, count, slots)] + step_scratch,
        [state, radius, inner, springs, partners, gas, leaving] + halos,
        flops=1 << 25,
    )
    arrivals = exchange(out, sizes)
    force, new_pressure = call(
        bind(deposit_kernel, plan, sizes),
        [((3, nx, ny, nz), f32), ((nx, ny, nz), f32)],
        [],
        [speeds, radius, counts, cells, gas, pressure, pressure_source] + first_halos,
        smem=(2,),
        flops=1 << 25,
    )
    arrived, arrived_partners = call(
        bind(arrive_kernel, sizes),
        [((10 + 3 * hist, 6, slots), f32), ((hist, 6, slots), jnp.int32)],
        [],
        arrivals,
        flops=1 << 20,
    )
    wide = lambda a: a.reshape(a.shape[:-2] + radii.shape)
    return (
        wide(places),
        wide(speeds),
        wide(turns),
        wide(springs),
        force,
        new_pressure,
        arrived[None, None, None],
        arrived_partners[None, None, None],
    )


def solution(mesh):
    sizes = tuple(mesh.shape[a] for a in AXES)
    return jax.shard_map(
        functools.partial(body, sizes),
        mesh=mesh,
        in_specs=(
            P(None, "gx", "gy", "gz", None),
            P(None, "gx", "gy", "gz", None),
            P(None, "gx", "gy", "gz", None),
            P("gx", "gy", "gz", None),
            P("gx", "gy", "gz"),
            P(None, None, "gx", "gy", "gz", None),
            P(None, "gx", "gy", "gz", None),
            P("gx", "gy", "gz", None),
            P("gx", "gy", "gz", None, None),
            P(None, "gx", "gy", "gz"),
            P("gx", "gy", "gz"),
            P("gx", "gy", "gz"),
        ),
        out_specs=(
            P(None, "gx", "gy", "gz", None),
            P(None, "gx", "gy", "gz", None),
            P(None, "gx", "gy", "gz", None),
            P(None, None, "gx", "gy", "gz", None),
            P(None, "gx", "gy", "gz"),
            P("gx", "gy", "gz"),
            P("gx", "gy", "gz", None, None, None),
            P("gx", "gy", "gz", None, None, None),
        ),
        check_vma=False,
    )
```

profile of v0, /device:TPU:0, one launch (start us, length us, event | category | flops | bytes accessed | tf_op | source)
XLA Modules:
  0.0 57.3 jit_solution(11081158082934175319)
XLA Ops:
  0.7 0.8 %reshape.59.counts.refs_2_ = s32[8]{0:T(128)S(1)} reshape(s32[2,2,2]{2,1,0:T(2,128)} %param.16) | data formatting | bytes 64 | tf_op jit(solution)/shard_map/reshape | solution.py:586
  1.4 1.0 %copy-done = f32[16,32,256]{2,1,0:T(8,128)S(1)} copy-done((f32[16,32,256]{2,1,0:T(8,128)S(1)}, f32[16,32,256]{2,1,0:T(8,128)}, u32[]{:S(2)}) %copy-start) | copy-done | bytes 524312
  2.5 0.7 %copy-done.4 = f32[2,2,2,128]{3,2,1,0:T(2,128)S(1)} copy-done((f32[2,2,2,128]{3,2,1,0:T(2,128)S(1)}, f32[2,2,2,128]{3,2,1,0:T(2,128)}, u32[]{:S(2)}) %copy-start.4) | copy-done | bytes 4120
  3.2 0.7 %copy-done.10 = f32[3,2,2,2,128]{4,3,2,1,0:T(2,128)S(1)} copy-done((f32[3,2,2,2,128]{4,3,2,1,0:T(2,128)S(1)}, f32[3,2,2,2,128]{4,3,2,1,0:T(2,128)}, u32[]{:S(2)}) %copy-start.10) | copy-done | bytes 12312
  3.9 0.7 %copy-done.11 = f32[3,2,2,2,128]{4,3,2,1,0:T(2,128)S(1)} copy-done((f32[3,2,2,2,128]{4,3,2,1,0:T(2,128)S(1)}, f32[3,2,2,2,128]{4,3,2,1,0:T(2,128)}, u32[]{:S(2)}) %copy-start.11) | copy-done | bytes 12312
  4.6 0.7 %copy-done.12 = f32[3,2,2,2,128]{4,3,2,1,0:T(2,128)S(1)} copy-done((f32[3,2,2,2,128]{4,3,2,1,0:T(2,128)S(1)}, f32[3,2,2,2,128]{4,3,2,1,0:T(2,128)}, u32[]{:S(2)}) %copy-start.12) | copy-done | bytes 12312
  5.3 0.8 %shard_map.179 = (f32[10,8,128]{2,1,0:T(8,128)S(1)}, f32[104,128]{1,0:T(8,128)S(1)}, f32[104,128]{1,0:T(8,128)S(1)}, f32[72,128]{1,0:T(8,128)S(1)}, f32[72,128]{1,0:T(8,128)S(1)}, /*index=5*/f32[72,128]{1,0:T(8,128)S(1)}) custom-call(f32[3,8,128]{2,1,0:T(8,128)S(1)} %bitcast.31, f32[3,8,128]{2,1,0:T(8,128)S(1)} %bitcast.32, f32[3,8,128]{2,1,0:T(8,128)S(1)} %bitcast.33, ...), custom_call_target="tpu_custom_call" | custom-call | flops 1048576 | bytes 1048576 | tf_op jit(solution)/shard_map/pallas_call | solution.py:561
  6.7 2.0 %collective-permute-start.1 = (f32[104,128]{1,0:T(8,128)S(1)}, f32[104,128]{1,0:T(8,128)S(1)}, u32[]{:S(2)}, u32[]{:S(2)}) collective-permute-start(f32[104,128]{1,0:T(8,128)S(1)} %get-tuple-element.40), channel_id=1, source_target_pairs={{8,0},{16,8},{24,16},{0,24},{9,1},{17,9},{25,17},{1,25},{10,2},{18... | collective-permute-start | bytes 159752 | tf_op jit(solution)/shard_map/ppermute | solution.py:107
  8.6 2.3 %collective-permute-start.2 = (f32[72,128]{1,0:T(8,128)S(1)}, f32[72,128]{1,0:T(8,128)S(1)}, u32[]{:S(2)}, u32[]{:S(2)}) collective-permute-start(f32[72,128]{1,0:T(8,128)S(1)} %get-tuple-element.41), channel_id=1, source_target_pairs={{0,2},{2,0},{4,6},{6,4},{1,3},{3,1},{5,7},{7,5},{8,10},{10,8},{12,... | collective-permute-start | bytes 110600 | tf_op jit(solution)/shard_map/ppermute | solution.py:107
  11.6 1.6 %collective-permute-start.4 = (f32[72,128]{1,0:T(8,128)S(1)}, f32[72,128]{1,0:T(8,128)S(1)}, u32[]{:S(2)}, u32[]{:S(2)}) collective-permute-start(f32[72,128]{1,0:T(8,128)S(1)} %get-tuple-element.43), channel_id=1, source_target_pairs={{0,1},{1,0},{2,3},{3,2},{4,5},{5,4},{6,7},{7,6},{8,9},{9,8},{10,11... | collective-permute-start | bytes 110600 | tf_op jit(solution)/shard_map/ppermute | solution.py:107
  13.2 1.4 %copy-done.2 = f32[3,16,32,256]{3,2,1,0:T(8,128)S(1)} copy-done((f32[3,16,32,256]{3,2,1,0:T(8,128)S(1)}, f32[3,16,32,256]{3,2,1,0:T(8,128)}, u32[]{:S(2)}) %copy-start.2) | copy-done | bytes 1572888
  14.6 0.7 %copy-done.8 = s32[2,2,2,128]{3,2,1,0:T(2,128)S(1)} copy-done((s32[2,2,2,128]{3,2,1,0:T(2,128)S(1)}, s32[2,2,2,128]{3,2,1,0:T(2,128)}, u32[]{:S(2)}) %copy-start.8) | copy-done | bytes 4120
  15.3 6.2 %shard_map.180 = (f32[3,8,128]{2,1,0:T(8,128)S(1)}, f32[3,8,128]{2,1,0:T(8,128)S(1)}) custom-call(f32[10,8,128]{2,1,0:T(8,128)S(1)} %get-tuple-element.36.refs_0_, f32[8,128]{1,0:T(8,128)S(1)} %bitcast.17, s32[8,128]{1,0:T(8,128)S(1)} %bitcast.26, f32[3,16,32,256]{3,2,1,0:T(8,128)S(1)} %copy-done.2), custom_call_target="tpu_custom_call" | custom-call | flops 33554432 | bytes 1048576 | tf_op jit(solution)/shard_map/pallas_call | solution.py:561
  21.6 5.8 %shard_map.181 = (f32[10,8,128]{2,1,0:T(8,128)S(1)}, f32[3,4,8,128]{3,2,1,0:T(8,128)S(1)}, f32[40,128]{1,0:T(8,128)S(1)}, f32[40,128]{1,0:T(8,128)S(1)}, f32[40,...) custom-call(f32[10,8,128]{2,1,0:T(8,128)S(1)} %get-tuple-element.36.refs_0_, f32[8,128]{1,0:T(8,128)S(1)} %bitcast.18, ...), custom_call_target="tpu_custom_call" | custom-call | flops 33554432 | bytes 1048576 | tf_op jit(solution)/shard_map/pallas_call | solution.py:561
  27.4 1.7 %collective-permute-start.6 = (f32[40,128]{1,0:T(8,128)S(1)}, f32[40,128]{1,0:T(8,128)S(1)}, u32[]{:S(2)}, u32[]{:S(2)}) collective-permute-start(f32[40,128]{1,0:T(8,128)S(1)} %get-tuple-element.47), channel_id=1, source_target_pairs={{8,0},{16,8},{24,16},{0,24},{9,1},{17,9},{25,17},{1,25},{10,2},{18... | collective-permute-start | bytes 61448 | tf_op jit(solution)/shard_map/ppermute | solution.py:107
  29.2 4.4 %collective-permute-start.7 = (f32[40,128]{1,0:T(8,128)S(1)}, f32[40,128]{1,0:T(8,128)S(1)}, u32[]{:S(2)}, u32[]{:S(2)}) collective-permute-start(f32[40,128]{1,0:T(8,128)S(1)} %get-tuple-element.48), channel_id=1, source_target_pairs={{0,2},{2,0},{4,6},{6,4},{1,3},{3,1},{5,7},{7,5},{8,10},{10,8},{12,... | collective-permute-start | bytes 61448 | tf_op jit(solution)/shard_map/ppermute | solution.py:107
  34.8 5.8 %shard_map.182.refs_2_ = f32[3,8,128]{2,1,0:T(8,128)S(1)} custom-call(f32[10,8,128]{2,1,0:T(8,128)S(1)} %get-tuple-element.44.refs_0_, f32[8,128]{1,0:T(8,128)S(1)} %bitcast.19), custom_call_target="tpu_custom_call" | custom-call | flops 33554432 | bytes 1048576 | tf_op jit(solution)/shard_map/pallas_call | solution.py:561
  40.6 6.3 %shard_map.183 = (f32[3,8,128]{2,1,0:T(8,128)}, f32[3,8,128]{2,1,0:T(8,128)}, f32[3,8,128]{2,1,0:T(8,128)}, f32[3,4,8,128]{3,2,1,0:T(8,128)}, f32[32,128]{1,0:T(...) custom-call(f32[10,8,128]{2,1,0:T(8,128)S(1)} %get-tuple-element.44.r, ...), custom_call_target="tpu_custom_call" | custom-call | flops 33554432 | bytes 1048576 | tf_op jit(solution)/shard_map/pallas_call | solution.py:561
  46.9 1.7 %collective-permute-start.11 = (f32[32,128]{1,0:T(8,128)S(1)}, f32[32,128]{1,0:T(8,128)S(1)}, u32[]{:S(2)}, u32[]{:S(2)}) collective-permute-start(f32[32,128]{1,0:T(8,128)S(1)} %get-tuple-element.58), channel_id=1, source_target_pairs={{8,0},{16,8},{24,16},{0,24},{9,1},{17,9},{25,17},{1,25},{10,2},{18... | collective-permute-start | bytes 49160 | tf_op jit(solution)/shard_map/ppermute | solution.py:107
  48.7 1.3 %collective-permute-start.12 = (f32[32,128]{1,0:T(8,128)S(1)}, f32[32,128]{1,0:T(8,128)S(1)}, u32[]{:S(2)}, u32[]{:S(2)}) collective-permute-start(f32[32,128]{1,0:T(8,128)S(1)} %get-tuple-element.59), channel_id=1, source_target_pairs={{0,2},{2,0},{4,6},{6,4},{1,3},{3,1},{5,7},{7,5},{8,10},{10,8},{12,... | collective-permute-start | bytes 49160 | tf_op jit(solution)/shard_map/ppermute | solution.py:107
  50.6 1.6 %collective-permute-start.14 = (f32[32,128]{1,0:T(8,128)S(1)}, f32[32,128]{1,0:T(8,128)S(1)}, u32[]{:S(2)}, u32[]{:S(2)}) collective-permute-start(f32[32,128]{1,0:T(8,128)S(1)} %get-tuple-element.61), channel_id=1, source_target_pairs={{0,1},{1,0},{2,3},{3,2},{4,5},{5,4},{6,7},{7,6},{8,9},{9,8},{10,11... | collective-permute-start | bytes 49160 | tf_op jit(solution)/shard_map/ppermute | solution.py:107
  52.2 0.7 %copy-done.9 = f32[3,8,128]{2,1,0:T(8,128)S(1)} copy-done((f32[3,8,128]{2,1,0:T(8,128)S(1)}, f32[3,8,128]{2,1,0:T(8,128)}, u32[]{:S(2)}) %copy-start.9) | copy-done | bytes 12312
  52.9 3.0 %shard_map.184 = (f32[3,16,32,256]{3,2,1,0:T(8,128)}, f32[16,32,256]{2,1,0:T(8,128)}) custom-call(f32[3,8,128]{2,1,0:T(8,128)S(1)} %copy-done.9, f32[8,128]{1,0:T(8,128)S(1)} %bitcast.21, s32[8]{0:T(128)S(1)} %reshape.59.counts.refs_2_, s32[8,128]{1,0:T(8,128)S(1)} %bitcast.27, f32[3,8,128]{2,1,0:T(8,128)S(1)} %get-tuple-element.38.refs_5_.refs_4_, ...), custom_call_target="tpu_custom_call" | custom-call | flops 33554432 | bytes 1048576 | tf_op jit(solution)/shard_map/pallas_call | solution.py:561
  56.0 0.7 %copy.20 = f32[1,1,1,22,6,128]{5,2,4,3,1,0:T(1,128)} copy(f32[1,1,1,22,6,128]{5,4,3,2,1,0:T(8,128)S(1)} %bitcast.22) | data formatting | bytes 135168
  (45 shorter events, 3.9 us)
Async XLA Ops:
  0.6 34.2 %copy-start.5 = (f32[2,2,2,128]{3,2,1,0:T(2,128)S(1)}, f32[2,2,2,128]{3,2,1,0:T(2,128)}, u32[]{:S(2)}) copy-start(f32[2,2,2,128]{3,2,1,0:T(2,128)} %param.15) | copy-start | bytes 12292
  0.6 34.1 %copy-start.13 = (s32[1,1,1,6,128]{4,2,3,1,0:T(1,128)S(1)}, s32[1,1,1,6,128]{4,2,3,1,0:T(1,128)}, u32[]{:S(2)}) copy-start(s32[1,1,1,6,128]{4,2,3,1,0:T(1,128)} %param.20) | copy-start | bytes 9220
  1.4 1.0 %copy-start = (f32[16,32,256]{2,1,0:T(8,128)S(1)}, f32[16,32,256]{2,1,0:T(8,128)}, u32[]{:S(2)}) copy-start(f32[16,32,256]{2,1,0:T(8,128)} %refs_5_.1) | copy-start | bytes 1572868
  5.3 16.3 %copy-start.6 = (s32[4,2,2,2,128]{4,3,2,1,0:T(2,128)S(1)}, s32[4,2,2,2,128]{4,3,2,1,0:T(2,128)}, u32[]{:S(2)}) copy-start(s32[4,2,2,2,128]{4,3,2,1,0:T(2,128)} %param.18) | copy-start | bytes 49156
  5.3 46.9 %copy-start.1 = (f32[16,32,256]{2,1,0:T(8,128)S(1)}, f32[16,32,256]{2,1,0:T(8,128)}, u32[]{:S(2)}) copy-start(f32[16,32,256]{2,1,0:T(8,128)} %refs_5_.1) | copy-start | bytes 1572868
  6.1 15.4 %collective-permute-start = (f32[104,128]{1,0:T(8,128)S(1)}, f32[104,128]{1,0:T(8,128)S(1)}, u32[]{:S(2)}, u32[]{:S(2)}) collective-permute-start(f32[104,128]{1,0:T(8,128)S(1)} %get-tuple-element.39), channel_id=1, source_target_pairs={{0,8},{8,16},{16,24},{24,0},{1,9},{9,17},{17,25},{25,1},{2,10},{10... | collective-permute-start | bytes 159752 | tf_op jit(solution)/shard_map/ppermute | solution.py:107
  6.7 14.9 %collective-permute-start.1 = (f32[104,128]{1,0:T(8,128)S(1)}, f32[104,128]{1,0:T(8,128)S(1)}, u32[]{:S(2)}, u32[]{:S(2)}) collective-permute-start(f32[104,128]{1,0:T(8,128)S(1)} %get-tuple-element.40), channel_id=1, source_target_pairs={{8,0},{16,8},{24,16},{0,24},{9,1},{17,9},{25,17},{1,25},{10,2},{18... | collective-permute-start | bytes 159752 | tf_op jit(solution)/shard_map/ppermute | solution.py:107
  8.6 12.9 %collective-permute-start.2 = (f32[72,128]{1,0:T(8,128)S(1)}, f32[72,128]{1,0:T(8,128)S(1)}, u32[]{:S(2)}, u32[]{:S(2)}) collective-permute-start(f32[72,128]{1,0:T(8,128)S(1)} %get-tuple-element.41), channel_id=1, source_target_pairs={{0,2},{2,0},{4,6},{6,4},{1,3},{3,1},{5,7},{7,5},{8,10},{10,8},{12,... | collective-permute-start | bytes 110600 | tf_op jit(solution)/shard_map/ppermute | solution.py:107
  11.0 10.6 %collective-permute-start.3 = (f32[72,128]{1,0:T(8,128)S(1)}, f32[72,128]{1,0:T(8,128)S(1)}, u32[]{:S(2)}, u32[]{:S(2)}) collective-permute-start(f32[72,128]{1,0:T(8,128)S(1)} %get-tuple-element.42), channel_id=1, source_target_pairs={{2,4},{4,2},{3,5},{5,3},{10,12},{12,10},{11,13},{13,11},{18,20},{2... | collective-permute-start | bytes 110600 | tf_op jit(solution)/shard_map/ppermute | solution.py:107
  11.6 9.9 %collective-permute-start.4 = (f32[72,128]{1,0:T(8,128)S(1)}, f32[72,128]{1,0:T(8,128)S(1)}, u32[]{:S(2)}, u32[]{:S(2)}) collective-permute-start(f32[72,128]{1,0:T(8,128)S(1)} %get-tuple-element.43), channel_id=1, source_target_pairs={{0,1},{1,0},{2,3},{3,2},{4,5},{5,4},{6,7},{7,6},{8,9},{9,8},{10,11... | collective-permute-start | bytes 110600 | tf_op jit(solution)/shard_map/ppermute | solution.py:107
  13.2 1.4 %copy-start.2 = (f32[3,16,32,256]{3,2,1,0:T(8,128)S(1)}, f32[3,16,32,256]{3,2,1,0:T(8,128)}, u32[]{:S(2)}) copy-start(f32[3,16,32,256]{3,2,1,0:T(8,128)} %refs_3_.1) | copy-start | bytes 4718596
  15.3 6.3 %copy-start.7 = (f32[3,4,2,2,2,128]{5,4,3,2,1,0:T(2,128)S(1)}, f32[3,4,2,2,2,128]{5,4,3,2,1,0:T(2,128)}, u32[]{:S(2)}) copy-start(f32[3,4,2,2,2,128]{5,4,3,2,1,0:T(2,128)} %param.17) | copy-start | bytes 147460
  15.3 36.9 %copy-start.3 = (f32[16,32,256]{2,1,0:T(8,128)S(1)}, f32[16,32,256]{2,1,0:T(8,128)}, u32[]{:S(2)}) copy-start(f32[16,32,256]{2,1,0:T(8,128)} %refs_6_.1) | copy-start | bytes 1572868
  27.4 13.2 %collective-permute-start.5 = (f32[40,128]{1,0:T(8,128)S(1)}, f32[40,128]{1,0:T(8,128)S(1)}, u32[]{:S(2)}, u32[]{:S(2)}) collective-permute-start(f32[40,128]{1,0:T(8,128)S(1)} %get-tuple-element.46), channel_id=1, source_target_pairs={{0,8},{8,16},{16,24},{24,0},{1,9},{9,17},{17,25},{25,1},{2,10},{10... | collective-permute-start | bytes 61448 | tf_op jit(solution)/shard_map/ppermute | solution.py:107
  27.4 13.2 %collective-permute-start.6 = (f32[40,128]{1,0:T(8,128)S(1)}, f32[40,128]{1,0:T(8,128)S(1)}, u32[]{:S(2)}, u32[]{:S(2)}) collective-permute-start(f32[40,128]{1,0:T(8,128)S(1)} %get-tuple-element.47), channel_id=1, source_target_pairs={{8,0},{16,8},{24,16},{0,24},{9,1},{17,9},{25,17},{1,25},{10,2},{18... | collective-permute-start | bytes 61448 | tf_op jit(solution)/shard_map/ppermute | solution.py:107
  29.2 11.4 %collective-permute-start.7 = (f32[40,128]{1,0:T(8,128)S(1)}, f32[40,128]{1,0:T(8,128)S(1)}, u32[]{:S(2)}, u32[]{:S(2)}) collective-permute-start(f32[40,128]{1,0:T(8,128)S(1)} %get-tuple-element.48), channel_id=1, source_target_pairs={{0,2},{2,0},{4,6},{6,4},{1,3},{3,1},{5,7},{7,5},{8,10},{10,8},{12,... | collective-permute-start | bytes 61448 | tf_op jit(solution)/shard_map/ppermute | solution.py:107
  33.6 7.0 %collective-permute-start.8 = (f32[40,128]{1,0:T(8,128)S(1)}, f32[40,128]{1,0:T(8,128)S(1)}, u32[]{:S(2)}, u32[]{:S(2)}) collective-permute-start(f32[40,128]{1,0:T(8,128)S(1)} %get-tuple-element.49), channel_id=1, source_target_pairs={{2,4},{4,2},{3,5},{5,3},{10,12},{12,10},{11,13},{13,11},{18,20},{2... | collective-permute-start | bytes 61448 | tf_op jit(solution)/shard_map/ppermute | solution.py:107
  34.2 6.4 %collective-permute-start.9 = (f32[40,128]{1,0:T(8,128)S(1)}, f32[40,128]{1,0:T(8,128)S(1)}, u32[]{:S(2)}, u32[]{:S(2)}) collective-permute-start(f32[40,128]{1,0:T(8,128)S(1)} %get-tuple-element.50), channel_id=1, source_target_pairs={{0,1},{1,0},{2,3},{3,2},{4,5},{5,4},{6,7},{7,6},{8,9},{9,8},{10,11... | collective-permute-start | bytes 61448 | tf_op jit(solution)/shard_map/ppermute | solution.py:107
  46.9 8.9 %collective-permute-start.10 = (f32[32,128]{1,0:T(8,128)S(1)}, f32[32,128]{1,0:T(8,128)S(1)}, u32[]{:S(2)}, u32[]{:S(2)}) collective-permute-start(f32[32,128]{1,0:T(8,128)S(1)} %get-tuple-element.57), channel_id=1, source_target_pairs={{0,8},{8,16},{16,24},{24,0},{1,9},{9,17},{17,25},{25,1},{2,10},{10... | collective-permute-start | bytes 49160 | tf_op jit(solution)/shard_map/ppermute | solution.py:107
  46.9 8.9 %collective-permute-start.11 = (f32[32,128]{1,0:T(8,128)S(1)}, f32[32,128]{1,0:T(8,128)S(1)}, u32[]{:S(2)}, u32[]{:S(2)}) collective-permute-start(f32[32,128]{1,0:T(8,128)S(1)} %get-tuple-element.58), channel_id=1, source_target_pairs={{8,0},{16,8},{24,16},{0,24},{9,1},{17,9},{25,17},{1,25},{10,2},{18... | collective-permute-start | bytes 49160 | tf_op jit(solution)/shard_map/ppermute | solution.py:107
  48.7 7.2 %collective-permute-start.12 = (f32[32,128]{1,0:T(8,128)S(1)}, f32[32,128]{1,0:T(8,128)S(1)}, u32[]{:S(2)}, u32[]{:S(2)}) collective-permute-start(f32[32,128]{1,0:T(8,128)S(1)} %get-tuple-element.59), channel_id=1, source_target_pairs={{0,2},{2,0},{4,6},{6,4},{1,3},{3,1},{5,7},{7,5},{8,10},{10,8},{12,... | collective-permute-start | bytes 49160 | tf_op jit(solution)/shard_map/ppermute | solution.py:107
  49.9 5.9 %collective-permute-start.13 = (f32[32,128]{1,0:T(8,128)S(1)}, f32[32,128]{1,0:T(8,128)S(1)}, u32[]{:S(2)}, u32[]{:S(2)}) collective-permute-start(f32[32,128]{1,0:T(8,128)S(1)} %get-tuple-element.60), channel_id=1, source_target_pairs={{2,4},{4,2},{3,5},{5,3},{10,12},{12,10},{11,13},{13,11},{18,20},{2... | collective-permute-start | bytes 49160 | tf_op jit(solution)/shard_map/ppermute | solution.py:107
  50.6 5.3 %collective-permute-start.14 = (f32[32,128]{1,0:T(8,128)S(1)}, f32[32,128]{1,0:T(8,128)S(1)}, u32[]{:S(2)}, u32[]{:S(2)}) collective-permute-start(f32[32,128]{1,0:T(8,128)S(1)} %get-tuple-element.61), channel_id=1, source_target_pairs={{0,1},{1,0},{2,3},{3,2},{4,5},{5,4},{6,7},{7,6},{8,9},{9,8},{10,11... | collective-permute-start | bytes 49160 | tf_op jit(solution)/shard_map/ppermute | solution.py:107
  52.2 0.7 %copy-start.9 = (f32[3,8,128]{2,1,0:T(8,128)S(1)}, f32[3,8,128]{2,1,0:T(8,128)}, u32[]{:S(2)}) copy-start(f32[3,8,128]{2,1,0:T(8,128)} %get-tuple-element.52.refs_0_) | copy-start | bytes 36868
  (5 other events, 3.5 us)
where the time goes:
time: 58.1 us; the launch traced here: 57.3 us
  Pallas kernels  27.9 us (48%)
  starting transfers between devices  19.7 us (34%)
  local copies, waits for them, and re-layouts  8.75 us (15%)
  between operations  0.84 us (1%)
    pallas_call x7, Pallas kernels, call(): pl.pallas_call(kernel, out_shape=[jax.ShapeDtypeStruct(s, d) for s, d in...  27.9 us
    ppermute x15, starting transfers between devices, exchange(): out.append(lax.ppermute(blocks[k], axis, pairs))  19.7 us
    unnamed x31, local copies, waits for them, and re-layouts  7.98 us
  transfers between devices with their start and end apart: 15, of which 0 were waited for; matrix products, arithmetic and copies ran while one was open for 0% of the time, Pallas kernels for 26%

commit v1 on v0

--- a/solution.py
+++ b/solution.py
@@ -25,7 +25,6 @@
 FIELDS = 10
 DEAD = -8.0
 TINY = 1e-30
-GROUP = 4
 f32 = jnp.float32
 
 
@@ -56,18 +55,33 @@
         return False, across[0] * width + across[1]
 
 
-def rolls(axis, size):
-    if axis == "gx" and size > 2:
+def rolls(axis, sizes):
+    size = sizes[AXES.index(axis)]
+    if is_ring(axis, size):
         return [
-            [(i, (i + 1) % size) for i in range(size)],
-            [((i + 1) % size, i) for i in range(size)],
+            (axis, [(i, (i + 1) % size) for i in range(size)]),
+            (axis, [((i + 1) % size, i) for i in range(size)]),
         ]
-    out = []
-    for start in range(2 if size > 2 else 1):
+
+    def swaps(start):
         pairs = []
         for i in range(start, size - 1, 2):
             pairs += [(i, i + 1), (i + 1, i)]
-        out.append(pairs)
+        return pairs
+
+    out = [(axis, swaps(0))]
+    if size > 2:
+        pairs = swaps(1)
+        inside = [i for i, _ in pairs]
+        across = sizes[0]
+        if axis != "gx" and across % 2 == 0:
+            joint = []
+            for x in range(across):
+                joint += [(x * size + i, x * size + j) for i, j in pairs]
+                joint += [(x * size + i, (x ^ 1) * size + i) for i in range(size) if i not in inside]
+            out.append((("gx", axis), joint))
+        else:
+            out.append((axis, pairs))
     return out
 
 
@@ -100,27 +114,22 @@
 
 
 def exchange(blocks, sizes):
-    out = []
-    k = 0
-    for axis, size in zip(AXES, sizes):
-        for pairs in rolls(axis, size):
-            out.append(lax.ppermute(blocks[k], axis, pairs))
-            k += 1
-    return out
+    routes = [route for axis in AXES for route in rolls(axis, sizes)]
+    return [lax.ppermute(block, axes, pairs) for block, (axes, pairs) in zip(blocks, routes)]
 
 
 def per_axis(refs, sizes):
     out = []
     k = 0
-    for axis, size in zip(AXES, sizes):
-        n = len(rolls(axis, size))
+    for axis in AXES:
+        n = len(rolls(axis, sizes))
         out.append(refs[k : k + n])
         k += n
     return out
 
 
 def send_count(sizes):
-    return sum(len(rolls(a, s)) for a, s in zip(AXES, sizes))
+    return sum(len(rolls(a, sizes)) for a in AXES)
 
 
 def put_faces(plan, sizes, state_ref, send_refs):
@@ -135,17 +144,31 @@
                 ref[pl.ds(k, FIELDS, stride=width), :] = block
 
 
-def pack_kernel(plan, sizes, pos, vel, spin, rad, counts, pressure, *outs):
-    state = outs[0]
-    sends = outs[1:]
-    state[0:3] = pos[...]
-    state[3:6] = vel[...]
-    state[6:9] = spin[...]
+def pack_kernel(plan, sizes, pos, vel, spin, rad, counts_hbm, pressure_hbm, *refs):
+    state, radius = refs[:2]
+    sends = refs[2:-3]
+    counts, pressure, sems = refs[-3:]
+    copies = [
+        pltpu.make_async_copy(rad, radius, sems.at[0]),
+        pltpu.make_async_copy(pos, state.at[0:3], sems.at[1]),
+        pltpu.make_async_copy(vel, state.at[3:6], sems.at[2]),
+        pltpu.make_async_copy(spin, state.at[6:9], sems.at[3]),
+        pltpu.make_async_copy(counts_hbm, counts, sems.at[4]),
+        pltpu.make_async_copy(pressure_hbm, pressure, sems.at[5]),
+    ]
+    for copy in copies:
+        copy.start()
     slots = rad.shape[-1]
     lane = lax.broadcasted_iota(jnp.int32, (1, slots), 1)
+    places = plan.places()
+    for copy in copies[:5]:
+        copy.wait()
     for b in range(plan.count):
-        state[9, b : b + 1, :] = jnp.where(lane < counts[b], rad[b : b + 1, :], DEAD)
+        x, y, z = places[b]
+        live = lane < counts[x, y : y + 1, z : z + 1]
+        state[9, b : b + 1, :] = jnp.where(live, radius[b : b + 1, :], DEAD)
     put_faces(plan, sizes, state, sends)
+    copies[5].wait()
     nx, ny, nz = pressure.shape
     lanes = slots
     chunks = nz // lanes
@@ -175,87 +198,117 @@
         ref[base : base + ny, :] = block
 
 
-def spread_own(b, state, radius, spread, columns):
-    for f in range(3):
-        columns[f : f + 1, :] = state[f, b : b + 1, :]
-        columns[3 + f : 4 + f, :] = state[3 + f, b : b + 1, :] * (normal_damp / normal_stiff)
-    columns[6:7, :] = radius[b : b + 1, :]
-    columns[7:8, :] = radius[b : b + 1, :]
-    slots = columns.shape[-1]
-    turned = jnp.transpose(columns[...], (1, 0))
-    for f in range(7):
-        spread[f] = jnp.broadcast_to(turned[:, f : f + 1], (slots, slots))
-
-
-def pair_forces(b, chosen, others, spread, parts, total, first):
-    slots = spread.shape[-1]
-    trips = slots // (8 * GROUP)
-
-    def trip(g, carry):
-        for t in range(GROUP):
-            rows = pl.ds(pl.multiple_of((g * GROUP + t) * 8, 8), 8)
-            mine = [spread[f, rows, :] for f in range(7)]
-            sums = None
-            for n in chosen:
-                their = [jnp.broadcast_to(others[n, f, b : b + 1, :], (8, slots)) for f in range(7)]
-                sep = [mine[k] - their[k] for k in range(3)]
-                square = sep[0] * sep[0] + (sep[1] * sep[1] + (sep[2] * sep[2] + soft_length**2))
-                inverse = lax.rsqrt(square)
-                over = (mine[6] + their[6]) - square * inverse
-                positive = jnp.maximum(over, 0.0)
-                root = positive * lax.rsqrt(jnp.maximum(over, TINY))
-                dot = (mine[3] - their[3]) * sep[0]
-                dot = dot + (mine[4] - their[4]) * sep[1]
-                dot = dot + (mine[5] - their[5]) * sep[2]
-                weight = (positive - dot * inverse) * (root * inverse)
-                new = [weight * sep[k] for k in range(3)]
-                sums = new if sums is None else [s + w for s, w in zip(sums, new)]
+def pair_rows(state, radius, mine):
+    scale = normal_damp / normal_stiff
+    for k in range(3):
+        mine[:, k, :] = state[k]
+        mine[:, 3 + k, :] = state[3 + k] * scale
+    mine[:, 6, :] = radius[...]
+    mine[:, 7, :] = radius[...]
+
+
+def spread_rows(mine, spread):
+    slots = mine.shape[-1]
+    turned = [jnp.transpose(mine[b], (1, 0)) for b in range(mine.shape[0])]
+    for b in range(mine.shape[0]):
+        for f in range(7):
+            spread[b, f] = jnp.broadcast_to(turned[b][:, f : f + 1], (slots, slots))
+
+
+def list_pairs(plan, entries, packed, table):
+    slots = packed.shape[-1]
+    lane = lax.broadcasted_iota(jnp.int32, (8, slots), 1)
+    field = lax.broadcasted_iota(jnp.int32, (8, slots), 0)
+    empty = jnp.where(field == 6, DEAD, 0.0)
+    jobs = jnp.int32(0)
+    for b in range(plan.count):
+        start = jobs
+        at = None
+        for rows, count, move in entries[b]:
+            value = rows
             for k in range(3):
-                parts[k, rows, :] = sums[k]
+                if move[k]:
+                    value = value + jnp.where(field == k, float(move[k]), 0.0)
+            if at is None:
+                packed[start] = jnp.where(lane < count, value, empty)
+                packed[start + 1] = empty
+                at = count
+                continue
+            shift = at % slots
+            job = start + at // slots
+            moved = pltpu.roll(value, shift, 1)
+            packed[job] = jnp.where(
+                (lane >= shift) & (lane < shift + count), moved, packed[job]
+            )
+            packed[job + 1] = jnp.where(lane < shift + count - slots, moved, empty)
+            at = at + count
+        jobs = start + (at + slots - 1) // slots
+        for q in range(len(entries[b])):
+            table[start + q] = b
+    return jobs
+
+
+def run_pairs(jobs, spread, packed, table, parts):
+    slots = packed.shape[-1]
+
+    def job(t, carry):
+        b = table[t]
+        their = [jnp.broadcast_to(packed[t, f : f + 1, :], (8, slots)) for f in range(7)]
+        for tile in range(slots // 8):
+            rows = slice(tile * 8, tile * 8 + 8)
+            own = [spread[b, f, rows, :] for f in range(7)]
+            sep = [own[k] - their[k] for k in range(3)]
+            square = sep[0] * sep[0] + (sep[1] * sep[1] + (sep[2] * sep[2] + soft_length**2))
+            inverse = lax.rsqrt(square)
+            over = (own[6] + their[6]) - square * inverse
+            positive = jnp.maximum(over, 0.0)
+            root = positive * lax.rsqrt(jnp.maximum(over, TINY))
+            dot = (own[3] - their[3]) * sep[0]
+            dot = dot + (own[4] - their[4]) * sep[1]
+            dot = dot + (own[5] - their[5]) * sep[2]
+            weight = (positive - dot * inverse) * (root * inverse)
+            for k in range(3):
+                parts[b, k, rows, :] = parts[b, k, rows, :] + weight * sep[k]
         return carry
 
-    lax.fori_loop(0, trips, trip, 0)
-    for k in range(3):
-        row = jnp.sum(jnp.transpose(parts[k], (1, 0)), axis=0, keepdims=True) * normal_stiff
-        total[k, b : b + 1, :] = row if first else total[k, b : b + 1, :] + row
-
-
-def scale_rows(n, place, rows):
-    move = neighbours[n]
-    return rows
-
-
-def own_pairs(plan, state, radius, total, others, spread, columns, parts):
-    scale = normal_damp / normal_stiff
-    places = plan.places()
-    for n in range(7):
-        for place in places:
-            own, other = plan.neighbour(place, n)
-            b = plan.index(place)
-            if not own:
-                continue
-            for f in range(3):
-                row = state[f, other : other + 1, :]
-                if neighbours[n][f]:
-                    row = row + float(neighbours[n][f])
-                others[n, f, b : b + 1, :] = row
-                others[n, 3 + f, b : b + 1, :] = state[3 + f, other : other + 1, :] * scale
-            others[n, 6, b : b + 1, :] = state[9, other : other + 1, :]
-    for place in places:
-        b = plan.index(place)
-        spread_own(b, state, radius, spread, columns)
-        chosen = [n for n in range(7) if plan.neighbour(place, n)[0]]
-        pair_forces(b, chosen, others, spread, parts, total, True)
+    lax.fori_loop(0, jobs, job, 0)
 
 
 def inner_kernel(plan, with_fluid, *refs):
     if with_fluid:
-        state, radius, cells, fluid, total, gas, others, spread, columns, parts = refs
+        (state, radius, cells_hbm, fluid_hbm, spread, parts, gas, cells, mine, packed,
+         table, fluid, sems) = refs
+        fetches = [
+            pltpu.make_async_copy(cells_hbm, cells, sems.at[0]),
+            pltpu.make_async_copy(fluid_hbm, fluid, sems.at[1]),
+        ]
+        for fetch in fetches:
+            fetch.start()
     else:
-        state, radius, total, others, spread, columns, parts = refs
-    own_pairs(plan, state, radius, total, others, spread, columns, parts)
+        state, radius, spread, parts, mine, packed, table = refs
+    parts[...] = jnp.zeros_like(parts)
+    pair_rows(state, radius, mine)
+    spread_rows(mine, spread)
+    records = []
+    for b in range(plan.count):
+        rows = mine[b]
+        field = lax.broadcasted_iota(jnp.int32, rows.shape, 0)
+        records.append(jnp.where(field == 6, state[9, b : b + 1, :], rows))
+    filled = jnp.sum(jnp.where(state[9] > 0.0, 1, 0), axis=1, keepdims=True)
+    entries = []
+    for place in plan.places():
+        entry = []
+        for n in range(7):
+            own, other = plan.neighbour(place, n)
+            if own:
+                entry.append((records[other], filled[other, 0], neighbours[n]))
+        entries.append(entry)
+    jobs = list_pairs(plan, entries, packed, table)
+    run_pairs(jobs, spread, packed, table, parts)
     if not with_fluid:
         return
+    for fetch in fetches:
+        fetch.wait()
     slots = radius.shape[-1]
     span = [s // d for s, d in zip(fluid.shape[1:], plan.dims)]
     sub = lax.broadcasted_iota(jnp.int32, (8, slots), 0)
@@ -264,7 +317,7 @@
         cell = cells[b : b + 1, :]
         column = jnp.broadcast_to(cell % span[2], (8, slots))
         row = jnp.broadcast_to(cell // span[2], (8, slots)) - sub
-        sums = [jnp.zeros((8, slots), f32) for c in range(3)]
+        sums_c = [jnp.zeros((8, slots), f32) for c in range(3)]
         for a in range(span[0]):
             for h in range(span[1] // 8):
                 hit = row == a * span[1] + h * 8
@@ -273,13 +326,13 @@
                 for c in range(3):
                     block = fluid[c, place[0] * span[0] + a, y0 : y0 + 8, z0 : z0 + span[2]]
                     got = jnp.take_along_axis(block, column, axis=1)
-                    sums[c] = jnp.where(hit, got, sums[c])
+                    sums_c[c] = jnp.where(hit, got, sums_c[c])
         for c in range(3):
-            gas[c, b : b + 1, :] = jnp.sum(sums[c], axis=0, keepdims=True)
-
-
-def step_core(plan, sizes, state, radius, inner, springs, partners, gas, halos, out, new_springs,
-              around, others, spread, columns, parts, outer):
+            gas[c, b : b + 1, :] = jnp.sum(sums_c[c], axis=0, keepdims=True)
+
+
+def step_core(plan, sizes, state, radius, spread, inner, springs, partners, gas, halos, out,
+              new_springs, around, packed, table, parts):
     scale = normal_damp / normal_stiff
     places = plan.places()
     slots = radius.shape[-1]
@@ -300,23 +353,36 @@
                 around[n, :, b, :] = after if side else before
     sub = lax.broadcasted_iota(jnp.int32, (plan.count, slots), 0)
     inner_count = [plan.dims[1] * plan.dims[2], plan.dims[2], 1]
+    entries = [[] for _ in places]
+    parts[...] = inner[...]
     for n in range(1, 7):
         axis = (n - 1) // 2
         side = 1 if n % 2 == 0 else -1
         edge = plan.dims[axis] - 1 if side > 0 else 0
         level = sub // inner_count[axis] % plan.dims[axis]
-        outside = (level == edge) & at_end(AXES[axis], sizes[axis], side)
+        gone = at_end(AXES[axis], sizes[axis], side)
         reach = around[n, 9]
-        around[n, 9] = jnp.where(outside | (reach <= 0.0), DEAD, reach)
-        for f in range(3):
-            others[n, f] = around[n, f] + float(neighbours[n][f])
-            others[n, 3 + f] = around[n, 3 + f] * scale
-        others[n, 6] = around[n, 9]
-    for place in places:
-        b = plan.index(place)
-        chosen = [n for n in range(7) if not plan.neighbour(place, n)[0]]
-        spread_own(b, state, radius, spread, columns)
-        pair_forces(b, chosen, others, spread, parts, outer, True)
+        reach = jnp.where(((level == edge) & gone) | (reach <= 0.0), DEAD, reach)
+        around[n, 9] = reach
+        filled = jnp.sum(jnp.where(reach > 0.0, 1, 0), axis=1, keepdims=True)
+        for place in places:
+            b = plan.index(place)
+            if plan.neighbour(place, n)[0]:
+                continue
+            rows = around[n, 0:8, b, :]
+            field = lax.broadcasted_iota(jnp.int32, rows.shape, 0)
+            rows = jnp.where((field > 2) & (field < 6), rows * scale, rows)
+            rows = jnp.where(field == 6, reach[b : b + 1, :], rows)
+            entries[b].append((rows, filled[b, 0], neighbours[n]))
+    jobs = list_pairs(plan, entries, packed, table)
+    run_pairs(jobs, spread, packed, table, parts)
+    normal = []
+    for k in range(3):
+        sums = [
+            jnp.sum(jnp.transpose(parts[b, k], (1, 0)), axis=0, keepdims=True)
+            for b in range(plan.count)
+        ]
+        normal.append(jnp.concatenate(sums, axis=0) * normal_stiff)
     place_i = [state[k] for k in range(3)]
     speed_i = [state[3 + k] for k in range(3)]
     turn_i = [state[6 + k] for k in range(3)]
@@ -383,7 +449,7 @@
     mass = ratio * ratio * ratio
     inertia = 0.4 * mass * safe * safe
     for k in range(3):
-        force = inner[k] + outer[k] + shear_sum[k] + drag_coeff * (gas[k] - speed_i[k])
+        force = normal[k] + shear_sum[k] + drag_coeff * (gas[k] - speed_i[k])
         lift = gravity if k == 2 else 0.0
         speed = speed_i[k] + time_step * (force / mass - lift)
         out[k] = place_i[k] + time_step * speed
@@ -394,26 +460,25 @@
 
 def middle_kernel(plan, sizes, *refs):
     n = send_count(sizes)
-    state, radius, inner, springs, partners, gas = refs[:6]
-    halos = refs[6 : 6 + n]
-    out, new_springs = refs[6 + n : 8 + n]
-    sends = refs[8 + n : 8 + 2 * n]
-    scratch = refs[8 + 2 * n :]
-    step_core(plan, sizes, state, radius, inner, springs, partners, gas, halos, out, new_springs,
-              *scratch)
+    state, radius, spread, inner, springs, partners, gas = refs[:7]
+    halos = refs[7 : 7 + n]
+    out, new_springs = refs[7 + n : 9 + n]
+    sends = refs[9 + n : 9 + 2 * n]
+    scratch = refs[9 + 2 * n :]
+    step_core(plan, sizes, state, radius, spread, inner, springs, partners, gas, halos, out,
+              new_springs, *scratch)
     put_faces(plan, sizes, out, sends)
 
 
 def last_kernel(plan, sizes, *refs):
     n = send_count(sizes)
-    state, radius, inner, springs, partners, gas, departures = refs[:7]
-    halos = refs[7 : 7 + n]
-    places, speeds, turns, new_springs = refs[7 + n : 11 + n]
-    sends = refs[11 + n : 11 + 2 * n]
-    out = refs[11 + 2 * n]
-    scratch = refs[12 + 2 * n :]
-    step_core(plan, sizes, state, radius, inner, springs, partners, gas, halos, out, new_springs,
-              *scratch)
+    state, radius, spread, inner, springs, partners, gas, departures = refs[:8]
+    halos = refs[8 : 8 + n]
+    places, speeds, turns, new_springs, out = refs[8 + n : 13 + n]
+    sends = refs[13 + n : 13 + 2 * n]
+    scratch = refs[13 + 2 * n :]
+    step_core(plan, sizes, state, radius, spread, inner, springs, partners, gas, halos, out,
+              new_springs, *scratch)
     places[...] = out[0:3]
     speeds[...] = out[3:6]
     turns[...] = out[6:9]
@@ -445,25 +510,30 @@
 
 def deposit_kernel(plan, sizes, *refs):
     n = send_count(sizes)
-    state, radius, counts, cells, gas, pressure, source = refs[:7]
-    halos = refs[7 : 7 + n]
-    force, new_pressure = refs[7 + n :]
+    state, radius, cells, gas, pressure, source = refs[:6]
+    halos = refs[6 : 6 + n]
+    force_out, pressure_out, force, new_pressure, sems = refs[6 + n :]
+    copies = []
+
+    def send(source, target):
+        copies.append(pltpu.make_async_copy(source, target, sems.at[len(copies)]))
+        copies[-1].start()
+
     slots = radius.shape[-1]
     nx, ny, nz = pressure.shape
     lanes = slots
     chunks = nz // lanes
     span = [s // d for s, d in zip(pressure.shape, plan.dims)]
     rows = span[0] * span[1]
-    lane = lax.broadcasted_iota(jnp.int32, (1, slots), 1)
     high_row = lax.broadcasted_iota(jnp.int32, (rows, slots), 0)
     column_row = lax.broadcasted_iota(jnp.int32, (span[2], slots), 0)
     for place in plan.places():
         b = plan.index(place)
         cell = cells[b : b + 1, :]
-        live = lane < counts[b]
+        live = state[9, b : b + 1, :] > 0.0
         rad = radius[b : b + 1, :]
         values = [
-            jnp.where(live, drag_coeff * (state[c, b : b + 1, :] - gas[c, b : b + 1, :]), 0.0)
+            jnp.where(live, drag_coeff * (state[3 + c, b : b + 1, :] - gas[c, b : b + 1, :]), 0.0)
             for c in range(3)
         ]
         values.append(jnp.where(live, 4.0 / 3.0 * math.pi * rad * rad * rad, 0.0))
@@ -473,16 +543,14 @@
         for v in values:
             top = v.astype(jnp.bfloat16).astype(f32)
             left = v - top
-            mid = left.astype(jnp.bfloat16).astype(f32)
-            low = left - mid
             halves.append(
                 jnp.concatenate(
-                    [jnp.where(at_row, part, 0.0).astype(jnp.bfloat16) for part in (top, mid, low)],
+                    [jnp.where(at_row, part, 0.0).astype(jnp.bfloat16) for part in (top, left)],
                     axis=1,
                 )
             )
         left = jnp.concatenate(halves, axis=0)
-        right = jnp.concatenate([at_column] * 3, axis=1)
+        right = jnp.concatenate([at_column] * 2, axis=1)
         got = lax.dot_general(
             left, right, (((1,), (1,)), ((), ())), preferred_element_type=f32
         )
@@ -491,6 +559,7 @@
         pieces = [got[c * rows : (c + 1) * rows].reshape(span) for c in range(4)]
         for c in range(3):
             force[(c,) + block] = pieces[c]
+            send(force.at[(c,) + block], force_out.at[(c,) + block])
         new_pressure[block] = volume_coeff * pieces[3] + pieces[2]
     split = per_axis(halos, sizes)
     dead = [
@@ -534,6 +603,11 @@
             column == nz - 1, z_ends[1][:, x : x + 1], pltpu.roll(here, nz - 1, 1)
         )
         new_pressure[x] = (total + (source[x] + new_pressure[x])) * (1.0 / 6.0)
+        if (x + 1) % span[0] == 0:
+            part = slice(x + 1 - span[0], x + 1)
+            send(new_pressure.at[part], pressure_out.at[part])
+    for copy in copies:
+        copy.wait()
 
 
 def arrive_kernel(sizes, *refs):
@@ -542,27 +616,31 @@
     state, codes = refs[n:]
     split = per_axis(halos, sizes)
     width = state.shape[0]
-    hist = codes.shape[0]
+    hist = codes.shape[1]
     for axis in range(3):
         got = [ref[0 : width + hist, :] for ref in split[axis]]
         before, after = ordered_receive(AXES[axis], sizes[axis], got)
         after = jnp.where(at_end(AXES[axis], sizes[axis], 1), 0.0, after)
         before = jnp.where(at_end(AXES[axis], sizes[axis], -1), 0.0, before)
         for d, block in ((2 * axis, after), (2 * axis + 1, before)):
-            state[:, d, :] = block[0:width]
-            codes[:, d, :] = block[width : width + hist].astype(jnp.int32) - 1
-
-
-def call(kernel, outs, scratch, args, smem=(), flops=0):
-    specs = [
-        pl.BlockSpec(memory_space=pltpu.SMEM) if k in smem else pl.BlockSpec(memory_space=pltpu.VMEM)
-        for k in range(len(args))
+            state[:, d, 0, :] = block[0:width]
+            codes[d] = block[width : width + hist].astype(jnp.int32) - 1
+
+
+def call(kernel, outs, scratch, args, hbm=(), flops=0, outs_hbm=False):
+    specs = []
+    args = [
+        pltpu.with_memory_space_constraint(a, pltpu.HBM) if k in hbm else a
+        for k, a in enumerate(args)
     ]
+    for k in range(len(args)):
+        space = pltpu.HBM if k in hbm else pltpu.VMEM
+        specs.append(pl.BlockSpec(memory_space=space))
     return pl.pallas_call(
         kernel,
         out_shape=[jax.ShapeDtypeStruct(s, d) for s, d in outs],
         in_specs=specs,
-        out_specs=[pl.BlockSpec(memory_space=pltpu.VMEM)] * len(outs),
+        out_specs=[pl.BlockSpec(memory_space=pltpu.HBM if outs_hbm else pltpu.VMEM)] * len(outs),
         scratch_shapes=scratch,
         compiler_params=pltpu.CompilerParams(vmem_limit_bytes=32 * 1024 * 1024),
         cost_estimate=pl.CostEstimate(flops=flops, bytes_accessed=1 << 20, transcendentals=0),
@@ -583,7 +661,6 @@
     springs = springs.reshape(3, hist, count, slots)
     partners = partners.reshape(hist, count, slots)
     cells = cells.reshape(count, slots)
-    counts = counts.reshape(count)
     leaving = departures.reshape(6, slots)
 
     faces = [FIELDS * len(plan.face(a, 1)) for a in range(3)]
@@ -593,65 +670,83 @@
     def sends(rows):
         out = []
         for a in range(3):
-            for _ in rolls(AXES[a], sizes[a]):
+            for _ in rolls(AXES[a], sizes):
                 out.append(((rows[a], slots), f32))
         return out
 
-    pair_scratch = [vm(7, 7, count, slots), vm(7, slots, slots), vm(8, slots), vm(3, slots, slots)]
-    step_scratch = [vm(7, FIELDS, count, slots)] + pair_scratch + [vm(3, count, slots)]
+    inside = [sum(plan.neighbour(p, n)[0] for n in range(7)) for p in plan.places()]
+
+    def pair_scratch(jobs):
+        return [vm(jobs + 2, 8, slots), pltpu.SMEM((jobs + 8,), jnp.int32)]
+
+    own_scratch = [vm(count, 8, slots)] + pair_scratch(sum(inside))
+    spread_shape = ((count, 7, slots, slots), f32)
+    parts_shape = ((count, 3, slots, slots), f32)
+    step_scratch = [vm(7, FIELDS, count, slots)] + pair_scratch(7 * count - sum(inside))
+    step_scratch.append(vm(count, 3, slots, slots))
     state_shape = ((FIELDS, count, slots), f32)
     three = ((3, count, slots), f32)
     spring_shape = ((3, hist, count, slots), f32)
     bind = functools.partial
 
-    state, *out = call(
+    state, radius, *out = call(
         bind(pack_kernel, plan, sizes),
-        [state_shape] + sends([f + e for f, e in zip(faces, extra)]),
-        [],
+        [state_shape, ((count, slots), f32)] + sends([f + e for f, e in zip(faces, extra)]),
+        [
+            pltpu.VMEM(counts.shape, jnp.int32),
+            vm(nx, ny, nz),
+            pltpu.SemaphoreType.DMA((6,)),
+        ],
         [pos, vel, spin, radius, counts, pressure],
-        smem=(4,),
+        hbm=(0, 1, 2, 3, 4, 5),
         flops=1 << 20,
     )
     first_halos = exchange(out, sizes)
-    inner, gas = call(
+    spread, inner, gas, cells = call(
         bind(inner_kernel, plan, True),
-        [three, three],
-        pair_scratch,
+        [spread_shape, parts_shape, three, ((count, slots), jnp.int32)],
+        own_scratch + [vm(3, nx, ny, nz), pltpu.SemaphoreType.DMA((2,))],
         [state, radius, cells, fluid_velocity],
+        hbm=(2, 3),
         flops=1 << 25,
     )
     state, springs, *out = call(
         bind(middle_kernel, plan, sizes),
         [state_shape, spring_shape] + sends(faces),
         step_scratch,
-        [state, radius, inner, springs, partners, gas] + first_halos,
+        [state, radius, spread, inner, springs, partners, gas] + first_halos,
         flops=1 << 25,
     )
     halos = exchange(out, sizes)
-    (inner,) = call(
-        bind(inner_kernel, plan, False), [three], pair_scratch, [state, radius], flops=1 << 25
+    spread, inner = call(
+        bind(inner_kernel, plan, False), [spread_shape, parts_shape], own_scratch,
+        [state, radius], flops=1 << 25
     )
     width = 10 + 4 * hist
     padded = (width + 7) // 8 * 8
-    places, speeds, turns, springs, *out = call(
+    places, speeds, turns, springs, state, *out = call(
         bind(last_kernel, plan, sizes),
-        [three, three, three, spring_shape] + sends([padded] * 3),
-        [vm(FIELDS, count, slots)] + step_scratch,
-        [state, radius, inner, springs, partners, gas, leaving] + halos,
+        [three, three, three, spring_shape, state_shape] + sends([padded] * 3),
+        step_scratch,
+        [state, radius, spread, inner, springs, partners, gas, leaving] + halos,
         flops=1 << 25,
     )
     arrivals = exchange(out, sizes)
     force, new_pressure = call(
         bind(deposit_kernel, plan, sizes),
         [((3, nx, ny, nz), f32), ((nx, ny, nz), f32)],
-        [],
-        [speeds, radius, counts, cells, gas, pressure, pressure_source] + first_halos,
-        smem=(2,),
+        [
+            vm(3, nx, ny, nz),
+            vm(nx, ny, nz),
+            pltpu.SemaphoreType.DMA((3 * count + plan.dims[0],)),
+        ],
+        [state, radius, cells, gas, pressure, pressure_source] + first_halos,
+        outs_hbm=True,
         flops=1 << 25,
     )
     arrived, arrived_partners = call(
         bind(arrive_kernel, sizes),
-        [((10 + 3 * hist, 6, slots), f32), ((hist, 6, slots), jnp.int32)],
+        [((10 + 3 * hist, 6, 1, slots), f32), ((6, hist, slots), jnp.int32)],
         [],
         arrivals,
         flops=1 << 20,
@@ -664,8 +759,8 @@
         wide(springs),
         force,
         new_pressure,
-        arrived[None, None, None],
-        arrived_partners[None, None, None],
+        arrived.reshape(1, 1, 1, 10 + 3 * hist, 6, slots),
+        jnp.transpose(arrived_partners, (1, 0, 2))[None, None, None],
     )
 
 

time: 58.1 us -> 36.9 us (0.64)
  Pallas kernels: 27.9 us -> 19 us
  local copies, waits for them, and re-layouts: 8.75 us -> 0.02 us
  starting transfers between devices: 19.7 us -> 16.6 us
    pallas_call x7, Pallas kernels: 27.9 us -> 19 us  [call(): pl.pallas_call(kernel, out_shape=[jax.ShapeDtypeStruct(s, d) for s, d in...]
    unnamed x31 -> x11, local copies, waits for them, and re-layouts: 7.98 us -> 0.02 us
    ppermute x15, starting transfers between devices: 19.7 us -> 16.6 us  [exchange(): lax.ppermute(block, axes, pairs)]
    reshape x1 -> x0, local copies, waits for them, and re-layouts: 0.77 us -> none  [body(): counts = counts.reshape(count)]
  transfers between devices with their start and end apart: 15 -> 15, of which waited for: 0 -> 1; matrix products, arithmetic and copies ran while one was open for 0% -> 0% of each run, Pallas kernels for 26% -> 30%
where the time goes in v1:
time: 36.9 us; the launch traced here: 36.6 us
  Pallas kernels  19 us (51%)
  starting transfers between devices  16.6 us (45%)
  between operations  0.83 us (2%)
    pallas_call x7, Pallas kernels, call(): pl.pallas_call(kernel, out_shape=[jax.ShapeDtypeStruct(s, d) for s, d in...  19 us
    ppermute x15, starting transfers between devices, exchange(): lax.ppermute(block, axes, pairs)  16.6 us
  transfers between devices with their start and end apart: 15, of which 1 were waited for; matrix products, arithmetic and copies ran while one was open for 0% of the time, Pallas kernels for 30%

profile of v1, /device:TPU:0, one launch (start us, length us, event | category | flops | bytes accessed | tf_op | source)
XLA Modules:
  0.0 36.6 jit_solution(11250155059211383580)
XLA Ops:
  0.7 1.4 %shard_map.179 = (f32[10,8,128]{2,1,0:T(8,128)S(1)}, f32[8,128]{1,0:T(8,128)S(1)}, f32[104,128]{1,0:T(8,128)S(1)}, f32[104,128]{1,0:T(8,128)S(1)}, f32[72,128]{1...) custom-call(f32[3,8,128]{2,1,0:T(8,128)} %bitcast.24, f32[3,8,128]{2,1,0:T(8,128)} %bitcast.25, ...), custom_call_target="tpu_custom_call" | custom-call | flops 1048576 | bytes 1048576 | tf_op jit(solution)/shard_map/pallas_call | solution.py:639
  2.1 0.5 %collective-permute-start = (f32[104,128]{1,0:T(8,128)S(1)}, f32[104,128]{1,0:T(8,128)S(1)}, u32[]{:S(2)}, u32[]{:S(2)}) collective-permute-start(f32[104,128]{1,0:T(8,128)S(1)} %get-tuple-element.47), channel_id=1, source_target_pairs={{0,8},{8,16},{16,24},{24,0},{1,9},{9,17},{17,25},{25,1},{2,10},{10... | collective-permute-start | bytes 159752 | tf_op jit(solution)/shard_map/ppermute | solution.py:118
  2.7 2.0 %collective-permute-start.1 = (f32[104,128]{1,0:T(8,128)S(1)}, f32[104,128]{1,0:T(8,128)S(1)}, u32[]{:S(2)}, u32[]{:S(2)}) collective-permute-start(f32[104,128]{1,0:T(8,128)S(1)} %get-tuple-element.48), channel_id=1, source_target_pairs={{8,0},{16,8},{24,16},{0,24},{9,1},{17,9},{25,17},{1,25},{10,2},{18... | collective-permute-start | bytes 159752 | tf_op jit(solution)/shard_map/ppermute | solution.py:118
  4.6 2.3 %collective-permute-start.2 = (f32[72,128]{1,0:T(8,128)S(1)}, f32[72,128]{1,0:T(8,128)S(1)}, u32[]{:S(2)}, u32[]{:S(2)}) collective-permute-start(f32[72,128]{1,0:T(8,128)S(1)} %get-tuple-element.49), channel_id=1, source_target_pairs={{0,2},{2,0},{4,6},{6,4},{1,3},{3,1},{5,7},{7,5},{8,10},{10,8},{12,... | collective-permute-start | bytes 110600 | tf_op jit(solution)/shard_map/ppermute | solution.py:118
  7.0 0.0 collective-permute-start.3
  7.0 1.5 %collective-permute-start.4 = (f32[72,128]{1,0:T(8,128)S(1)}, f32[72,128]{1,0:T(8,128)S(1)}, u32[]{:S(2)}, u32[]{:S(2)}) collective-permute-start(f32[72,128]{1,0:T(8,128)S(1)} %get-tuple-element.51), channel_id=1, source_target_pairs={{0,1},{1,0},{2,3},{3,2},{4,5},{5,4},{6,7},{7,6},{8,9},{9,8},{10,11... | collective-permute-start | bytes 110600 | tf_op jit(solution)/shard_map/ppermute | solution.py:118
  8.5 4.0 %shard_map.180 = (f32[8,7,128,128]{3,2,1,0:T(8,128)S(1)}, f32[8,3,128,128]{3,2,1,0:T(8,128)S(1)}, f32[3,8,128]{2,1,0:T(8,128)S(1)}, s32[8,128]{1,0:T(8,128)S(1)}) custom-call(f32[10,8,128]{2,1,0:T(8,128)S(1)} %get-tuple-element.42.refs_0_, f32[8,128]{1,0:T(8,128)S(1)} %get-tuple-element.43.refs_1_, s32[8,128]{1,0:T(8,128)} %bitcast.28, ...), custom_call_target="tpu_custom_call" | custom-call | flops 33554432 | bytes 1048576 | tf_op jit(solution)/shard_map/pallas_call | solution.py:639
  12.5 0.0 collective-permute-done.2.refs_9_.refs_8_
  12.5 0.0 collective-permute-done.3.refs_10_.refs_9_
  12.6 0.0 copy-start.4
  12.6 2.5 %shard_map.181 = (f32[10,8,128]{2,1,0:T(8,128)S(1)}, f32[3,4,8,128]{3,2,1,0:T(8,128)S(1)}, f32[40,128]{1,0:T(8,128)S(1)}, f32[40,128]{1,0:T(8,128)S(1)}, f32[40,...) custom-call(f32[10,8,128]{2,1,0:T(8,128)S(1)} %get-tuple-element.42.refs_0_, ...), custom_call_target="tpu_custom_call" | custom-call | flops 33554432 | bytes 1048576 | tf_op jit(solution)/shard_map/pallas_call | solution.py:639
  15.1 0.4 %collective-permute-start.5 = (f32[40,128]{1,0:T(8,128)S(1)}, f32[40,128]{1,0:T(8,128)S(1)}, u32[]{:S(2)}, u32[]{:S(2)}) collective-permute-start(f32[40,128]{1,0:T(8,128)S(1)} %get-tuple-element.56), channel_id=1, source_target_pairs={{0,8},{8,16},{16,24},{24,0},{1,9},{9,17},{17,25},{25,1},{2,10},{10... | collective-permute-start | bytes 61448 | tf_op jit(solution)/shard_map/ppermute | solution.py:118
  15.5 1.4 %collective-permute-start.6 = (f32[40,128]{1,0:T(8,128)S(1)}, f32[40,128]{1,0:T(8,128)S(1)}, u32[]{:S(2)}, u32[]{:S(2)}) collective-permute-start(f32[40,128]{1,0:T(8,128)S(1)} %get-tuple-element.57), channel_id=1, source_target_pairs={{8,0},{16,8},{24,16},{0,24},{9,1},{17,9},{25,17},{1,25},{10,2},{18... | collective-permute-start | bytes 61448 | tf_op jit(solution)/shard_map/ppermute | solution.py:118
  16.9 3.9 %collective-permute-start.7 = (f32[40,128]{1,0:T(8,128)S(1)}, f32[40,128]{1,0:T(8,128)S(1)}, u32[]{:S(2)}, u32[]{:S(2)}) collective-permute-start(f32[40,128]{1,0:T(8,128)S(1)} %get-tuple-element.58), channel_id=1, source_target_pairs={{0,2},{2,0},{4,6},{6,4},{1,3},{3,1},{5,7},{7,5},{8,10},{10,8},{12,... | collective-permute-start | bytes 61448 | tf_op jit(solution)/shard_map/ppermute | solution.py:118
  20.8 0.1 collective-permute-start.9
  21.0 3.5 %shard_map.182 = (f32[8,7,128,128]{3,2,1,0:T(8,128)S(1)}, f32[8,3,128,128]{3,2,1,0:T(8,128)S(1)}) custom-call(f32[10,8,128]{2,1,0:T(8,128)S(1)} %get-tuple-element.52.refs_0_, f32[8,128]{1,0:T(8,128)S(1)} %get-tuple-element.43.refs_1_), custom_call_target="tpu_custom_call" | custom-call | flops 33554432 | bytes 1048576 | tf_op jit(solution)/shard_map/pallas_call | solution.py:639
  24.5 0.1 collective-permute-done.9.refs_12_
  24.6 3.2 %shard_map.183 = (f32[3,8,128]{2,1,0:T(8,128)}, f32[3,8,128]{2,1,0:T(8,128)}, f32[3,8,128]{2,1,0:T(8,128)}, f32[3,4,8,128]{3,2,1,0:T(8,128)}, f32[10,8,128]{2,1,...) custom-call(f32[10,8,128]{2,1,0:T(8,128)S(1)} %get-tuple-element.52., ...), custom_call_target="tpu_custom_call" | custom-call | flops 33554432 | bytes 1048576 | tf_op jit(solution)/shard_map/pallas_call | solution.py:639
  27.8 0.5 %collective-permute-start.10 = (f32[32,128]{1,0:T(8,128)S(1)}, f32[32,128]{1,0:T(8,128)S(1)}, u32[]{:S(2)}, u32[]{:S(2)}) collective-permute-start(f32[32,128]{1,0:T(8,128)S(1)} %get-tuple-element.69), channel_id=1, source_target_pairs={{0,8},{8,16},{16,24},{24,0},{1,9},{9,17},{17,25},{25,1},{2,10},{10... | collective-permute-start | bytes 49160 | tf_op jit(solution)/shard_map/ppermute | solution.py:118
  28.3 1.6 %collective-permute-start.11 = (f32[32,128]{1,0:T(8,128)S(1)}, f32[32,128]{1,0:T(8,128)S(1)}, u32[]{:S(2)}, u32[]{:S(2)}) collective-permute-start(f32[32,128]{1,0:T(8,128)S(1)} %get-tuple-element.70), channel_id=1, source_target_pairs={{8,0},{16,8},{24,16},{0,24},{9,1},{17,9},{25,17},{1,25},{10,2},{18... | collective-permute-start | bytes 49160 | tf_op jit(solution)/shard_map/ppermute | solution.py:118
  29.9 1.1 %collective-permute-start.12 = (f32[32,128]{1,0:T(8,128)S(1)}, f32[32,128]{1,0:T(8,128)S(1)}, u32[]{:S(2)}, u32[]{:S(2)}) collective-permute-start(f32[32,128]{1,0:T(8,128)S(1)} %get-tuple-element.71), channel_id=1, source_target_pairs={{0,2},{2,0},{4,6},{6,4},{1,3},{3,1},{5,7},{7,5},{8,10},{10,8},{12,... | collective-permute-start | bytes 49160 | tf_op jit(solution)/shard_map/ppermute | solution.py:118
  30.9 1.3 %collective-permute-start.14 = (f32[32,128]{1,0:T(8,128)S(1)}, f32[32,128]{1,0:T(8,128)S(1)}, u32[]{:S(2)}, u32[]{:S(2)}) collective-permute-start(f32[32,128]{1,0:T(8,128)S(1)} %get-tuple-element.73), channel_id=1, source_target_pairs={{0,1},{1,0},{2,3},{3,2},{4,5},{5,4},{6,7},{7,6},{8,9},{9,8},{10,11... | collective-permute-start | bytes 49160 | tf_op jit(solution)/shard_map/ppermute | solution.py:118
  32.2 3.6 %shard_map.184 = (f32[3,16,32,256]{3,2,1,0:T(8,128)}, f32[16,32,256]{2,1,0:T(8,128)}) custom-call(f32[10,8,128]{2,1,0:T(8,128)S(1)} %get-tuple-element.65.refs_0_, f32[8,128]{1,0:T(8,128)S(1)} %get-tuple-element.43.refs_1_, s32[8,128]{1,0:T(8,128)S(1)} %get-tuple-element.66.refs_2_, f32[3,8,128]{2,1,0:T(8,128)S(1)} %get-tuple-element.46.refs_6_.refs_3_, ...), custom_call_target="tpu_custom_call" | custom-call | flops 33554432 | bytes 1048576 | tf_op jit(solution)/shard_map/pallas_call | solution.py:639
  35.9 0.7 %shard_map.185 = (f32[22,6,1,128]{3,2,1,0:T(1,128)}, s32[6,4,128]{2,1,0:T(4,128)}) custom-call(f32[32,128]{1,0:T(8,128)S(1)} %collective-permute-done.10.refs_0_, f32[32,128]{1,0:T(8,128)S(1)} %collective-permute-done.11.refs_1_, f32[32,128]{1,0:T(8,128)S(1)} %collective-permute-done.12.refs_2_, f32[32,128]{1,0:T(8,128)S(1)} %collective-permute-done.13.refs_3_, ...), custom_call_target="tpu_custom_call" | custom-call | flops 1048576 | bytes 1048576 | tf_op jit(solution)/shard_map/pallas_call | solution.py:639
  (24 shorter events, 0.1 us)
Async XLA Ops:
  0.6 11.9 %copy-start.2 = (s32[4,2,2,2,128]{4,3,2,1,0:T(2,128)S(1)}, s32[4,2,2,2,128]{4,3,2,1,0:T(2,128)}, u32[]{:S(2)}) copy-start(s32[4,2,2,2,128]{4,3,2,1,0:T(2,128)} %param.18) | copy-start | bytes 49156
  0.6 11.9 %copy-start.3 = (f32[3,4,2,2,2,128]{5,4,3,2,1,0:T(2,128)S(1)}, f32[3,4,2,2,2,128]{5,4,3,2,1,0:T(2,128)}, u32[]{:S(2)}) copy-start(f32[3,4,2,2,2,128]{5,4,3,2,1,0:T(2,128)} %param.17) | copy-start | bytes 147460
  2.1 10.5 %collective-permute-start = (f32[104,128]{1,0:T(8,128)S(1)}, f32[104,128]{1,0:T(8,128)S(1)}, u32[]{:S(2)}, u32[]{:S(2)}) collective-permute-start(f32[104,128]{1,0:T(8,128)S(1)} %get-tuple-element.47), channel_id=1, source_target_pairs={{0,8},{8,16},{16,24},{24,0},{1,9},{9,17},{17,25},{25,1},{2,10},{10... | collective-permute-start | bytes 159752 | tf_op jit(solution)/shard_map/ppermute | solution.py:118
  2.7 9.9 %collective-permute-start.1 = (f32[104,128]{1,0:T(8,128)S(1)}, f32[104,128]{1,0:T(8,128)S(1)}, u32[]{:S(2)}, u32[]{:S(2)}) collective-permute-start(f32[104,128]{1,0:T(8,128)S(1)} %get-tuple-element.48), channel_id=1, source_target_pairs={{8,0},{16,8},{24,16},{0,24},{9,1},{17,9},{25,17},{1,25},{10,2},{18... | collective-permute-start | bytes 159752 | tf_op jit(solution)/shard_map/ppermute | solution.py:118
  4.6 7.9 %collective-permute-start.2 = (f32[72,128]{1,0:T(8,128)S(1)}, f32[72,128]{1,0:T(8,128)S(1)}, u32[]{:S(2)}, u32[]{:S(2)}) collective-permute-start(f32[72,128]{1,0:T(8,128)S(1)} %get-tuple-element.49), channel_id=1, source_target_pairs={{0,2},{2,0},{4,6},{6,4},{1,3},{3,1},{5,7},{7,5},{8,10},{10,8},{12,... | collective-permute-start | bytes 110600 | tf_op jit(solution)/shard_map/ppermute | solution.py:118
  7.0 5.6 %collective-permute-start.3 = (f32[72,128]{1,0:T(8,128)S(1)}, f32[72,128]{1,0:T(8,128)S(1)}, u32[]{:S(2)}, u32[]{:S(2)}) collective-permute-start(f32[72,128]{1,0:T(8,128)S(1)} %get-tuple-element.50), channel_id=1, source_target_pairs={{2,4},{4,2},{0,8},{6,14},{10,12},{12,10},{8,0},{14,6},{18,20},{20,... | collective-permute-start | bytes 110600 | tf_op jit(solution)/shard_map/ppermute | solution.py:118
  7.0 5.6 %collective-permute-start.4 = (f32[72,128]{1,0:T(8,128)S(1)}, f32[72,128]{1,0:T(8,128)S(1)}, u32[]{:S(2)}, u32[]{:S(2)}) collective-permute-start(f32[72,128]{1,0:T(8,128)S(1)} %get-tuple-element.51), channel_id=1, source_target_pairs={{0,1},{1,0},{2,3},{3,2},{4,5},{5,4},{6,7},{7,6},{8,9},{9,8},{10,11... | collective-permute-start | bytes 110600 | tf_op jit(solution)/shard_map/ppermute | solution.py:118
  12.6 8.3 %copy-start.4 = (s32[1,1,1,6,128]{4,2,3,1,0:T(1,128)S(1)}, s32[1,1,1,6,128]{4,2,3,1,0:T(1,128)}, u32[]{:S(2)}) copy-start(s32[1,1,1,6,128]{4,2,3,1,0:T(1,128)} %param.20) | copy-start | bytes 9220
  15.1 9.4 %collective-permute-start.5 = (f32[40,128]{1,0:T(8,128)S(1)}, f32[40,128]{1,0:T(8,128)S(1)}, u32[]{:S(2)}, u32[]{:S(2)}) collective-permute-start(f32[40,128]{1,0:T(8,128)S(1)} %get-tuple-element.56), channel_id=1, source_target_pairs={{0,8},{8,16},{16,24},{24,0},{1,9},{9,17},{17,25},{25,1},{2,10},{10... | collective-permute-start | bytes 61448 | tf_op jit(solution)/shard_map/ppermute | solution.py:118
  15.5 9.0 %collective-permute-start.6 = (f32[40,128]{1,0:T(8,128)S(1)}, f32[40,128]{1,0:T(8,128)S(1)}, u32[]{:S(2)}, u32[]{:S(2)}) collective-permute-start(f32[40,128]{1,0:T(8,128)S(1)} %get-tuple-element.57), channel_id=1, source_target_pairs={{8,0},{16,8},{24,16},{0,24},{9,1},{17,9},{25,17},{1,25},{10,2},{18... | collective-permute-start | bytes 61448 | tf_op jit(solution)/shard_map/ppermute | solution.py:118
  16.9 7.6 %collective-permute-start.7 = (f32[40,128]{1,0:T(8,128)S(1)}, f32[40,128]{1,0:T(8,128)S(1)}, u32[]{:S(2)}, u32[]{:S(2)}) collective-permute-start(f32[40,128]{1,0:T(8,128)S(1)} %get-tuple-element.58), channel_id=1, source_target_pairs={{0,2},{2,0},{4,6},{6,4},{1,3},{3,1},{5,7},{7,5},{8,10},{10,8},{12,... | collective-permute-start | bytes 61448 | tf_op jit(solution)/shard_map/ppermute | solution.py:118
  20.8 3.7 %collective-permute-start.8 = (f32[40,128]{1,0:T(8,128)S(1)}, f32[40,128]{1,0:T(8,128)S(1)}, u32[]{:S(2)}, u32[]{:S(2)}) collective-permute-start(f32[40,128]{1,0:T(8,128)S(1)} %get-tuple-element.59), channel_id=1, source_target_pairs={{2,4},{4,2},{0,8},{6,14},{10,12},{12,10},{8,0},{14,6},{18,20},{20,... | collective-permute-start | bytes 61448 | tf_op jit(solution)/shard_map/ppermute | solution.py:118
  20.8 3.8 %collective-permute-start.9 = (f32[40,128]{1,0:T(8,128)S(1)}, f32[40,128]{1,0:T(8,128)S(1)}, u32[]{:S(2)}, u32[]{:S(2)}) collective-permute-start(f32[40,128]{1,0:T(8,128)S(1)} %get-tuple-element.60), channel_id=1, source_target_pairs={{0,1},{1,0},{2,3},{3,2},{4,5},{5,4},{6,7},{7,6},{8,9},{9,8},{10,11... | collective-permute-start | bytes 61448 | tf_op jit(solution)/shard_map/ppermute | solution.py:118
  24.6 7.7 %copy-start = (f32[16,32,256]{2,1,0:T(8,128)S(1)}, f32[16,32,256]{2,1,0:T(8,128)}, u32[]{:S(2)}) copy-start(f32[16,32,256]{2,1,0:T(8,128)} %refs_4_.1) | copy-start | bytes 1572868
  24.6 7.7 %copy-start.1 = (f32[16,32,256]{2,1,0:T(8,128)S(1)}, f32[16,32,256]{2,1,0:T(8,128)}, u32[]{:S(2)}) copy-start(f32[16,32,256]{2,1,0:T(8,128)} %refs_5_.1) | copy-start | bytes 1572868
  27.8 8.0 %collective-permute-start.10 = (f32[32,128]{1,0:T(8,128)S(1)}, f32[32,128]{1,0:T(8,128)S(1)}, u32[]{:S(2)}, u32[]{:S(2)}) collective-permute-start(f32[32,128]{1,0:T(8,128)S(1)} %get-tuple-element.69), channel_id=1, source_target_pairs={{0,8},{8,16},{16,24},{24,0},{1,9},{9,17},{17,25},{25,1},{2,10},{10... | collective-permute-start | bytes 49160 | tf_op jit(solution)/shard_map/ppermute | solution.py:118
  28.3 7.6 %collective-permute-start.11 = (f32[32,128]{1,0:T(8,128)S(1)}, f32[32,128]{1,0:T(8,128)S(1)}, u32[]{:S(2)}, u32[]{:S(2)}) collective-permute-start(f32[32,128]{1,0:T(8,128)S(1)} %get-tuple-element.70), channel_id=1, source_target_pairs={{8,0},{16,8},{24,16},{0,24},{9,1},{17,9},{25,17},{1,25},{10,2},{18... | collective-permute-start | bytes 49160 | tf_op jit(solution)/shard_map/ppermute | solution.py:118
  29.9 6.0 %collective-permute-start.12 = (f32[32,128]{1,0:T(8,128)S(1)}, f32[32,128]{1,0:T(8,128)S(1)}, u32[]{:S(2)}, u32[]{:S(2)}) collective-permute-start(f32[32,128]{1,0:T(8,128)S(1)} %get-tuple-element.71), channel_id=1, source_target_pairs={{0,2},{2,0},{4,6},{6,4},{1,3},{3,1},{5,7},{7,5},{8,10},{10,8},{12,... | collective-permute-start | bytes 49160 | tf_op jit(solution)/shard_map/ppermute | solution.py:118
  30.9 5.0 %collective-permute-start.13 = (f32[32,128]{1,0:T(8,128)S(1)}, f32[32,128]{1,0:T(8,128)S(1)}, u32[]{:S(2)}, u32[]{:S(2)}) collective-permute-start(f32[32,128]{1,0:T(8,128)S(1)} %get-tuple-element.72), channel_id=1, source_target_pairs={{2,4},{4,2},{0,8},{6,14},{10,12},{12,10},{8,0},{14,6},{18,20},{20,... | collective-permute-start | bytes 49160 | tf_op jit(solution)/shard_map/ppermute | solution.py:118
  30.9 5.0 %collective-permute-start.14 = (f32[32,128]{1,0:T(8,128)S(1)}, f32[32,128]{1,0:T(8,128)S(1)}, u32[]{:S(2)}, u32[]{:S(2)}) collective-permute-start(f32[32,128]{1,0:T(8,128)S(1)} %get-tuple-element.73), channel_id=1, source_target_pairs={{0,1},{1,0},{2,3},{3,2},{4,5},{5,4},{6,7},{7,6},{8,9},{9,8},{10,11... | collective-permute-start | bytes 49160 | tf_op jit(solution)/shard_map/ppermute | solution.py:118

commit v2 on v1

--- a/solution.py
+++ b/solution.py
@@ -113,17 +113,29 @@
     return lax.axis_index(axis) == edge
 
 
+START_ORDER = (3, 2, 4, 1, 0)
+
+
+def start_order(sizes):
+    count = send_count(sizes)
+    return START_ORDER if count == len(START_ORDER) else tuple(range(count))
+
+
 def exchange(blocks, sizes):
     routes = [route for axis in AXES for route in rolls(axis, sizes)]
+    routes = [routes[k] for k in start_order(sizes)]
     return [lax.ppermute(block, axes, pairs) for block, (axes, pairs) in zip(blocks, routes)]
 
 
 def per_axis(refs, sizes):
+    sorted_refs = [None] * len(refs)
+    for ref, k in zip(refs, start_order(sizes)):
+        sorted_refs[k] = ref
     out = []
     k = 0
     for axis in AXES:
         n = len(rolls(axis, sizes))
-        out.append(refs[k : k + n])
+        out.append(sorted_refs[k : k + n])
         k += n
     return out
 
@@ -144,33 +156,33 @@
                 ref[pl.ds(k, FIELDS, stride=width), :] = block
 
 
-def pack_kernel(plan, sizes, pos, vel, spin, rad, counts_hbm, pressure_hbm, *refs):
+def pack_kernel(plan, sizes, pos, vel, spin, rad, counts_hbm, *refs):
     state, radius = refs[:2]
-    sends = refs[2:-3]
-    counts, pressure, sems = refs[-3:]
+    sends = refs[2:-2]
+    counts, sems = refs[-2:]
     copies = [
         pltpu.make_async_copy(rad, radius, sems.at[0]),
         pltpu.make_async_copy(pos, state.at[0:3], sems.at[1]),
         pltpu.make_async_copy(vel, state.at[3:6], sems.at[2]),
         pltpu.make_async_copy(spin, state.at[6:9], sems.at[3]),
         pltpu.make_async_copy(counts_hbm, counts, sems.at[4]),
-        pltpu.make_async_copy(pressure_hbm, pressure, sems.at[5]),
     ]
     for copy in copies:
         copy.start()
     slots = rad.shape[-1]
     lane = lax.broadcasted_iota(jnp.int32, (1, slots), 1)
     places = plan.places()
-    for copy in copies[:5]:
+    for copy in copies:
         copy.wait()
     for b in range(plan.count):
         x, y, z = places[b]
         live = lane < counts[x, y : y + 1, z : z + 1]
         state[9, b : b + 1, :] = jnp.where(live, radius[b : b + 1, :], DEAD)
     put_faces(plan, sizes, state, sends)
-    copies[5].wait()
+
+
+def put_pressure(plan, sizes, lanes, pressure, sends):
     nx, ny, nz = pressure.shape
-    lanes = slots
     chunks = nz // lanes
     split = per_axis(sends, sizes)
     base = FIELDS * len(plan.face(0, 1))
@@ -208,11 +220,21 @@
 
 
 def spread_rows(mine, spread):
-    slots = mine.shape[-1]
-    turned = [jnp.transpose(mine[b], (1, 0)) for b in range(mine.shape[0])]
-    for b in range(mine.shape[0]):
+    bins, fields, slots = mine.shape
+    part = lax.broadcasted_iota(jnp.int32, (3 * fields, 7 * slots), 0) % fields
+    block = lax.broadcasted_iota(jnp.int32, (3 * fields, 7 * slots), 1) // slots
+    ones = (part == block).astype(jnp.bfloat16)
+    for b in range(bins):
+        rows = mine[b]
+        top = rows.astype(jnp.bfloat16).astype(f32)
+        left = rows - top
+        mid = left.astype(jnp.bfloat16).astype(f32)
+        parts = jnp.concatenate([top, mid, left - mid], axis=0).astype(jnp.bfloat16)
+        wide = lax.dot_general(
+            parts, ones, (((0,), (0,)), ((), ())), preferred_element_type=f32
+        )
         for f in range(7):
-            spread[b, f] = jnp.broadcast_to(turned[b][:, f : f + 1], (slots, slots))
+            spread[b, f] = wide[:, f * slots : (f + 1) * slots]
 
 
 def list_pairs(plan, entries, packed, table):
@@ -460,11 +482,12 @@
 
 def middle_kernel(plan, sizes, *refs):
     n = send_count(sizes)
-    state, radius, spread, inner, springs, partners, gas = refs[:7]
-    halos = refs[7 : 7 + n]
-    out, new_springs = refs[7 + n : 9 + n]
-    sends = refs[9 + n : 9 + 2 * n]
-    scratch = refs[9 + 2 * n :]
+    state, radius, spread, inner, springs, partners, gas, pressure = refs[:8]
+    halos = refs[8 : 8 + n]
+    out, new_springs = refs[8 + n : 10 + n]
+    sends = refs[10 + n : 10 + 2 * n]
+    scratch = refs[10 + 2 * n :]
+    put_pressure(plan, sizes, radius.shape[-1], pressure, sends)
     step_core(plan, sizes, state, radius, spread, inner, springs, partners, gas, halos, out,
               new_springs, *scratch)
     put_faces(plan, sizes, out, sends)
@@ -527,7 +550,7 @@
     rows = span[0] * span[1]
     high_row = lax.broadcasted_iota(jnp.int32, (rows, slots), 0)
     column_row = lax.broadcasted_iota(jnp.int32, (span[2], slots), 0)
-    for place in plan.places():
+    def deposit(place):
         b = plan.index(place)
         cell = cells[b : b + 1, :]
         live = state[9, b : b + 1, :] > 0.0
@@ -559,7 +582,6 @@
         pieces = [got[c * rows : (c + 1) * rows].reshape(span) for c in range(4)]
         for c in range(3):
             force[(c,) + block] = pieces[c]
-            send(force.at[(c,) + block], force_out.at[(c,) + block])
         new_pressure[block] = volume_coeff * pieces[3] + pieces[2]
     split = per_axis(halos, sizes)
     dead = [
@@ -590,7 +612,7 @@
     z_ends = [jnp.where(dead[2][s], 0.0, z_ends[s]) for s in (0, 1)]
     row = lax.broadcasted_iota(jnp.int32, (ny, nz), 0)
     column = lax.broadcasted_iota(jnp.int32, (ny, nz), 1)
-    for x in range(nx):
+    def sweep(x):
         here = pressure[x]
         total = pressure[x - 1] if x > 0 else x_ends[0]
         total = total + (pressure[x + 1] if x < nx - 1 else x_ends[1])
@@ -603,8 +625,22 @@
             column == nz - 1, z_ends[1][:, x : x + 1], pltpu.roll(here, nz - 1, 1)
         )
         new_pressure[x] = (total + (source[x] + new_pressure[x])) * (1.0 / 6.0)
-        if (x + 1) % span[0] == 0:
-            part = slice(x + 1 - span[0], x + 1)
+
+    layers = plan.dims[0]
+    for layer in range(layers + 1):
+        if layer < layers:
+            for place in plan.places():
+                if place[0] == layer:
+                    deposit(place)
+        if layer > 0:
+            for x in range((layer - 1) * span[0], layer * span[0]):
+                sweep(x)
+        if layer < layers:
+            part = slice(layer * span[0], (layer + 1) * span[0])
+            for c in range(3):
+                send(force.at[c, part], force_out.at[c, part])
+        if layer > 0:
+            part = slice((layer - 1) * span[0], layer * span[0])
             send(new_pressure.at[part], pressure_out.at[part])
     for copy in copies:
         copy.wait()
@@ -672,7 +708,7 @@
         for a in range(3):
             for _ in rolls(AXES[a], sizes):
                 out.append(((rows[a], slots), f32))
-        return out
+        return [out[k] for k in start_order(sizes)]
 
     inside = [sum(plan.neighbour(p, n)[0] for n in range(7)) for p in plan.places()]
 
@@ -691,14 +727,13 @@
 
     state, radius, *out = call(
         bind(pack_kernel, plan, sizes),
-        [state_shape, ((count, slots), f32)] + sends([f + e for f, e in zip(faces, extra)]),
+        [state_shape, ((count, slots), f32)] + sends(faces),
         [
             pltpu.VMEM(counts.shape, jnp.int32),
-            vm(nx, ny, nz),
-            pltpu.SemaphoreType.DMA((6,)),
+            pltpu.SemaphoreType.DMA((5,)),
         ],
-        [pos, vel, spin, radius, counts, pressure],
-        hbm=(0, 1, 2, 3, 4, 5),
+        [pos, vel, spin, radius, counts],
+        hbm=(0, 1, 2, 3, 4),
         flops=1 << 20,
     )
     first_halos = exchange(out, sizes)
@@ -712,9 +747,9 @@
     )
     state, springs, *out = call(
         bind(middle_kernel, plan, sizes),
-        [state_shape, spring_shape] + sends(faces),
+        [state_shape, spring_shape] + sends([f + e for f, e in zip(faces, extra)]),
         step_scratch,
-        [state, radius, spread, inner, springs, partners, gas] + first_halos,
+        [state, radius, spread, inner, springs, partners, gas, pressure] + first_halos,
         flops=1 << 25,
     )
     halos = exchange(out, sizes)
@@ -738,9 +773,9 @@
         [
             vm(3, nx, ny, nz),
             vm(nx, ny, nz),
-            pltpu.SemaphoreType.DMA((3 * count + plan.dims[0],)),
+            pltpu.SemaphoreType.DMA((4 * plan.dims[0],)),
         ],
-        [state, radius, cells, gas, pressure, pressure_source] + first_halos,
+        [state, radius, cells, gas, pressure, pressure_source] + halos,
         outs_hbm=True,
         flops=1 << 25,
     )

time: 36.9 us -> 32.6 us (0.88)
  Pallas kernels: 19 us -> 15.9 us
  starting transfers between devices: 16.6 us -> 13.8 us
  waiting for transfers between devices: 0.09 us -> 1.74 us
    pallas_call x7, Pallas kernels: 19 us -> 15.9 us  [call(): pl.pallas_call(kernel, out_shape=[jax.ShapeDtypeStruct(s, d) for s, d in...]
    ppermute x15, starting transfers between devices: 16.6 us -> 13.8 us  [exchange(): lax.ppermute(block, axes, pairs)]
    ppermute x15, waiting for transfers between devices: 0.09 us -> 1.74 us  [exchange(): lax.ppermute(block, axes, pairs)]
  transfers between devices with their start and end apart: 15 -> 15, of which waited for: 1 -> 3; matrix products, arithmetic and copies ran while one was open for 0% -> 0% of each run, Pallas kernels for 30% -> 26%
where the time goes in v2:
time: 32.6 us; the launch traced here: 32.3 us
  Pallas kernels  15.9 us (49%)
  starting transfers between devices  13.8 us (42%)
  waiting for transfers between devices  1.74 us (5%)
  between operations  0.82 us (3%)
    pallas_call x7, Pallas kernels, call(): pl.pallas_call(kernel, out_shape=[jax.ShapeDtypeStruct(s, d) for s, d in...  15.9 us
    ppermute x15, starting transfers between devices, exchange(): lax.ppermute(block, axes, pairs)  13.8 us
    ppermute x15, waiting for transfers between devices, exchange(): lax.ppermute(block, axes, pairs)  1.74 us
  transfers between devices with their start and end apart: 15, of which 3 were waited for; matrix products, arithmetic and copies ran while one was open for 0% of the time, Pallas kernels for 26%

profile of v2, /device:TPU:0, one launch (start us, length us, event | category | flops | bytes accessed | tf_op | source)
XLA Modules:
  0.0 32.3 jit_solution(12053522140030016911)
XLA Ops:
  0.7 0.9 %shard_map.179 = (f32[10,8,128]{2,1,0:T(8,128)S(1)}, f32[8,128]{1,0:T(8,128)S(1)}, f32[40,128]{1,0:T(8,128)S(1)}, f32[40,128]{1,0:T(8,128)S(1)}, f32[40,128]{1,0...) custom-call(f32[3,8,128]{2,1,0:T(8,128)} %bitcast.24, f32[3,8,128]{2,1,0:T(8,128)} %bitcast.25, ...), custom_call_target="tpu_custom_call" | custom-call | flops 1048576 | bytes 1048576 | tf_op jit(solution)/shard_map/pallas_call | solution.py:675
  1.6 0.6 %collective-permute-start = (f32[40,128]{1,0:T(8,128)S(1)}, f32[40,128]{1,0:T(8,128)S(1)}, u32[]{:S(2)}, u32[]{:S(2)}) collective-permute-start(f32[40,128]{1,0:T(8,128)S(1)} %get-tuple-element.47), channel_id=1, source_target_pairs={{2,4},{4,2},{0,8},{6,14},{10,12},{12,10},{8,0},{14,6},{18,20},{20,... | collective-permute-start | bytes 61448 | tf_op jit(solution)/shard_map/ppermute | solution.py:127
  2.2 4.1 %collective-permute-start.1 = (f32[40,128]{1,0:T(8,128)S(1)}, f32[40,128]{1,0:T(8,128)S(1)}, u32[]{:S(2)}, u32[]{:S(2)}) collective-permute-start(f32[40,128]{1,0:T(8,128)S(1)} %get-tuple-element.48), channel_id=1, source_target_pairs={{0,2},{2,0},{4,6},{6,4},{1,3},{3,1},{5,7},{7,5},{8,10},{10,8},{12,... | collective-permute-start | bytes 61448 | tf_op jit(solution)/shard_map/ppermute | solution.py:127
  6.3 1.5 %collective-permute-start.2 = (f32[40,128]{1,0:T(8,128)S(1)}, f32[40,128]{1,0:T(8,128)S(1)}, u32[]{:S(2)}, u32[]{:S(2)}) collective-permute-start(f32[40,128]{1,0:T(8,128)S(1)} %get-tuple-element.49), channel_id=1, source_target_pairs={{0,1},{1,0},{2,3},{3,2},{4,5},{5,4},{6,7},{7,6},{8,9},{9,8},{10,11... | collective-permute-start | bytes 61448 | tf_op jit(solution)/shard_map/ppermute | solution.py:127
  7.8 0.1 collective-permute-start.3
  7.9 0.4 %collective-permute-start.4 = (f32[40,128]{1,0:T(8,128)S(1)}, f32[40,128]{1,0:T(8,128)S(1)}, u32[]{:S(2)}, u32[]{:S(2)}) collective-permute-start(f32[40,128]{1,0:T(8,128)S(1)} %get-tuple-element.51), channel_id=1, source_target_pairs={{0,8},{8,16},{16,24},{24,0},{1,9},{9,17},{17,25},{25,1},{2,10},{10... | collective-permute-start | bytes 61448 | tf_op jit(solution)/shard_map/ppermute | solution.py:127
  8.3 3.5 %shard_map.180 = (f32[8,7,128,128]{3,2,1,0:T(8,128)S(1)}, f32[8,3,128,128]{3,2,1,0:T(8,128)S(1)}, f32[3,8,128]{2,1,0:T(8,128)S(1)}, s32[8,128]{1,0:T(8,128)S(1)}) custom-call(f32[10,8,128]{2,1,0:T(8,128)S(1)} %get-tuple-element.42.refs_0_, f32[8,128]{1,0:T(8,128)S(1)} %get-tuple-element.43.refs_1_, s32[8,128]{1,0:T(8,128)} %bitcast.27, ...), custom_call_target="tpu_custom_call" | custom-call | flops 33554432 | bytes 1048576 | tf_op jit(solution)/shard_map/pallas_call | solution.py:675
  12.0 0.0 copy-start.4
  12.0 2.5 %shard_map.181 = (f32[10,8,128]{2,1,0:T(8,128)S(1)}, f32[3,4,8,128]{3,2,1,0:T(8,128)S(1)}, f32[72,128]{1,0:T(8,128)S(1)}, f32[72,128]{1,0:T(8,128)S(1)}, f32[72,...) custom-call(f32[10,8,128]{2,1,0:T(8,128)S(1)} %get-tuple-element.42.refs_0_, ...), custom_call_target="tpu_custom_call" | custom-call | flops 33554432 | bytes 1048576 | tf_op jit(solution)/shard_map/pallas_call | solution.py:675
  14.5 1.0 %collective-permute-start.8 = (f32[104,128]{1,0:T(8,128)S(1)}, f32[104,128]{1,0:T(8,128)S(1)}, u32[]{:S(2)}, u32[]{:S(2)}) collective-permute-start(f32[104,128]{1,0:T(8,128)S(1)} %get-tuple-element.59), channel_id=1, source_target_pairs={{8,0},{16,8},{24,16},{0,24},{9,1},{17,9},{25,17},{1,25},{10,2},{18... | collective-permute-start | bytes 159752 | tf_op jit(solution)/shard_map/ppermute | solution.py:127
  15.5 1.6 %collective-permute-start.5 = (f32[72,128]{1,0:T(8,128)S(1)}, f32[72,128]{1,0:T(8,128)S(1)}, u32[]{:S(2)}, u32[]{:S(2)}) collective-permute-start(f32[72,128]{1,0:T(8,128)S(1)} %get-tuple-element.56), channel_id=1, source_target_pairs={{2,4},{4,2},{0,8},{6,14},{10,12},{12,10},{8,0},{14,6},{18,20},{20,... | collective-permute-start | bytes 110600 | tf_op jit(solution)/shard_map/ppermute | solution.py:127
  17.2 1.9 %collective-permute-start.6 = (f32[72,128]{1,0:T(8,128)S(1)}, f32[72,128]{1,0:T(8,128)S(1)}, u32[]{:S(2)}, u32[]{:S(2)}) collective-permute-start(f32[72,128]{1,0:T(8,128)S(1)} %get-tuple-element.57), channel_id=1, source_target_pairs={{0,2},{2,0},{4,6},{6,4},{1,3},{3,1},{5,7},{7,5},{8,10},{10,8},{12,... | collective-permute-start | bytes 110600 | tf_op jit(solution)/shard_map/ppermute | solution.py:127
  19.1 0.2 collective-permute-start.7
  19.3 3.0 %shard_map.182 = (f32[8,7,128,128]{3,2,1,0:T(8,128)S(1)}, f32[8,3,128,128]{3,2,1,0:T(8,128)S(1)}) custom-call(f32[10,8,128]{2,1,0:T(8,128)S(1)} %get-tuple-element.52.refs_0_, f32[8,128]{1,0:T(8,128)S(1)} %get-tuple-element.43.refs_1_), custom_call_target="tpu_custom_call" | custom-call | flops 33554432 | bytes 1048576 | tf_op jit(solution)/shard_map/pallas_call | solution.py:675
  22.3 0.7 %collective-permute-done.7.refs_10_.refs_8_ = f32[72,128]{1,0:T(8,128)S(1)} collective-permute-done((f32[72,128]{1,0:T(8,128)S(1)}, f32[72,128]{1,0:T(8,128)S(1)}, u32[]{:S(2)}, u32[]{:S(2)}) %collective-permute-start.7) | collective-permute-done | bytes 36896 | tf_op jit(solution)/shard_map/ppermute | solution.py:127
  23.0 3.2 %shard_map.183 = (f32[3,8,128]{2,1,0:T(8,128)}, f32[3,8,128]{2,1,0:T(8,128)}, f32[3,8,128]{2,1,0:T(8,128)}, f32[3,4,8,128]{3,2,1,0:T(8,128)}, f32[10,8,128]{2,1,...) custom-call(f32[10,8,128]{2,1,0:T(8,128)S(1)} %get-tuple-element.52., ...), custom_call_target="tpu_custom_call" | custom-call | flops 33554432 | bytes 1048576 | tf_op jit(solution)/shard_map/pallas_call | solution.py:675
  26.3 1.0 %collective-permute-start.11 = (f32[32,128]{1,0:T(8,128)S(1)}, f32[32,128]{1,0:T(8,128)S(1)}, u32[]{:S(2)}, u32[]{:S(2)}) collective-permute-start(f32[32,128]{1,0:T(8,128)S(1)} %get-tuple-element.70), channel_id=1, source_target_pairs={{0,2},{2,0},{4,6},{6,4},{1,3},{3,1},{5,7},{7,5},{8,10},{10,8},{12,... | collective-permute-start | bytes 49160 | tf_op jit(solution)/shard_map/ppermute | solution.py:127
  27.3 0.8 %collective-permute-start.12 = (f32[32,128]{1,0:T(8,128)S(1)}, f32[32,128]{1,0:T(8,128)S(1)}, u32[]{:S(2)}, u32[]{:S(2)}) collective-permute-start(f32[32,128]{1,0:T(8,128)S(1)} %get-tuple-element.71), channel_id=1, source_target_pairs={{0,1},{1,0},{2,3},{3,2},{4,5},{5,4},{6,7},{7,6},{8,9},{9,8},{10,11... | collective-permute-start | bytes 49160 | tf_op jit(solution)/shard_map/ppermute | solution.py:127
  28.0 0.4 %collective-permute-start.13 = (f32[32,128]{1,0:T(8,128)S(1)}, f32[32,128]{1,0:T(8,128)S(1)}, u32[]{:S(2)}, u32[]{:S(2)}) collective-permute-start(f32[32,128]{1,0:T(8,128)S(1)} %get-tuple-element.72), channel_id=1, source_target_pairs={{8,0},{16,8},{24,16},{0,24},{9,1},{17,9},{25,17},{1,25},{10,2},{18... | collective-permute-start | bytes 49160 | tf_op jit(solution)/shard_map/ppermute | solution.py:127
  28.4 0.2 collective-permute-start.14
  28.6 2.0 %shard_map.184 = (f32[3,16,32,256]{3,2,1,0:T(8,128)}, f32[16,32,256]{2,1,0:T(8,128)}) custom-call(f32[10,8,128]{2,1,0:T(8,128)S(1)} %get-tuple-element.65.refs_0_, f32[8,128]{1,0:T(8,128)S(1)} %get-tuple-element.43.refs_1_, s32[8,128]{1,0:T(8,128)S(1)} %get-tuple-element.66.refs_2_, f32[3,8,128]{2,1,0:T(8,128)S(1)} %get-tuple-element.46.refs_6_.refs_3_, ...), custom_call_target="tpu_custom_call" | custom-call | flops 33554432 | bytes 1048576 | tf_op jit(solution)/shard_map/pallas_call | solution.py:675
  30.5 0.5 %collective-permute-done.12.refs_2_ = f32[32,128]{1,0:T(8,128)S(1)} collective-permute-done((f32[32,128]{1,0:T(8,128)S(1)}, f32[32,128]{1,0:T(8,128)S(1)}, u32[]{:S(2)}, u32[]{:S(2)}) %collective-permute-start.12) | collective-permute-done | bytes 16416 | tf_op jit(solution)/shard_map/ppermute | solution.py:127
  31.0 0.5 %collective-permute-done.14.refs_4_ = f32[32,128]{1,0:T(8,128)S(1)} collective-permute-done((f32[32,128]{1,0:T(8,128)S(1)}, f32[32,128]{1,0:T(8,128)S(1)}, u32[]{:S(2)}, u32[]{:S(2)}) %collective-permute-start.14) | collective-permute-done | bytes 16416 | tf_op jit(solution)/shard_map/ppermute | solution.py:127
  31.6 0.7 %shard_map.185 = (f32[22,6,1,128]{3,2,1,0:T(1,128)}, s32[6,4,128]{2,1,0:T(4,128)}) custom-call(f32[32,128]{1,0:T(8,128)S(1)} %collective-permute-done.10.refs_0_, f32[32,128]{1,0:T(8,128)S(1)} %collective-permute-done.11.refs_1_, f32[32,128]{1,0:T(8,128)S(1)} %collective-permute-done.12.refs_2_, f32[32,128]{1,0:T(8,128)S(1)} %collective-permute-done.13.refs_3_, ...), custom_call_target="tpu_custom_call" | custom-call | flops 1048576 | bytes 1048576 | tf_op jit(solution)/shard_map/pallas_call | solution.py:675
  (24 shorter events, 0.1 us)
Async XLA Ops:
  0.6 11.3 %copy-start = (f32[16,32,256]{2,1,0:T(8,128)S(1)}, f32[16,32,256]{2,1,0:T(8,128)}, u32[]{:S(2)}) copy-start(f32[16,32,256]{2,1,0:T(8,128)} %refs_4_.1) | copy-start | bytes 1572868
  0.6 11.3 %copy-start.2 = (s32[4,2,2,2,128]{4,3,2,1,0:T(2,128)S(1)}, s32[4,2,2,2,128]{4,3,2,1,0:T(2,128)}, u32[]{:S(2)}) copy-start(s32[4,2,2,2,128]{4,3,2,1,0:T(2,128)} %param.18) | copy-start | bytes 49156
  0.7 11.3 %copy-start.3 = (f32[3,4,2,2,2,128]{5,4,3,2,1,0:T(2,128)S(1)}, f32[3,4,2,2,2,128]{5,4,3,2,1,0:T(2,128)}, u32[]{:S(2)}) copy-start(f32[3,4,2,2,2,128]{5,4,3,2,1,0:T(2,128)} %param.17) | copy-start | bytes 147460
  1.6 10.3 %collective-permute-start = (f32[40,128]{1,0:T(8,128)S(1)}, f32[40,128]{1,0:T(8,128)S(1)}, u32[]{:S(2)}, u32[]{:S(2)}) collective-permute-start(f32[40,128]{1,0:T(8,128)S(1)} %get-tuple-element.47), channel_id=1, source_target_pairs={{2,4},{4,2},{0,8},{6,14},{10,12},{12,10},{8,0},{14,6},{18,20},{20,... | collective-permute-start | bytes 61448 | tf_op jit(solution)/shard_map/ppermute | solution.py:127
  2.2 9.7 %collective-permute-start.1 = (f32[40,128]{1,0:T(8,128)S(1)}, f32[40,128]{1,0:T(8,128)S(1)}, u32[]{:S(2)}, u32[]{:S(2)}) collective-permute-start(f32[40,128]{1,0:T(8,128)S(1)} %get-tuple-element.48), channel_id=1, source_target_pairs={{0,2},{2,0},{4,6},{6,4},{1,3},{3,1},{5,7},{7,5},{8,10},{10,8},{12,... | collective-permute-start | bytes 61448 | tf_op jit(solution)/shard_map/ppermute | solution.py:127
  6.3 5.6 %collective-permute-start.2 = (f32[40,128]{1,0:T(8,128)S(1)}, f32[40,128]{1,0:T(8,128)S(1)}, u32[]{:S(2)}, u32[]{:S(2)}) collective-permute-start(f32[40,128]{1,0:T(8,128)S(1)} %get-tuple-element.49), channel_id=1, source_target_pairs={{0,1},{1,0},{2,3},{3,2},{4,5},{5,4},{6,7},{7,6},{8,9},{9,8},{10,11... | collective-permute-start | bytes 61448 | tf_op jit(solution)/shard_map/ppermute | solution.py:127
  7.8 4.1 %collective-permute-start.3 = (f32[40,128]{1,0:T(8,128)S(1)}, f32[40,128]{1,0:T(8,128)S(1)}, u32[]{:S(2)}, u32[]{:S(2)}) collective-permute-start(f32[40,128]{1,0:T(8,128)S(1)} %get-tuple-element.50), channel_id=1, source_target_pairs={{8,0},{16,8},{24,16},{0,24},{9,1},{17,9},{25,17},{1,25},{10,2},{18... | collective-permute-start | bytes 61448 | tf_op jit(solution)/shard_map/ppermute | solution.py:127
  7.9 4.0 %collective-permute-start.4 = (f32[40,128]{1,0:T(8,128)S(1)}, f32[40,128]{1,0:T(8,128)S(1)}, u32[]{:S(2)}, u32[]{:S(2)}) collective-permute-start(f32[40,128]{1,0:T(8,128)S(1)} %get-tuple-element.51), channel_id=1, source_target_pairs={{0,8},{8,16},{16,24},{24,0},{1,9},{9,17},{17,25},{25,1},{2,10},{10... | collective-permute-start | bytes 61448 | tf_op jit(solution)/shard_map/ppermute | solution.py:127
  12.0 7.4 %copy-start.4 = (s32[1,1,1,6,128]{4,2,3,1,0:T(1,128)S(1)}, s32[1,1,1,6,128]{4,2,3,1,0:T(1,128)}, u32[]{:S(2)}) copy-start(s32[1,1,1,6,128]{4,2,3,1,0:T(1,128)} %param.20) | copy-start | bytes 9220
  14.5 8.5 %collective-permute-start.8 = (f32[104,128]{1,0:T(8,128)S(1)}, f32[104,128]{1,0:T(8,128)S(1)}, u32[]{:S(2)}, u32[]{:S(2)}) collective-permute-start(f32[104,128]{1,0:T(8,128)S(1)} %get-tuple-element.59), channel_id=1, source_target_pairs={{8,0},{16,8},{24,16},{0,24},{9,1},{17,9},{25,17},{1,25},{10,2},{18... | collective-permute-start | bytes 159752 | tf_op jit(solution)/shard_map/ppermute | solution.py:127
  15.5 7.5 %collective-permute-start.9 = (f32[104,128]{1,0:T(8,128)S(1)}, f32[104,128]{1,0:T(8,128)S(1)}, u32[]{:S(2)}, u32[]{:S(2)}) collective-permute-start(f32[104,128]{1,0:T(8,128)S(1)} %get-tuple-element.60), channel_id=1, source_target_pairs={{0,8},{8,16},{16,24},{24,0},{1,9},{9,17},{17,25},{25,1},{2,10},{10... | collective-permute-start | bytes 159752 | tf_op jit(solution)/shard_map/ppermute | solution.py:127
  15.5 6.8 %collective-permute-start.5 = (f32[72,128]{1,0:T(8,128)S(1)}, f32[72,128]{1,0:T(8,128)S(1)}, u32[]{:S(2)}, u32[]{:S(2)}) collective-permute-start(f32[72,128]{1,0:T(8,128)S(1)} %get-tuple-element.56), channel_id=1, source_target_pairs={{2,4},{4,2},{0,8},{6,14},{10,12},{12,10},{8,0},{14,6},{18,20},{20,... | collective-permute-start | bytes 110600 | tf_op jit(solution)/shard_map/ppermute | solution.py:127
  17.2 5.2 %collective-permute-start.6 = (f32[72,128]{1,0:T(8,128)S(1)}, f32[72,128]{1,0:T(8,128)S(1)}, u32[]{:S(2)}, u32[]{:S(2)}) collective-permute-start(f32[72,128]{1,0:T(8,128)S(1)} %get-tuple-element.57), channel_id=1, source_target_pairs={{0,2},{2,0},{4,6},{6,4},{1,3},{3,1},{5,7},{7,5},{8,10},{10,8},{12,... | collective-permute-start | bytes 110600 | tf_op jit(solution)/shard_map/ppermute | solution.py:127
  19.1 4.0 %collective-permute-start.7 = (f32[72,128]{1,0:T(8,128)S(1)}, f32[72,128]{1,0:T(8,128)S(1)}, u32[]{:S(2)}, u32[]{:S(2)}) collective-permute-start(f32[72,128]{1,0:T(8,128)S(1)} %get-tuple-element.58), channel_id=1, source_target_pairs={{0,1},{1,0},{2,3},{3,2},{4,5},{5,4},{6,7},{7,6},{8,9},{9,8},{10,11... | collective-permute-start | bytes 110600 | tf_op jit(solution)/shard_map/ppermute | solution.py:127
  23.0 5.5 %copy-start.1 = (f32[16,32,256]{2,1,0:T(8,128)S(1)}, f32[16,32,256]{2,1,0:T(8,128)}, u32[]{:S(2)}) copy-start(f32[16,32,256]{2,1,0:T(8,128)} %refs_5_.1) | copy-start | bytes 1572868
  26.3 4.3 %collective-permute-start.10 = (f32[32,128]{1,0:T(8,128)S(1)}, f32[32,128]{1,0:T(8,128)S(1)}, u32[]{:S(2)}, u32[]{:S(2)}) collective-permute-start(f32[32,128]{1,0:T(8,128)S(1)} %get-tuple-element.69), channel_id=1, source_target_pairs={{2,4},{4,2},{0,8},{6,14},{10,12},{12,10},{8,0},{14,6},{18,20},{20,... | collective-permute-start | bytes 49160 | tf_op jit(solution)/shard_map/ppermute | solution.py:127
  26.3 4.3 %collective-permute-start.11 = (f32[32,128]{1,0:T(8,128)S(1)}, f32[32,128]{1,0:T(8,128)S(1)}, u32[]{:S(2)}, u32[]{:S(2)}) collective-permute-start(f32[32,128]{1,0:T(8,128)S(1)} %get-tuple-element.70), channel_id=1, source_target_pairs={{0,2},{2,0},{4,6},{6,4},{1,3},{3,1},{5,7},{7,5},{8,10},{10,8},{12,... | collective-permute-start | bytes 49160 | tf_op jit(solution)/shard_map/ppermute | solution.py:127
  27.3 3.7 %collective-permute-start.12 = (f32[32,128]{1,0:T(8,128)S(1)}, f32[32,128]{1,0:T(8,128)S(1)}, u32[]{:S(2)}, u32[]{:S(2)}) collective-permute-start(f32[32,128]{1,0:T(8,128)S(1)} %get-tuple-element.71), channel_id=1, source_target_pairs={{0,1},{1,0},{2,3},{3,2},{4,5},{5,4},{6,7},{7,6},{8,9},{9,8},{10,11... | collective-permute-start | bytes 49160 | tf_op jit(solution)/shard_map/ppermute | solution.py:127
  28.0 3.0 %collective-permute-start.13 = (f32[32,128]{1,0:T(8,128)S(1)}, f32[32,128]{1,0:T(8,128)S(1)}, u32[]{:S(2)}, u32[]{:S(2)}) collective-permute-start(f32[32,128]{1,0:T(8,128)S(1)} %get-tuple-element.72), channel_id=1, source_target_pairs={{8,0},{16,8},{24,16},{0,24},{9,1},{17,9},{25,17},{1,25},{10,2},{18... | collective-permute-start | bytes 49160 | tf_op jit(solution)/shard_map/ppermute | solution.py:127
  28.4 3.2 %collective-permute-start.14 = (f32[32,128]{1,0:T(8,128)S(1)}, f32[32,128]{1,0:T(8,128)S(1)}, u32[]{:S(2)}, u32[]{:S(2)}) collective-permute-start(f32[32,128]{1,0:T(8,128)S(1)} %get-tuple-element.73), channel_id=1, source_target_pairs={{0,8},{8,16},{16,24},{24,0},{1,9},{9,17},{17,25},{25,1},{2,10},{10... | collective-permute-start | bytes 49160 | tf_op jit(solution)/shard_map/ppermute | solution.py:127

commit v3 on v2

--- a/solution.py
+++ b/solution.py
@@ -32,6 +32,7 @@
     def __init__(self, shape):
         self.dims = shape
         self.count = shape[0] * shape[1] * shape[2]
+        self.strides = (shape[1] * shape[2], shape[2], 1)
 
     def index(self, place):
         return (place[0] * self.dims[1] + place[1]) * self.dims[2] + place[2]
@@ -113,7 +114,7 @@
     return lax.axis_index(axis) == edge
 
 
-START_ORDER = (3, 2, 4, 1, 0)
+START_ORDER = (1, 0, 3, 2, 4)
 
 
 def start_order(sizes):
@@ -144,16 +145,18 @@
     return sum(len(rolls(a, sizes)) for a in AXES)
 
 
-def put_faces(plan, sizes, state_ref, send_refs):
-    for axis, refs in enumerate(per_axis(send_refs, sizes)):
-        low = plan.face(axis, -1)
-        high = plan.face(axis, 1)
-        width = len(low)
-        for k in range(width):
-            a = state_ref[:, low[k], :]
-            b = state_ref[:, high[k], :]
-            for ref, block in zip(refs, ordered_send(AXES[axis], sizes[axis], a, b)):
-                ref[pl.ds(k, FIELDS, stride=width), :] = block
+def put_faces(plan, sizes, state, sends):
+    bins = plan.count
+    sub = lax.broadcasted_iota(jnp.int32, state.shape[1:], 0)
+    for axis, refs in enumerate(per_axis(sends, sizes)):
+        stride, dim = plan.strides[axis], plan.dims[axis]
+        level = sub // stride % dim
+        for g in range(FIELDS // 2):
+            one, two = state[2 * g], state[2 * g + 1]
+            low = jnp.where(level == 0, one, pltpu.roll(two, stride % bins, 0))
+            high = jnp.where(level == dim - 1, one, pltpu.roll(two, -stride % bins, 0))
+            for ref, block in zip(refs, ordered_send(AXES[axis], sizes[axis], low, high)):
+                ref[g * bins : (g + 1) * bins, :] = block
 
 
 def pack_kernel(plan, sizes, pos, vel, spin, rad, counts_hbm, *refs):
@@ -185,19 +188,19 @@
     nx, ny, nz = pressure.shape
     chunks = nz // lanes
     split = per_axis(sends, sizes)
-    base = FIELDS * len(plan.face(0, 1))
+    base = FIELDS // 2 * plan.count
     for ref, block in zip(
         split[0], ordered_send("gx", sizes[0], pressure[0], pressure[nx - 1])
     ):
         for c in range(chunks):
             ref[base + c * ny : base + (c + 1) * ny, :] = block[:, c * lanes : (c + 1) * lanes]
-    base = FIELDS * len(plan.face(1, 1))
+    base = FIELDS // 2 * plan.count
     for ref, block in zip(
         split[1], ordered_send("gy", sizes[1], pressure[:, 0, :], pressure[:, ny - 1, :])
     ):
         for c in range(chunks):
             ref[base + c * nx : base + (c + 1) * nx, :] = block[:, c * lanes : (c + 1) * lanes]
-    base = FIELDS * len(plan.face(2, 1))
+    base = FIELDS // 2 * plan.count
     wide = lax.broadcasted_iota(jnp.int32, (ny, lanes), 1)
     low = jnp.zeros((ny, lanes), f32)
     high = jnp.zeros((ny, lanes), f32)
@@ -354,48 +357,49 @@
 
 
 def step_core(plan, sizes, state, radius, spread, inner, springs, partners, gas, halos, out,
-              new_springs, around, packed, table, parts):
+              new_springs, around, beside, packed, table, parts):
     scale = normal_damp / normal_stiff
     places = plan.places()
     slots = radius.shape[-1]
     split = per_axis(halos, sizes)
     around[0] = state[...]
-    for axis in range(3):
-        width = len(plan.face(axis, 1))
-        for place in places:
-            b = plan.index(place)
-            for side in (0, 1):
-                n = 1 + 2 * axis + side
-                own, other = plan.neighbour(place, n)
-                if own:
-                    around[n, :, b, :] = state[:, other, :]
-                    continue
-                got = [ref[pl.ds(other, FIELDS, stride=width), :] for ref in split[axis]]
-                before, after = ordered_receive(AXES[axis], sizes[axis], got)
-                around[n, :, b, :] = after if side else before
     sub = lax.broadcasted_iota(jnp.int32, (plan.count, slots), 0)
     inner_count = [plan.dims[1] * plan.dims[2], plan.dims[2], 1]
     entries = [[] for _ in places]
     parts[...] = inner[...]
-    for n in range(1, 7):
-        axis = (n - 1) // 2
-        side = 1 if n % 2 == 0 else -1
-        edge = plan.dims[axis] - 1 if side > 0 else 0
-        level = sub // inner_count[axis] % plan.dims[axis]
-        gone = at_end(AXES[axis], sizes[axis], side)
-        reach = around[n, 9]
-        reach = jnp.where(((level == edge) & gone) | (reach <= 0.0), DEAD, reach)
-        around[n, 9] = reach
-        filled = jnp.sum(jnp.where(reach > 0.0, 1, 0), axis=1, keepdims=True)
-        for place in places:
-            b = plan.index(place)
-            if plan.neighbour(place, n)[0]:
-                continue
-            rows = around[n, 0:8, b, :]
-            field = lax.broadcasted_iota(jnp.int32, rows.shape, 0)
-            rows = jnp.where((field > 2) & (field < 6), rows * scale, rows)
-            rows = jnp.where(field == 6, reach[b : b + 1, :], rows)
-            entries[b].append((rows, filled[b, 0], neighbours[n]))
+    bins = plan.count
+    for axis in range(3):
+        stride = inner_count[axis]
+        dim = plan.dims[axis]
+        level = sub // stride % dim
+        for f in range(FIELDS):
+            rows = slice(f // 2 * bins, (f // 2 + 1) * bins)
+            far = (dim - 1 - f % 2) * stride
+            got = ordered_receive(AXES[axis], sizes[axis], [ref[rows, :] for ref in split[axis]])
+            for side in (-1, 1):
+                n = 2 * axis + (1 if side < 0 else 2)
+                edge = dim - 1 if side > 0 else 0
+                own = pltpu.roll(state[f], -side * stride % bins, 0)
+                other = pltpu.roll(got[1 if side > 0 else 0], side * far % bins, 0)
+                value = jnp.where(level == edge, other, own)
+                if f == 9:
+                    gone = at_end(AXES[axis], sizes[axis], side)
+                    value = jnp.where(((level == edge) & gone) | (value <= 0.0), DEAD, value)
+                    beside[n, :, 6, :] = value
+                    beside[n, :, 7, :] = value
+                    filled = jnp.sum(jnp.where(value > 0.0, 1, 0), axis=1, keepdims=True)
+                    for place in places:
+                        if not plan.neighbour(place, n)[0]:
+                            b = plan.index(place)
+                            entries[b].append((n, filled[b, 0]))
+                elif f < 3:
+                    beside[n, :, f, :] = value + float(neighbours[n][f])
+                elif f < 6:
+                    beside[n, :, f, :] = value * scale
+                around[n, f] = value
+    entries = [
+        [(beside[n, b], count, (0, 0, 0)) for n, count in entries[b]] for b in range(bins)
+    ]
     jobs = list_pairs(plan, entries, packed, table)
     run_pairs(jobs, spread, packed, table, parts)
     normal = []
@@ -587,7 +591,7 @@
     dead = [
         [at_end(AXES[axis], sizes[axis], side) for side in (-1, 1)] for axis in range(3)
     ]
-    base = FIELDS * len(plan.face(0, 1))
+    base = FIELDS // 2 * plan.count
     slabs = []
     for ref in split[0]:
         slabs.append(
@@ -597,7 +601,7 @@
         )
     x_ends = ordered_receive("gx", sizes[0], slabs)
     x_ends = [jnp.where(dead[0][s], 0.0, x_ends[s]) for s in (0, 1)]
-    base = FIELDS * len(plan.face(1, 1))
+    base = FIELDS // 2 * plan.count
     slabs = []
     for ref in split[1]:
         slabs.append(
@@ -607,7 +611,7 @@
         )
     y_ends = ordered_receive("gy", sizes[1], slabs)
     y_ends = [jnp.where(dead[1][s], 0.0, y_ends[s]) for s in (0, 1)]
-    base = FIELDS * len(plan.face(2, 1))
+    base = FIELDS // 2 * plan.count
     z_ends = ordered_receive("gz", sizes[2], [ref[base : base + ny, :] for ref in split[2]])
     z_ends = [jnp.where(dead[2][s], 0.0, z_ends[s]) for s in (0, 1)]
     row = lax.broadcasted_iota(jnp.int32, (ny, nz), 0)
@@ -699,7 +703,7 @@
     cells = cells.reshape(count, slots)
     leaving = departures.reshape(6, slots)
 
-    faces = [FIELDS * len(plan.face(a, 1)) for a in range(3)]
+    faces = [FIELDS // 2 * count] * 3
     extra = [chunks * ny, chunks * nx, ny]
     vm = lambda *s: pltpu.VMEM(s, f32)
 
@@ -718,7 +722,7 @@
     own_scratch = [vm(count, 8, slots)] + pair_scratch(sum(inside))
     spread_shape = ((count, 7, slots, slots), f32)
     parts_shape = ((count, 3, slots, slots), f32)
-    step_scratch = [vm(7, FIELDS, count, slots)] + pair_scratch(7 * count - sum(inside))
+    step_scratch = [vm(7, FIELDS, count, slots), vm(7, count, 8, slots)] + pair_scratch(7 * count - sum(inside))
     step_scratch.append(vm(count, 3, slots, slots))
     state_shape = ((FIELDS, count, slots), f32)
     three = ((3, count, slots), f32)

time: 32.6 us -> 31.9 us (0.979)
    ppermute x15, starting transfers between devices: 13.8 us -> 13.5 us  [exchange(): lax.ppermute(block, axes, pairs)]
  transfers between devices with their start and end apart: 15 -> 15, of which waited for: 3 -> 3; matrix products, arithmetic and copies ran while one was open for 0% -> 0% of each run, Pallas kernels for 26% -> 28%
where the time goes in v3:
time: 31.9 us; the launch traced here: 31.8 us
  Pallas kernels  15.7 us (49%)
  starting transfers between devices  13.5 us (42%)
  waiting for transfers between devices  1.81 us (6%)
  between operations  0.82 us (3%)
    pallas_call x7, Pallas kernels, call(): pl.pallas_call(kernel, out_shape=[jax.ShapeDtypeStruct(s, d) for s, d in...  15.7 us
    ppermute x15, starting transfers between devices, exchange(): lax.ppermute(block, axes, pairs)  13.5 us
    ppermute x15, waiting for transfers between devices, exchange(): lax.ppermute(block, axes, pairs)  1.81 us
  transfers between devices with their start and end apart: 15, of which 3 were waited for; matrix products, arithmetic and copies ran while one was open for 0% of the time, Pallas kernels for 28%

profile of v3, /device:TPU:0, one launch (start us, length us, event | category | flops | bytes accessed | tf_op | source)
XLA Modules:
  0.0 31.8 jit_solution(4788085994532342247)
XLA Ops:
  0.7 0.9 %shard_map.179 = (f32[10,8,128]{2,1,0:T(8,128)S(1)}, f32[8,128]{1,0:T(8,128)S(1)}, f32[40,128]{1,0:T(8,128)S(1)}, f32[40,128]{1,0:T(8,128)S(1)}, f32[40,128]{1,0...) custom-call(f32[3,8,128]{2,1,0:T(8,128)} %bitcast.24, f32[3,8,128]{2,1,0:T(8,128)} %bitcast.25, ...), custom_call_target="tpu_custom_call" | custom-call | flops 1048576 | bytes 1048576 | tf_op jit(solution)/shard_map/pallas_call | solution.py:679
  1.6 2.5 %collective-permute-start = (f32[40,128]{1,0:T(8,128)S(1)}, f32[40,128]{1,0:T(8,128)S(1)}, u32[]{:S(2)}, u32[]{:S(2)}) collective-permute-start(f32[40,128]{1,0:T(8,128)S(1)} %get-tuple-element.47), channel_id=1, source_target_pairs={{8,0},{16,8},{24,16},{0,24},{9,1},{17,9},{25,17},{1,25},{10,2},{18... | collective-permute-start | bytes 61448 | tf_op jit(solution)/shard_map/ppermute | solution.py:128
  4.1 0.0 collective-permute-start.1
  4.1 0.7 %collective-permute-start.2 = (f32[40,128]{1,0:T(8,128)S(1)}, f32[40,128]{1,0:T(8,128)S(1)}, u32[]{:S(2)}, u32[]{:S(2)}) collective-permute-start(f32[40,128]{1,0:T(8,128)S(1)} %get-tuple-element.49), channel_id=1, source_target_pairs={{2,4},{4,2},{0,8},{6,14},{10,12},{12,10},{8,0},{14,6},{18,20},{20,... | collective-permute-start | bytes 61448 | tf_op jit(solution)/shard_map/ppermute | solution.py:128
  4.8 2.4 %collective-permute-start.3 = (f32[40,128]{1,0:T(8,128)S(1)}, f32[40,128]{1,0:T(8,128)S(1)}, u32[]{:S(2)}, u32[]{:S(2)}) collective-permute-start(f32[40,128]{1,0:T(8,128)S(1)} %get-tuple-element.50), channel_id=1, source_target_pairs={{0,2},{2,0},{4,6},{6,4},{1,3},{3,1},{5,7},{7,5},{8,10},{10,8},{12,... | collective-permute-start | bytes 61448 | tf_op jit(solution)/shard_map/ppermute | solution.py:128
  7.2 1.5 %collective-permute-start.4 = (f32[40,128]{1,0:T(8,128)S(1)}, f32[40,128]{1,0:T(8,128)S(1)}, u32[]{:S(2)}, u32[]{:S(2)}) collective-permute-start(f32[40,128]{1,0:T(8,128)S(1)} %get-tuple-element.51), channel_id=1, source_target_pairs={{0,1},{1,0},{2,3},{3,2},{4,5},{5,4},{6,7},{7,6},{8,9},{9,8},{10,11... | collective-permute-start | bytes 61448 | tf_op jit(solution)/shard_map/ppermute | solution.py:128
  8.8 3.7 %shard_map.180 = (f32[8,7,128,128]{3,2,1,0:T(8,128)S(1)}, f32[8,3,128,128]{3,2,1,0:T(8,128)S(1)}, f32[3,8,128]{2,1,0:T(8,128)S(1)}, s32[8,128]{1,0:T(8,128)S(1)}) custom-call(f32[10,8,128]{2,1,0:T(8,128)S(1)} %get-tuple-element.42.refs_0_, f32[8,128]{1,0:T(8,128)S(1)} %get-tuple-element.43.refs_1_, s32[8,128]{1,0:T(8,128)} %bitcast.27, ...), custom_call_target="tpu_custom_call" | custom-call | flops 33554432 | bytes 1048576 | tf_op jit(solution)/shard_map/pallas_call | solution.py:679
  12.6 0.0 copy-start.4
  12.6 2.2 %shard_map.181 = (f32[10,8,128]{2,1,0:T(8,128)S(1)}, f32[3,4,8,128]{3,2,1,0:T(8,128)S(1)}, f32[104,128]{1,0:T(8,128)S(1)}, f32[104,128]{1,0:T(8,128)S(1)}, f32[7...) custom-call(f32[10,8,128]{2,1,0:T(8,128)S(1)} %get-tuple-element.42.refs_0_, ...), custom_call_target="tpu_custom_call" | custom-call | flops 33554432 | bytes 1048576 | tf_op jit(solution)/shard_map/pallas_call | solution.py:679
  14.8 0.6 %collective-permute-start.5 = (f32[104,128]{1,0:T(8,128)S(1)}, f32[104,128]{1,0:T(8,128)S(1)}, u32[]{:S(2)}, u32[]{:S(2)}) collective-permute-start(f32[104,128]{1,0:T(8,128)S(1)} %get-tuple-element.56), channel_id=1, source_target_pairs={{8,0},{16,8},{24,16},{0,24},{9,1},{17,9},{25,17},{1,25},{10,2},{18... | collective-permute-start | bytes 159752 | tf_op jit(solution)/shard_map/ppermute | solution.py:128
  15.4 0.8 %collective-permute-start.7 = (f32[72,128]{1,0:T(8,128)S(1)}, f32[72,128]{1,0:T(8,128)S(1)}, u32[]{:S(2)}, u32[]{:S(2)}) collective-permute-start(f32[72,128]{1,0:T(8,128)S(1)} %get-tuple-element.58), channel_id=1, source_target_pairs={{2,4},{4,2},{0,8},{6,14},{10,12},{12,10},{8,0},{14,6},{18,20},{20,... | collective-permute-start | bytes 110600 | tf_op jit(solution)/shard_map/ppermute | solution.py:128
  16.2 2.2 %collective-permute-start.8 = (f32[72,128]{1,0:T(8,128)S(1)}, f32[72,128]{1,0:T(8,128)S(1)}, u32[]{:S(2)}, u32[]{:S(2)}) collective-permute-start(f32[72,128]{1,0:T(8,128)S(1)} %get-tuple-element.59), channel_id=1, source_target_pairs={{0,2},{2,0},{4,6},{6,4},{1,3},{3,1},{5,7},{7,5},{8,10},{10,8},{12,... | collective-permute-start | bytes 110600 | tf_op jit(solution)/shard_map/ppermute | solution.py:128
  18.4 0.0 collective-permute-start.9
  18.5 3.2 %shard_map.182 = (f32[8,7,128,128]{3,2,1,0:T(8,128)S(1)}, f32[8,3,128,128]{3,2,1,0:T(8,128)S(1)}) custom-call(f32[10,8,128]{2,1,0:T(8,128)S(1)} %get-tuple-element.52.refs_0_, f32[8,128]{1,0:T(8,128)S(1)} %get-tuple-element.43.refs_1_), custom_call_target="tpu_custom_call" | custom-call | flops 33554432 | bytes 1048576 | tf_op jit(solution)/shard_map/pallas_call | solution.py:679
  21.7 0.7 %collective-permute-done.9.refs_12_.refs_10_ = f32[72,128]{1,0:T(8,128)S(1)} collective-permute-done((f32[72,128]{1,0:T(8,128)S(1)}, f32[72,128]{1,0:T(8,128)S(1)}, u32[]{:S(2)}, u32[]{:S(2)}) %collective-permute-start.9) | collective-permute-done | bytes 36896 | tf_op jit(solution)/shard_map/ppermute | solution.py:128
  22.4 3.0 %shard_map.183 = (f32[3,8,128]{2,1,0:T(8,128)}, f32[3,8,128]{2,1,0:T(8,128)}, f32[3,8,128]{2,1,0:T(8,128)}, f32[3,4,8,128]{3,2,1,0:T(8,128)}, f32[10,8,128]{2,1,...) custom-call(f32[10,8,128]{2,1,0:T(8,128)S(1)} %get-tuple-element.52., ...), custom_call_target="tpu_custom_call" | custom-call | flops 33554432 | bytes 1048576 | tf_op jit(solution)/shard_map/pallas_call | solution.py:679
  25.4 0.5 %collective-permute-start.11 = (f32[32,128]{1,0:T(8,128)S(1)}, f32[32,128]{1,0:T(8,128)S(1)}, u32[]{:S(2)}, u32[]{:S(2)}) collective-permute-start(f32[32,128]{1,0:T(8,128)S(1)} %get-tuple-element.70), channel_id=1, source_target_pairs={{0,8},{8,16},{16,24},{24,0},{1,9},{9,17},{17,25},{25,1},{2,10},{10... | collective-permute-start | bytes 49160 | tf_op jit(solution)/shard_map/ppermute | solution.py:128
  25.9 0.7 %collective-permute-start.12 = (f32[32,128]{1,0:T(8,128)S(1)}, f32[32,128]{1,0:T(8,128)S(1)}, u32[]{:S(2)}, u32[]{:S(2)}) collective-permute-start(f32[32,128]{1,0:T(8,128)S(1)} %get-tuple-element.71), channel_id=1, source_target_pairs={{2,4},{4,2},{0,8},{6,14},{10,12},{12,10},{8,0},{14,6},{18,20},{20,... | collective-permute-start | bytes 49160 | tf_op jit(solution)/shard_map/ppermute | solution.py:128
  26.7 0.8 %collective-permute-start.13 = (f32[32,128]{1,0:T(8,128)S(1)}, f32[32,128]{1,0:T(8,128)S(1)}, u32[]{:S(2)}, u32[]{:S(2)}) collective-permute-start(f32[32,128]{1,0:T(8,128)S(1)} %get-tuple-element.72), channel_id=1, source_target_pairs={{0,2},{2,0},{4,6},{6,4},{1,3},{3,1},{5,7},{7,5},{8,10},{10,8},{12,... | collective-permute-start | bytes 49160 | tf_op jit(solution)/shard_map/ppermute | solution.py:128
  27.4 0.7 %collective-permute-start.14 = (f32[32,128]{1,0:T(8,128)S(1)}, f32[32,128]{1,0:T(8,128)S(1)}, u32[]{:S(2)}, u32[]{:S(2)}) collective-permute-start(f32[32,128]{1,0:T(8,128)S(1)} %get-tuple-element.73), channel_id=1, source_target_pairs={{0,1},{1,0},{2,3},{3,2},{4,5},{5,4},{6,7},{7,6},{8,9},{9,8},{10,11... | collective-permute-start | bytes 49160 | tf_op jit(solution)/shard_map/ppermute | solution.py:128
  28.1 2.0 %shard_map.184 = (f32[3,16,32,256]{3,2,1,0:T(8,128)}, f32[16,32,256]{2,1,0:T(8,128)}) custom-call(f32[10,8,128]{2,1,0:T(8,128)S(1)} %get-tuple-element.65.refs_0_, f32[8,128]{1,0:T(8,128)S(1)} %get-tuple-element.43.refs_1_, s32[8,128]{1,0:T(8,128)S(1)} %get-tuple-element.66.refs_2_, f32[3,8,128]{2,1,0:T(8,128)S(1)} %get-tuple-element.46.refs_6_.refs_3_, ...), custom_call_target="tpu_custom_call" | custom-call | flops 33554432 | bytes 1048576 | tf_op jit(solution)/shard_map/pallas_call | solution.py:679
  30.1 0.3 %collective-permute-done.13.refs_3_ = f32[32,128]{1,0:T(8,128)S(1)} collective-permute-done((f32[32,128]{1,0:T(8,128)S(1)}, f32[32,128]{1,0:T(8,128)S(1)}, u32[]{:S(2)}, u32[]{:S(2)}) %collective-permute-start.13) | collective-permute-done | bytes 16416 | tf_op jit(solution)/shard_map/ppermute | solution.py:128
  30.4 0.8 %collective-permute-done.14.refs_4_ = f32[32,128]{1,0:T(8,128)S(1)} collective-permute-done((f32[32,128]{1,0:T(8,128)S(1)}, f32[32,128]{1,0:T(8,128)S(1)}, u32[]{:S(2)}, u32[]{:S(2)}) %collective-permute-start.14) | collective-permute-done | bytes 16416 | tf_op jit(solution)/shard_map/ppermute | solution.py:128
  31.2 0.7 %shard_map.185 = (f32[22,6,1,128]{3,2,1,0:T(1,128)}, s32[6,4,128]{2,1,0:T(4,128)}) custom-call(f32[32,128]{1,0:T(8,128)S(1)} %collective-permute-done.10.refs_0_, f32[32,128]{1,0:T(8,128)S(1)} %collective-permute-done.11.refs_1_, f32[32,128]{1,0:T(8,128)S(1)} %collective-permute-done.12.refs_2_, f32[32,128]{1,0:T(8,128)S(1)} %collective-permute-done.13.refs_3_, ...), custom_call_target="tpu_custom_call" | custom-call | flops 1048576 | bytes 1048576 | tf_op jit(solution)/shard_map/pallas_call | solution.py:679
  (24 shorter events, 0.1 us)
Async XLA Ops:
  0.6 11.9 %copy-start = (f32[16,32,256]{2,1,0:T(8,128)S(1)}, f32[16,32,256]{2,1,0:T(8,128)}, u32[]{:S(2)}) copy-start(f32[16,32,256]{2,1,0:T(8,128)} %refs_4_.1) | copy-start | bytes 1572868
  0.6 11.9 %copy-start.2 = (s32[4,2,2,2,128]{4,3,2,1,0:T(2,128)S(1)}, s32[4,2,2,2,128]{4,3,2,1,0:T(2,128)}, u32[]{:S(2)}) copy-start(s32[4,2,2,2,128]{4,3,2,1,0:T(2,128)} %param.18) | copy-start | bytes 49156
  0.7 11.9 %copy-start.3 = (f32[3,4,2,2,2,128]{5,4,3,2,1,0:T(2,128)S(1)}, f32[3,4,2,2,2,128]{5,4,3,2,1,0:T(2,128)}, u32[]{:S(2)}) copy-start(f32[3,4,2,2,2,128]{5,4,3,2,1,0:T(2,128)} %param.17) | copy-start | bytes 147460
  1.6 10.9 %collective-permute-start = (f32[40,128]{1,0:T(8,128)S(1)}, f32[40,128]{1,0:T(8,128)S(1)}, u32[]{:S(2)}, u32[]{:S(2)}) collective-permute-start(f32[40,128]{1,0:T(8,128)S(1)} %get-tuple-element.47), channel_id=1, source_target_pairs={{8,0},{16,8},{24,16},{0,24},{9,1},{17,9},{25,17},{1,25},{10,2},{18... | collective-permute-start | bytes 61448 | tf_op jit(solution)/shard_map/ppermute | solution.py:128
  4.1 8.4 %collective-permute-start.1 = (f32[40,128]{1,0:T(8,128)S(1)}, f32[40,128]{1,0:T(8,128)S(1)}, u32[]{:S(2)}, u32[]{:S(2)}) collective-permute-start(f32[40,128]{1,0:T(8,128)S(1)} %get-tuple-element.48), channel_id=1, source_target_pairs={{0,8},{8,16},{16,24},{24,0},{1,9},{9,17},{17,25},{25,1},{2,10},{10... | collective-permute-start | bytes 61448 | tf_op jit(solution)/shard_map/ppermute | solution.py:128
  4.1 8.4 %collective-permute-start.2 = (f32[40,128]{1,0:T(8,128)S(1)}, f32[40,128]{1,0:T(8,128)S(1)}, u32[]{:S(2)}, u32[]{:S(2)}) collective-permute-start(f32[40,128]{1,0:T(8,128)S(1)} %get-tuple-element.49), channel_id=1, source_target_pairs={{2,4},{4,2},{0,8},{6,14},{10,12},{12,10},{8,0},{14,6},{18,20},{20,... | collective-permute-start | bytes 61448 | tf_op jit(solution)/shard_map/ppermute | solution.py:128
  4.8 7.7 %collective-permute-start.3 = (f32[40,128]{1,0:T(8,128)S(1)}, f32[40,128]{1,0:T(8,128)S(1)}, u32[]{:S(2)}, u32[]{:S(2)}) collective-permute-start(f32[40,128]{1,0:T(8,128)S(1)} %get-tuple-element.50), channel_id=1, source_target_pairs={{0,2},{2,0},{4,6},{6,4},{1,3},{3,1},{5,7},{7,5},{8,10},{10,8},{12,... | collective-permute-start | bytes 61448 | tf_op jit(solution)/shard_map/ppermute | solution.py:128
  7.2 5.3 %collective-permute-start.4 = (f32[40,128]{1,0:T(8,128)S(1)}, f32[40,128]{1,0:T(8,128)S(1)}, u32[]{:S(2)}, u32[]{:S(2)}) collective-permute-start(f32[40,128]{1,0:T(8,128)S(1)} %get-tuple-element.51), channel_id=1, source_target_pairs={{0,1},{1,0},{2,3},{3,2},{4,5},{5,4},{6,7},{7,6},{8,9},{9,8},{10,11... | collective-permute-start | bytes 61448 | tf_op jit(solution)/shard_map/ppermute | solution.py:128
  12.6 5.9 %copy-start.4 = (s32[1,1,1,6,128]{4,2,3,1,0:T(1,128)S(1)}, s32[1,1,1,6,128]{4,2,3,1,0:T(1,128)}, u32[]{:S(2)}) copy-start(s32[1,1,1,6,128]{4,2,3,1,0:T(1,128)} %param.20) | copy-start | bytes 9220
  14.8 7.6 %collective-permute-start.5 = (f32[104,128]{1,0:T(8,128)S(1)}, f32[104,128]{1,0:T(8,128)S(1)}, u32[]{:S(2)}, u32[]{:S(2)}) collective-permute-start(f32[104,128]{1,0:T(8,128)S(1)} %get-tuple-element.56), channel_id=1, source_target_pairs={{8,0},{16,8},{24,16},{0,24},{9,1},{17,9},{25,17},{1,25},{10,2},{18... | collective-permute-start | bytes 159752 | tf_op jit(solution)/shard_map/ppermute | solution.py:128
  15.4 7.0 %collective-permute-start.6 = (f32[104,128]{1,0:T(8,128)S(1)}, f32[104,128]{1,0:T(8,128)S(1)}, u32[]{:S(2)}, u32[]{:S(2)}) collective-permute-start(f32[104,128]{1,0:T(8,128)S(1)} %get-tuple-element.57), channel_id=1, source_target_pairs={{0,8},{8,16},{16,24},{24,0},{1,9},{9,17},{17,25},{25,1},{2,10},{10... | collective-permute-start | bytes 159752 | tf_op jit(solution)/shard_map/ppermute | solution.py:128
  15.4 6.3 %collective-permute-start.7 = (f32[72,128]{1,0:T(8,128)S(1)}, f32[72,128]{1,0:T(8,128)S(1)}, u32[]{:S(2)}, u32[]{:S(2)}) collective-permute-start(f32[72,128]{1,0:T(8,128)S(1)} %get-tuple-element.58), channel_id=1, source_target_pairs={{2,4},{4,2},{0,8},{6,14},{10,12},{12,10},{8,0},{14,6},{18,20},{20,... | collective-permute-start | bytes 110600 | tf_op jit(solution)/shard_map/ppermute | solution.py:128
  16.2 5.4 %collective-permute-start.8 = (f32[72,128]{1,0:T(8,128)S(1)}, f32[72,128]{1,0:T(8,128)S(1)}, u32[]{:S(2)}, u32[]{:S(2)}) collective-permute-start(f32[72,128]{1,0:T(8,128)S(1)} %get-tuple-element.59), channel_id=1, source_target_pairs={{0,2},{2,0},{4,6},{6,4},{1,3},{3,1},{5,7},{7,5},{8,10},{10,8},{12,... | collective-permute-start | bytes 110600 | tf_op jit(solution)/shard_map/ppermute | solution.py:128
  18.4 4.0 %collective-permute-start.9 = (f32[72,128]{1,0:T(8,128)S(1)}, f32[72,128]{1,0:T(8,128)S(1)}, u32[]{:S(2)}, u32[]{:S(2)}) collective-permute-start(f32[72,128]{1,0:T(8,128)S(1)} %get-tuple-element.60), channel_id=1, source_target_pairs={{0,1},{1,0},{2,3},{3,2},{4,5},{5,4},{6,7},{7,6},{8,9},{9,8},{10,11... | collective-permute-start | bytes 110600 | tf_op jit(solution)/shard_map/ppermute | solution.py:128
  22.4 5.7 %copy-start.1 = (f32[16,32,256]{2,1,0:T(8,128)S(1)}, f32[16,32,256]{2,1,0:T(8,128)}, u32[]{:S(2)}) copy-start(f32[16,32,256]{2,1,0:T(8,128)} %refs_5_.1) | copy-start | bytes 1572868
  25.4 4.6 %collective-permute-start.10 = (f32[32,128]{1,0:T(8,128)S(1)}, f32[32,128]{1,0:T(8,128)S(1)}, u32[]{:S(2)}, u32[]{:S(2)}) collective-permute-start(f32[32,128]{1,0:T(8,128)S(1)} %get-tuple-element.69), channel_id=1, source_target_pairs={{8,0},{16,8},{24,16},{0,24},{9,1},{17,9},{25,17},{1,25},{10,2},{18... | collective-permute-start | bytes 49160 | tf_op jit(solution)/shard_map/ppermute | solution.py:128
  25.4 4.6 %collective-permute-start.11 = (f32[32,128]{1,0:T(8,128)S(1)}, f32[32,128]{1,0:T(8,128)S(1)}, u32[]{:S(2)}, u32[]{:S(2)}) collective-permute-start(f32[32,128]{1,0:T(8,128)S(1)} %get-tuple-element.70), channel_id=1, source_target_pairs={{0,8},{8,16},{16,24},{24,0},{1,9},{9,17},{17,25},{25,1},{2,10},{10... | collective-permute-start | bytes 49160 | tf_op jit(solution)/shard_map/ppermute | solution.py:128
  25.9 4.2 %collective-permute-start.12 = (f32[32,128]{1,0:T(8,128)S(1)}, f32[32,128]{1,0:T(8,128)S(1)}, u32[]{:S(2)}, u32[]{:S(2)}) collective-permute-start(f32[32,128]{1,0:T(8,128)S(1)} %get-tuple-element.71), channel_id=1, source_target_pairs={{2,4},{4,2},{0,8},{6,14},{10,12},{12,10},{8,0},{14,6},{18,20},{20,... | collective-permute-start | bytes 49160 | tf_op jit(solution)/shard_map/ppermute | solution.py:128
  26.7 3.7 %collective-permute-start.13 = (f32[32,128]{1,0:T(8,128)S(1)}, f32[32,128]{1,0:T(8,128)S(1)}, u32[]{:S(2)}, u32[]{:S(2)}) collective-permute-start(f32[32,128]{1,0:T(8,128)S(1)} %get-tuple-element.72), channel_id=1, source_target_pairs={{0,2},{2,0},{4,6},{6,4},{1,3},{3,1},{5,7},{7,5},{8,10},{10,8},{12,... | collective-permute-start | bytes 49160 | tf_op jit(solution)/shard_map/ppermute | solution.py:128
  27.4 3.7 %collective-permute-start.14 = (f32[32,128]{1,0:T(8,128)S(1)}, f32[32,128]{1,0:T(8,128)S(1)}, u32[]{:S(2)}, u32[]{:S(2)}) collective-permute-start(f32[32,128]{1,0:T(8,128)S(1)} %get-tuple-element.73), channel_id=1, source_target_pairs={{0,1},{1,0},{2,3},{3,2},{4,5},{5,4},{6,7},{7,6},{8,9},{9,8},{10,11... | collective-permute-start | bytes 49160 | tf_op jit(solution)/shard_map/ppermute | solution.py:128

commit v4 on v3

--- a/solution.py
+++ b/solution.py
@@ -114,7 +114,7 @@
     return lax.axis_index(axis) == edge
 
 
-START_ORDER = (1, 0, 3, 2, 4)
+START_ORDER = (1, 0, 3, 4, 2)
 
 
 def start_order(sizes):

time: 31.9 us -> 32.6 us (1.022)
  starting transfers between devices: 13.5 us -> 14.7 us
  Pallas kernels: 15.7 us -> 15.3 us
    ppermute x15, starting transfers between devices: 13.5 us -> 14.7 us  [exchange(): lax.ppermute(block, axes, pairs)]
    pallas_call x7, Pallas kernels: 15.7 us -> 15.3 us  [call(): pl.pallas_call(kernel, out_shape=[jax.ShapeDtypeStruct(s, d) for s, d in...]
  transfers between devices with their start and end apart: 15 -> 15, of which waited for: 3 -> 2; matrix products, arithmetic and copies ran while one was open for 0% -> 0% of each run, Pallas kernels for 28% -> 25%
where the time goes in v4:
time: 32.6 us; the launch traced here: 32.9 us
  Pallas kernels  15.3 us (47%)
  starting transfers between devices  14.7 us (45%)
  waiting for transfers between devices  1.93 us (6%)
  between operations  0.83 us (3%)
    pallas_call x7, Pallas kernels, call(): pl.pallas_call(kernel, out_shape=[jax.ShapeDtypeStruct(s, d) for s, d in...  15.3 us
    ppermute x15, starting transfers between devices, exchange(): lax.ppermute(block, axes, pairs)  14.7 us
    ppermute x15, waiting for transfers between devices, exchange(): lax.ppermute(block, axes, pairs)  1.93 us
  transfers between devices with their start and end apart: 15, of which 2 were waited for; matrix products, arithmetic and copies ran while one was open for 0% of the time, Pallas kernels for 25%

profile of v4, /device:TPU:0, one launch (start us, length us, event | category | flops | bytes accessed | tf_op | source)
XLA Modules:
  0.0 32.9 jit_solution(1506321364066862968)
XLA Ops:
  0.7 0.9 %shard_map.179 = (f32[10,8,128]{2,1,0:T(8,128)S(1)}, f32[8,128]{1,0:T(8,128)S(1)}, f32[40,128]{1,0:T(8,128)S(1)}, f32[40,128]{1,0:T(8,128)S(1)}, f32[40,128]{1,0...) custom-call(f32[3,8,128]{2,1,0:T(8,128)} %bitcast.24, f32[3,8,128]{2,1,0:T(8,128)} %bitcast.25, ...), custom_call_target="tpu_custom_call" | custom-call | flops 1048576 | bytes 1048576 | tf_op jit(solution)/shard_map/pallas_call | solution.py:679
  1.6 2.5 %collective-permute-start = (f32[40,128]{1,0:T(8,128)S(1)}, f32[40,128]{1,0:T(8,128)S(1)}, u32[]{:S(2)}, u32[]{:S(2)}) collective-permute-start(f32[40,128]{1,0:T(8,128)S(1)} %get-tuple-element.47), channel_id=1, source_target_pairs={{8,0},{16,8},{24,16},{0,24},{9,1},{17,9},{25,17},{1,25},{10,2},{18... | collective-permute-start | bytes 61448 | tf_op jit(solution)/shard_map/ppermute | solution.py:128
  4.1 0.0 collective-permute-start.1
  4.1 0.7 %collective-permute-start.2 = (f32[40,128]{1,0:T(8,128)S(1)}, f32[40,128]{1,0:T(8,128)S(1)}, u32[]{:S(2)}, u32[]{:S(2)}) collective-permute-start(f32[40,128]{1,0:T(8,128)S(1)} %get-tuple-element.49), channel_id=1, source_target_pairs={{2,4},{4,2},{0,8},{6,14},{10,12},{12,10},{8,0},{14,6},{18,20},{20,... | collective-permute-start | bytes 61448 | tf_op jit(solution)/shard_map/ppermute | solution.py:128
  4.8 1.5 %collective-permute-start.3 = (f32[40,128]{1,0:T(8,128)S(1)}, f32[40,128]{1,0:T(8,128)S(1)}, u32[]{:S(2)}, u32[]{:S(2)}) collective-permute-start(f32[40,128]{1,0:T(8,128)S(1)} %get-tuple-element.50), channel_id=1, source_target_pairs={{0,1},{1,0},{2,3},{3,2},{4,5},{5,4},{6,7},{7,6},{8,9},{9,8},{10,11... | collective-permute-start | bytes 61448 | tf_op jit(solution)/shard_map/ppermute | solution.py:128
  6.3 2.4 %collective-permute-start.4 = (f32[40,128]{1,0:T(8,128)S(1)}, f32[40,128]{1,0:T(8,128)S(1)}, u32[]{:S(2)}, u32[]{:S(2)}) collective-permute-start(f32[40,128]{1,0:T(8,128)S(1)} %get-tuple-element.51), channel_id=1, source_target_pairs={{0,2},{2,0},{4,6},{6,4},{1,3},{3,1},{5,7},{7,5},{8,10},{10,8},{12,... | collective-permute-start | bytes 61448 | tf_op jit(solution)/shard_map/ppermute | solution.py:128
  8.8 3.4 %shard_map.180 = (f32[8,7,128,128]{3,2,1,0:T(8,128)S(1)}, f32[8,3,128,128]{3,2,1,0:T(8,128)S(1)}, f32[3,8,128]{2,1,0:T(8,128)S(1)}, s32[8,128]{1,0:T(8,128)S(1)}) custom-call(f32[10,8,128]{2,1,0:T(8,128)S(1)} %get-tuple-element.42.refs_0_, f32[8,128]{1,0:T(8,128)S(1)} %get-tuple-element.43.refs_1_, s32[8,128]{1,0:T(8,128)} %bitcast.27, ...), custom_call_target="tpu_custom_call" | custom-call | flops 33554432 | bytes 1048576 | tf_op jit(solution)/shard_map/pallas_call | solution.py:679
  12.2 0.0 collective-permute-done.refs_8_
  12.2 0.0 collective-permute-done.2.refs_10_
  12.3 0.0 copy-start.4
  12.3 2.3 %shard_map.181 = (f32[10,8,128]{2,1,0:T(8,128)S(1)}, f32[3,4,8,128]{3,2,1,0:T(8,128)S(1)}, f32[104,128]{1,0:T(8,128)S(1)}, f32[104,128]{1,0:T(8,128)S(1)}, f32[7...) custom-call(f32[10,8,128]{2,1,0:T(8,128)S(1)} %get-tuple-element.42.refs_0_, ...), custom_call_target="tpu_custom_call" | custom-call | flops 33554432 | bytes 1048576 | tf_op jit(solution)/shard_map/pallas_call | solution.py:679
  14.6 1.1 %collective-permute-start.5 = (f32[104,128]{1,0:T(8,128)S(1)}, f32[104,128]{1,0:T(8,128)S(1)}, u32[]{:S(2)}, u32[]{:S(2)}) collective-permute-start(f32[104,128]{1,0:T(8,128)S(1)} %get-tuple-element.56), channel_id=1, source_target_pairs={{8,0},{16,8},{24,16},{0,24},{9,1},{17,9},{25,17},{1,25},{10,2},{18... | collective-permute-start | bytes 159752 | tf_op jit(solution)/shard_map/ppermute | solution.py:128
  15.8 0.9 %collective-permute-start.7 = (f32[72,128]{1,0:T(8,128)S(1)}, f32[72,128]{1,0:T(8,128)S(1)}, u32[]{:S(2)}, u32[]{:S(2)}) collective-permute-start(f32[72,128]{1,0:T(8,128)S(1)} %get-tuple-element.58), channel_id=1, source_target_pairs={{2,4},{4,2},{0,8},{6,14},{10,12},{12,10},{8,0},{14,6},{18,20},{20,... | collective-permute-start | bytes 110600 | tf_op jit(solution)/shard_map/ppermute | solution.py:128
  16.6 0.6 %collective-permute-start.8 = (f32[72,128]{1,0:T(8,128)S(1)}, f32[72,128]{1,0:T(8,128)S(1)}, u32[]{:S(2)}, u32[]{:S(2)}) collective-permute-start(f32[72,128]{1,0:T(8,128)S(1)} %get-tuple-element.59), channel_id=1, source_target_pairs={{0,1},{1,0},{2,3},{3,2},{4,5},{5,4},{6,7},{7,6},{8,9},{9,8},{10,11... | collective-permute-start | bytes 110600 | tf_op jit(solution)/shard_map/ppermute | solution.py:128
  17.2 0.9 %collective-permute-start.9 = (f32[72,128]{1,0:T(8,128)S(1)}, f32[72,128]{1,0:T(8,128)S(1)}, u32[]{:S(2)}, u32[]{:S(2)}) collective-permute-start(f32[72,128]{1,0:T(8,128)S(1)} %get-tuple-element.60), channel_id=1, source_target_pairs={{0,2},{2,0},{4,6},{6,4},{1,3},{3,1},{5,7},{7,5},{8,10},{10,8},{12,... | collective-permute-start | bytes 110600 | tf_op jit(solution)/shard_map/ppermute | solution.py:128
  18.1 2.9 %shard_map.182 = (f32[8,7,128,128]{3,2,1,0:T(8,128)S(1)}, f32[8,3,128,128]{3,2,1,0:T(8,128)S(1)}) custom-call(f32[10,8,128]{2,1,0:T(8,128)S(1)} %get-tuple-element.52.refs_0_, f32[8,128]{1,0:T(8,128)S(1)} %get-tuple-element.43.refs_1_), custom_call_target="tpu_custom_call" | custom-call | flops 33554432 | bytes 1048576 | tf_op jit(solution)/shard_map/pallas_call | solution.py:679
  21.0 0.2 collective-permute-done.9.refs_12_.refs_10_
  21.2 3.1 %shard_map.183 = (f32[3,8,128]{2,1,0:T(8,128)}, f32[3,8,128]{2,1,0:T(8,128)}, f32[3,8,128]{2,1,0:T(8,128)}, f32[3,4,8,128]{3,2,1,0:T(8,128)}, f32[10,8,128]{2,1,...) custom-call(f32[10,8,128]{2,1,0:T(8,128)S(1)} %get-tuple-element.52., ...), custom_call_target="tpu_custom_call" | custom-call | flops 33554432 | bytes 1048576 | tf_op jit(solution)/shard_map/pallas_call | solution.py:679
  24.3 1.0 %collective-permute-start.10 = (f32[32,128]{1,0:T(8,128)S(1)}, f32[32,128]{1,0:T(8,128)S(1)}, u32[]{:S(2)}, u32[]{:S(2)}) collective-permute-start(f32[32,128]{1,0:T(8,128)S(1)} %get-tuple-element.69), channel_id=1, source_target_pairs={{8,0},{16,8},{24,16},{0,24},{9,1},{17,9},{25,17},{1,25},{10,2},{18... | collective-permute-start | bytes 49160 | tf_op jit(solution)/shard_map/ppermute | solution.py:128
  25.2 1.4 %collective-permute-start.12 = (f32[32,128]{1,0:T(8,128)S(1)}, f32[32,128]{1,0:T(8,128)S(1)}, u32[]{:S(2)}, u32[]{:S(2)}) collective-permute-start(f32[32,128]{1,0:T(8,128)S(1)} %get-tuple-element.71), channel_id=1, source_target_pairs={{2,4},{4,2},{0,8},{6,14},{10,12},{12,10},{8,0},{14,6},{18,20},{20,... | collective-permute-start | bytes 49160 | tf_op jit(solution)/shard_map/ppermute | solution.py:128
  26.6 1.8 %collective-permute-start.13 = (f32[32,128]{1,0:T(8,128)S(1)}, f32[32,128]{1,0:T(8,128)S(1)}, u32[]{:S(2)}, u32[]{:S(2)}) collective-permute-start(f32[32,128]{1,0:T(8,128)S(1)} %get-tuple-element.72), channel_id=1, source_target_pairs={{0,1},{1,0},{2,3},{3,2},{4,5},{5,4},{6,7},{7,6},{8,9},{9,8},{10,11... | collective-permute-start | bytes 49160 | tf_op jit(solution)/shard_map/ppermute | solution.py:128
  28.4 2.0 %shard_map.184 = (f32[3,16,32,256]{3,2,1,0:T(8,128)}, f32[16,32,256]{2,1,0:T(8,128)}) custom-call(f32[10,8,128]{2,1,0:T(8,128)S(1)} %get-tuple-element.65.refs_0_, f32[8,128]{1,0:T(8,128)S(1)} %get-tuple-element.43.refs_1_, s32[8,128]{1,0:T(8,128)S(1)} %get-tuple-element.66.refs_2_, f32[3,8,128]{2,1,0:T(8,128)S(1)} %get-tuple-element.46.refs_6_.refs_3_, ...), custom_call_target="tpu_custom_call" | custom-call | flops 33554432 | bytes 1048576 | tf_op jit(solution)/shard_map/pallas_call | solution.py:679
  30.5 1.7 %collective-permute-done.14.refs_4_ = f32[32,128]{1,0:T(8,128)S(1)} collective-permute-done((f32[32,128]{1,0:T(8,128)S(1)}, f32[32,128]{1,0:T(8,128)S(1)}, u32[]{:S(2)}, u32[]{:S(2)}) %collective-permute-start.14) | collective-permute-done | bytes 16416 | tf_op jit(solution)/shard_map/ppermute | solution.py:128
  32.2 0.7 %shard_map.185 = (f32[22,6,1,128]{3,2,1,0:T(1,128)}, s32[6,4,128]{2,1,0:T(4,128)}) custom-call(f32[32,128]{1,0:T(8,128)S(1)} %collective-permute-done.10.refs_0_, f32[32,128]{1,0:T(8,128)S(1)} %collective-permute-done.11.refs_1_, f32[32,128]{1,0:T(8,128)S(1)} %collective-permute-done.12.refs_2_, f32[32,128]{1,0:T(8,128)S(1)} %collective-permute-done.13.refs_3_, ...), custom_call_target="tpu_custom_call" | custom-call | flops 1048576 | bytes 1048576 | tf_op jit(solution)/shard_map/pallas_call | solution.py:679
  (24 shorter events, 0.1 us)
Async XLA Ops:
  0.6 11.6 %copy-start = (f32[16,32,256]{2,1,0:T(8,128)S(1)}, f32[16,32,256]{2,1,0:T(8,128)}, u32[]{:S(2)}) copy-start(f32[16,32,256]{2,1,0:T(8,128)} %refs_4_.1) | copy-start | bytes 1572868
  0.6 11.6 %copy-start.2 = (s32[4,2,2,2,128]{4,3,2,1,0:T(2,128)S(1)}, s32[4,2,2,2,128]{4,3,2,1,0:T(2,128)}, u32[]{:S(2)}) copy-start(s32[4,2,2,2,128]{4,3,2,1,0:T(2,128)} %param.18) | copy-start | bytes 49156
  0.7 11.6 %copy-start.3 = (f32[3,4,2,2,2,128]{5,4,3,2,1,0:T(2,128)S(1)}, f32[3,4,2,2,2,128]{5,4,3,2,1,0:T(2,128)}, u32[]{:S(2)}) copy-start(f32[3,4,2,2,2,128]{5,4,3,2,1,0:T(2,128)} %param.17) | copy-start | bytes 147460
  1.6 10.6 %collective-permute-start = (f32[40,128]{1,0:T(8,128)S(1)}, f32[40,128]{1,0:T(8,128)S(1)}, u32[]{:S(2)}, u32[]{:S(2)}) collective-permute-start(f32[40,128]{1,0:T(8,128)S(1)} %get-tuple-element.47), channel_id=1, source_target_pairs={{8,0},{16,8},{24,16},{0,24},{9,1},{17,9},{25,17},{1,25},{10,2},{18... | collective-permute-start | bytes 61448 | tf_op jit(solution)/shard_map/ppermute | solution.py:128
  4.1 8.1 %collective-permute-start.1 = (f32[40,128]{1,0:T(8,128)S(1)}, f32[40,128]{1,0:T(8,128)S(1)}, u32[]{:S(2)}, u32[]{:S(2)}) collective-permute-start(f32[40,128]{1,0:T(8,128)S(1)} %get-tuple-element.48), channel_id=1, source_target_pairs={{0,8},{8,16},{16,24},{24,0},{1,9},{9,17},{17,25},{25,1},{2,10},{10... | collective-permute-start | bytes 61448 | tf_op jit(solution)/shard_map/ppermute | solution.py:128
  4.1 8.1 %collective-permute-start.2 = (f32[40,128]{1,0:T(8,128)S(1)}, f32[40,128]{1,0:T(8,128)S(1)}, u32[]{:S(2)}, u32[]{:S(2)}) collective-permute-start(f32[40,128]{1,0:T(8,128)S(1)} %get-tuple-element.49), channel_id=1, source_target_pairs={{2,4},{4,2},{0,8},{6,14},{10,12},{12,10},{8,0},{14,6},{18,20},{20,... | collective-permute-start | bytes 61448 | tf_op jit(solution)/shard_map/ppermute | solution.py:128
  4.8 7.4 %collective-permute-start.3 = (f32[40,128]{1,0:T(8,128)S(1)}, f32[40,128]{1,0:T(8,128)S(1)}, u32[]{:S(2)}, u32[]{:S(2)}) collective-permute-start(f32[40,128]{1,0:T(8,128)S(1)} %get-tuple-element.50), channel_id=1, source_target_pairs={{0,1},{1,0},{2,3},{3,2},{4,5},{5,4},{6,7},{7,6},{8,9},{9,8},{10,11... | collective-permute-start | bytes 61448 | tf_op jit(solution)/shard_map/ppermute | solution.py:128
  6.3 5.9 %collective-permute-start.4 = (f32[40,128]{1,0:T(8,128)S(1)}, f32[40,128]{1,0:T(8,128)S(1)}, u32[]{:S(2)}, u32[]{:S(2)}) collective-permute-start(f32[40,128]{1,0:T(8,128)S(1)} %get-tuple-element.51), channel_id=1, source_target_pairs={{0,2},{2,0},{4,6},{6,4},{1,3},{3,1},{5,7},{7,5},{8,10},{10,8},{12,... | collective-permute-start | bytes 61448 | tf_op jit(solution)/shard_map/ppermute | solution.py:128
  12.3 5.8 %copy-start.4 = (s32[1,1,1,6,128]{4,2,3,1,0:T(1,128)S(1)}, s32[1,1,1,6,128]{4,2,3,1,0:T(1,128)}, u32[]{:S(2)}) copy-start(s32[1,1,1,6,128]{4,2,3,1,0:T(1,128)} %param.20) | copy-start | bytes 9220
  14.6 6.5 %collective-permute-start.5 = (f32[104,128]{1,0:T(8,128)S(1)}, f32[104,128]{1,0:T(8,128)S(1)}, u32[]{:S(2)}, u32[]{:S(2)}) collective-permute-start(f32[104,128]{1,0:T(8,128)S(1)} %get-tuple-element.56), channel_id=1, source_target_pairs={{8,0},{16,8},{24,16},{0,24},{9,1},{17,9},{25,17},{1,25},{10,2},{18... | collective-permute-start | bytes 159752 | tf_op jit(solution)/shard_map/ppermute | solution.py:128
  15.8 5.4 %collective-permute-start.6 = (f32[104,128]{1,0:T(8,128)S(1)}, f32[104,128]{1,0:T(8,128)S(1)}, u32[]{:S(2)}, u32[]{:S(2)}) collective-permute-start(f32[104,128]{1,0:T(8,128)S(1)} %get-tuple-element.57), channel_id=1, source_target_pairs={{0,8},{8,16},{16,24},{24,0},{1,9},{9,17},{17,25},{25,1},{2,10},{10... | collective-permute-start | bytes 159752 | tf_op jit(solution)/shard_map/ppermute | solution.py:128
  15.8 5.2 %collective-permute-start.7 = (f32[72,128]{1,0:T(8,128)S(1)}, f32[72,128]{1,0:T(8,128)S(1)}, u32[]{:S(2)}, u32[]{:S(2)}) collective-permute-start(f32[72,128]{1,0:T(8,128)S(1)} %get-tuple-element.58), channel_id=1, source_target_pairs={{2,4},{4,2},{0,8},{6,14},{10,12},{12,10},{8,0},{14,6},{18,20},{20,... | collective-permute-start | bytes 110600 | tf_op jit(solution)/shard_map/ppermute | solution.py:128
  16.6 4.4 %collective-permute-start.8 = (f32[72,128]{1,0:T(8,128)S(1)}, f32[72,128]{1,0:T(8,128)S(1)}, u32[]{:S(2)}, u32[]{:S(2)}) collective-permute-start(f32[72,128]{1,0:T(8,128)S(1)} %get-tuple-element.59), channel_id=1, source_target_pairs={{0,1},{1,0},{2,3},{3,2},{4,5},{5,4},{6,7},{7,6},{8,9},{9,8},{10,11... | collective-permute-start | bytes 110600 | tf_op jit(solution)/shard_map/ppermute | solution.py:128
  17.2 4.0 %collective-permute-start.9 = (f32[72,128]{1,0:T(8,128)S(1)}, f32[72,128]{1,0:T(8,128)S(1)}, u32[]{:S(2)}, u32[]{:S(2)}) collective-permute-start(f32[72,128]{1,0:T(8,128)S(1)} %get-tuple-element.60), channel_id=1, source_target_pairs={{0,2},{2,0},{4,6},{6,4},{1,3},{3,1},{5,7},{7,5},{8,10},{10,8},{12,... | collective-permute-start | bytes 110600 | tf_op jit(solution)/shard_map/ppermute | solution.py:128
  21.2 7.3 %copy-start.1 = (f32[16,32,256]{2,1,0:T(8,128)S(1)}, f32[16,32,256]{2,1,0:T(8,128)}, u32[]{:S(2)}) copy-start(f32[16,32,256]{2,1,0:T(8,128)} %refs_5_.1) | copy-start | bytes 1572868
  24.3 6.1 %collective-permute-start.10 = (f32[32,128]{1,0:T(8,128)S(1)}, f32[32,128]{1,0:T(8,128)S(1)}, u32[]{:S(2)}, u32[]{:S(2)}) collective-permute-start(f32[32,128]{1,0:T(8,128)S(1)} %get-tuple-element.69), channel_id=1, source_target_pairs={{8,0},{16,8},{24,16},{0,24},{9,1},{17,9},{25,17},{1,25},{10,2},{18... | collective-permute-start | bytes 49160 | tf_op jit(solution)/shard_map/ppermute | solution.py:128
  25.2 5.2 %collective-permute-start.11 = (f32[32,128]{1,0:T(8,128)S(1)}, f32[32,128]{1,0:T(8,128)S(1)}, u32[]{:S(2)}, u32[]{:S(2)}) collective-permute-start(f32[32,128]{1,0:T(8,128)S(1)} %get-tuple-element.70), channel_id=1, source_target_pairs={{0,8},{8,16},{16,24},{24,0},{1,9},{9,17},{17,25},{25,1},{2,10},{10... | collective-permute-start | bytes 49160 | tf_op jit(solution)/shard_map/ppermute | solution.py:128
  25.2 5.2 %collective-permute-start.12 = (f32[32,128]{1,0:T(8,128)S(1)}, f32[32,128]{1,0:T(8,128)S(1)}, u32[]{:S(2)}, u32[]{:S(2)}) collective-permute-start(f32[32,128]{1,0:T(8,128)S(1)} %get-tuple-element.71), channel_id=1, source_target_pairs={{2,4},{4,2},{0,8},{6,14},{10,12},{12,10},{8,0},{14,6},{18,20},{20,... | collective-permute-start | bytes 49160 | tf_op jit(solution)/shard_map/ppermute | solution.py:128
  26.6 3.8 %collective-permute-start.13 = (f32[32,128]{1,0:T(8,128)S(1)}, f32[32,128]{1,0:T(8,128)S(1)}, u32[]{:S(2)}, u32[]{:S(2)}) collective-permute-start(f32[32,128]{1,0:T(8,128)S(1)} %get-tuple-element.72), channel_id=1, source_target_pairs={{0,1},{1,0},{2,3},{3,2},{4,5},{5,4},{6,7},{7,6},{8,9},{9,8},{10,11... | collective-permute-start | bytes 49160 | tf_op jit(solution)/shard_map/ppermute | solution.py:128
  28.4 3.7 %collective-permute-start.14 = (f32[32,128]{1,0:T(8,128)S(1)}, f32[32,128]{1,0:T(8,128)S(1)}, u32[]{:S(2)}, u32[]{:S(2)}) collective-permute-start(f32[32,128]{1,0:T(8,128)S(1)} %get-tuple-element.73), channel_id=1, source_target_pairs={{0,2},{2,0},{4,6},{6,4},{1,3},{3,1},{5,7},{7,5},{8,10},{10,8},{12,... | collective-permute-start | bytes 49160 | tf_op jit(solution)/shard_map/ppermute | solution.py:128
